TPU v7x, 32 devices: a whole 2x2x4 slice. The times are simulated.
32 devices in a mesh: dp: 8 (over y, x, core), tensor: 4 (over z).
Axes of the slice: x: 2, y: 2, z: 4, core: 2. Of those that a mesh axis runs over, the one named last changes fastest.
Arguments:
- hidden_in: bfloat16 [1024, 2048], P('dp'), may hold values from -6 to 6
- attn_gain: float32 [2048], replicated, may hold values from 0.5 to 1.5
- query_weight: bfloat16 [2048, 2048], P('dp', 'tensor'), may hold values from -0.125 to 0.125
- key_weight: bfloat16 [2048, 2048], P('dp', 'tensor'), may hold values from -0.125 to 0.125
- value_weight: bfloat16 [2048, 2048], P('dp', 'tensor'), may hold values from -0.125 to 0.125
- output_weight: bfloat16 [2048, 2048], P('dp', 'tensor'), may hold values from -1.5 to 1.5
- query_gain: float32 [2048], P('tensor'), may hold values from 0.5 to 1.5
- key_gain: float32 [2048], P('tensor'), may hold values from 0.5 to 1.5
- moe_gain: float32 [2048], replicated, may hold values from 0.5 to 1.5
- expert_gate_up: bfloat16 [2048, 16, 2, 1024], P(None, 'dp', None, 'tensor'), may hold values from -0.125 to 0.125
- expert_down: bfloat16 [2048, 16, 1024], P(None, 'dp', 'tensor'), may hold values from -0.1875 to 0.1875
- experts: int32 [1024, 8], P('dp'), may hold values from 0 to 15, all different within a row
- gates: float32 [1024, 8], P('dp'), may hold values from 0.25 to 0.75
- anchor: int32 [1024], P('dp'), may hold values from 0 to 1023, each once
- lengths: int32 [4], replicated, may hold values from 1 to 512, 1024 in all
- cotangent: bfloat16 [1024, 2048], P('dp'), may hold values from -8 to 8
Outputs:
- output: bfloat16 [1024, 2048], P('dp')
- input_grad: float32 [1024, 2048], P('dp')
- query_grad: float32 [2048, 2048], P('dp', 'tensor')
- key_grad: float32 [2048, 2048], P('dp', 'tensor')
- value_grad: float32 [2048, 2048], P('dp', 'tensor')
- output_grad: float32 [2048, 2048], P('dp', 'tensor')
- gate_up_grad: float32 [2048, 16, 2, 1024], P(None, 'dp', None, 'tensor')
- down_grad: float32 [2048, 16, 1024], P(None, 'dp', 'tensor')
- attn_gain_grad: float32 [2048], P('dp')
- query_gain_grad: float32 [2048], P('dp')
- key_gain_grad: float32 [2048], P('dp')
- moe_gain_grad: float32 [2048], P('dp')
Inputs may be any that keep to these rules, and one draw needn't show every extreme that they name: `anchor`: each number appears once. The lengths sum to 1024; the longest is exactly 512. Each row names 8 different experts.
All inputs are finite; a program needn't handle non-finite values.
Results may differ from a plain program's by a relative error of at most 0.033.
Values may be sent and summed in bfloat16 or wider, within the bound.
A program may use at most 256 MiB of HBM per device.

v0:
```python
import jax
import jax.numpy as jnp
from jax import lax
from jax.sharding import PartitionSpec as P

D = 2048
HD = 128
TOPK = 8


EPSILON = 1e-05
ROPE_BASE = 10000.0
NEG_FILL = -1e30


def rms_norm(values, gain):
    return values * lax.rsqrt(jnp.mean(values * values, axis=-1, keepdims=True) + EPSILON) * gain


def norm_back(values, gain, grad_out):
    inv_rms = lax.rsqrt(jnp.mean(values * values, axis=-1, keepdims=True) + EPSILON)
    weighted = grad_out * gain
    grad_in = inv_rms * weighted - values * inv_rms**3 * jnp.mean(
        weighted * values, axis=-1, keepdims=True
    )
    return (grad_in, jnp.sum(grad_out * values * inv_rms, axis=0))


def locate(anchor, lengths):
    ends = jnp.cumsum(lengths)
    starts = ends - lengths
    docs = jnp.sum((anchor[:, None] >= ends[None, :]).astype(jnp.int32), axis=1)
    which = docs[:, None] == jnp.arange(lengths.shape[0], dtype=jnp.int32)[None, :]
    begins = jnp.sum(jnp.where(which, starts[None, :], 0), axis=1)
    return (docs, (anchor - begins).astype(jnp.int32))


def rotary(tensor, positions):
    half_dim = HD // 2
    freqs = ROPE_BASE ** (-2.0 * jnp.arange(half_dim, dtype=jnp.float32) / HD)
    angles = positions.astype(jnp.float32)[:, None] * freqs[None, :]
    cosine = jnp.cos(angles)[:, None, :]
    sine_part = jnp.sin(angles)[:, None, :]
    first_half = tensor[..., :half_dim]
    second_half = tensor[..., half_dim:]
    return jnp.concatenate(
        [
            first_half * cosine - second_half * sine_part,
            second_half * cosine + first_half * sine_part,
        ],
        axis=-1,
    )


def routing(expert_rows, gate_rows, num_exp, capacity):
    tok_count = expert_rows.shape[0]
    flat_ids = expert_rows.reshape(-1)
    one_hot = (flat_ids[:, None] == jnp.arange(num_exp, dtype=jnp.int32)[None, :]).astype(jnp.int32)
    earlier = jnp.cumsum(one_hot, axis=0) - one_hot
    slot_ids = jnp.sum(earlier * one_hot, axis=1)
    dest_rows = jnp.where(slot_ids < capacity, flat_ids * capacity + slot_ids, num_exp * capacity)
    pair_token = jnp.arange(tok_count * TOPK, dtype=jnp.int32) // TOPK
    slot_source = jnp.zeros((num_exp * capacity + 1,), jnp.int32).at[dest_rows].set(pair_token)
    slot_filled = jnp.zeros((num_exp * capacity + 1,), jnp.float32).at[dest_rows].set(1.0)
    slot_gate = (
        jnp.zeros((num_exp * capacity + 1,), jnp.float32).at[dest_rows].set(gate_rows.reshape(-1))
    )
    return (dest_rows, slot_source[:-1], slot_filled[:-1], slot_gate[:-1])


def pair_allowed(query_anchor, query_docs, key_anchor, key_docs):
    return (
        (query_docs[:, None] == key_docs[None, :]) & (key_anchor[None, :] <= query_anchor[:, None])
    )[None]


def contract_last(left, right):
    return lax.dot_general(
        left, right, (((1,), (1,)), ((), ())), preferred_element_type=jnp.float32
    )


def contract_first(left, right):
    return lax.dot_general(
        left, right, (((0,), (0,)), ((), ())), preferred_element_type=jnp.float32
    )


def shards(
    hidden_in,
    attn_gain,
    query_weight,
    key_weight,
    value_weight,
    output_weight,
    query_gain,
    key_gain,
    moe_gain,
    expert_gate_up,
    expert_down,
    experts,
    gates,
    anchor,
    lengths,
    cotangent,
):
    tok_rows = hidden_in.shape[0]
    head_local = query_weight.shape[1] // HD
    score_scale = HD ** (-0.5)
    f32 = jnp.float32
    bf16 = jnp.bfloat16
    n_dp = lax.axis_size("dp")
    exp_local = expert_down.shape[1]
    num_exp = exp_local * n_dp
    capacity = 9 * tok_rows * TOPK // (8 * num_exp)
    inputs = hidden_in.astype(f32)
    grad_out = cotangent.astype(f32)
    docs, positions = locate(anchor, lengths)
    normed = rms_norm(inputs, attn_gain).astype(bf16)
    query_full, key_full, value_full, output_full = (
        lax.all_gather(query_weight, "dp", axis=0, tiled=True),
        lax.all_gather(key_weight, "dp", axis=0, tiled=True),
        lax.all_gather(value_weight, "dp", axis=0, tiled=True),
        lax.all_gather(output_weight, "dp", axis=0, tiled=True),
    )
    query_raw = jnp.dot(normed, query_full, preferred_element_type=f32)
    key_raw = jnp.dot(normed, key_full, preferred_element_type=f32)
    value_raw = jnp.dot(normed, value_full, preferred_element_type=f32)
    squares = lax.psum(
        (jnp.sum(query_raw * query_raw, axis=1), jnp.sum(key_raw * key_raw, axis=1)), "tensor"
    )
    query_inv = lax.rsqrt(squares[0] / D + EPSILON)[:, None]
    key_inv = lax.rsqrt(squares[1] / D + EPSILON)[:, None]
    query_rows = rotary(
        (query_raw * query_inv * query_gain).reshape(tok_rows, head_local, HD), positions
    ).astype(bf16)
    key_rows = rotary(
        (key_raw * key_inv * key_gain).reshape(tok_rows, head_local, HD), positions
    ).astype(bf16)
    value_rows = value_raw.astype(bf16).reshape(tok_rows, head_local, HD)
    run_max = jnp.full((head_local, tok_rows), NEG_FILL, f32)
    run_acc = jnp.zeros((tok_rows, head_local, HD), f32)
    key_piece = lax.all_gather(key_rows, "dp", axis=0, tiled=True)
    value_piece = lax.all_gather(value_rows, "dp", axis=0, tiled=True)
    anchor_piece = lax.all_gather(anchor, "dp", axis=0, tiled=True)
    piece_docs, unused = locate(anchor_piece, lengths)
    allowed = pair_allowed(anchor, docs, anchor_piece, piece_docs)
    scores = score_scale * jnp.einsum(
        "qhd,khd->hqk", query_rows, key_piece, preferred_element_type=f32
    )
    new_max = jnp.maximum(run_max, jnp.max(jnp.where(allowed, scores, NEG_FILL), axis=2))
    factor = jnp.exp(run_max - new_max)
    attn_probs = jnp.where(allowed, jnp.exp(scores - new_max[:, :, None]), 0.0)
    new_sum = jnp.sum(attn_probs, axis=2)
    update = jnp.einsum(
        "hqk,khd->qhd", attn_probs.astype(bf16), value_piece, preferred_element_type=f32
    )
    run_max, run_sum, run_acc = (new_max, new_sum, run_acc * factor.T[:, :, None] + update)
    log_total = run_max + jnp.log(run_sum)
    attended = run_acc / run_sum.T[:, :, None]
    attended_low = attended.reshape(tok_rows, -1).astype(bf16)
    attn_sum = lax.psum(
        contract_last(attended_low, output_full).astype(jnp.bfloat16), "tensor"
    ).astype(jnp.float32)
    residual = inputs + attn_sum
    moe_in = rms_norm(residual, moe_gain).astype(bf16)
    dest_rows, slot_source, slot_filled, slot_gate = routing(experts, gates, num_exp, capacity)
    buffer_rows = (moe_in[slot_source] * slot_filled[:, None].astype(bf16)).reshape(
        num_exp, capacity, D
    )
    slot_grad = (
        (grad_out[slot_source] * (slot_gate * slot_filled)[:, None])
        .astype(bf16)
        .reshape(num_exp, capacity, D)
    )
    recv_rows, recv_grad = (
        lax.all_to_all(buffer_rows, "dp", split_axis=0, concat_axis=1, tiled=True),
        lax.all_to_all(slot_grad, "dp", split_axis=0, concat_axis=1, tiled=True),
    )
    gate_up = jnp.einsum("ecd,dezf->eczf", recv_rows, expert_gate_up, preferred_element_type=f32)
    gate_part = gate_up[:, :, 0]
    up_part = gate_up[:, :, 1]
    activated = (jax.nn.silu(gate_part) * up_part).astype(bf16)
    expert_out = jnp.einsum("ecf,def->ecd", activated, expert_down, preferred_element_type=f32)
    grad_down = jnp.einsum("ecd,ecf->def", recv_grad, activated, preferred_element_type=f32)
    grad_act = jnp.einsum("ecd,def->ecf", recv_grad, expert_down, preferred_element_type=f32)
    sigmoid_gate = jax.nn.sigmoid(gate_part)
    grad_gate = grad_act * up_part * sigmoid_gate * (1.0 + gate_part * (1.0 - sigmoid_gate))
    grad_up = grad_act * jax.nn.silu(gate_part)
    grad_gateup = jnp.stack([grad_gate, grad_up], axis=2).astype(bf16)
    grad_gateup_w = jnp.einsum("ecd,eczf->dezf", recv_rows, grad_gateup, preferred_element_type=f32)
    grad_buffer = jnp.einsum(
        "eczf,dezf->ecd", grad_gateup, expert_gate_up, preferred_element_type=f32
    )
    back_out, back_grad = (
        lax.all_to_all(
            expert_out.astype(jnp.bfloat16), "dp", split_axis=1, concat_axis=0, tiled=True
        ).astype(expert_out.dtype),
        lax.all_to_all(
            grad_buffer.astype(jnp.bfloat16), "dp", split_axis=1, concat_axis=0, tiled=True
        ).astype(grad_buffer.dtype),
    )
    width = back_out.shape[2]
    zero_row = jnp.zeros((1, width), f32)
    table_rows = jnp.concatenate([back_out.reshape(num_exp * capacity, width), zero_row], axis=0)
    combined = jnp.sum(
        table_rows[dest_rows].reshape(tok_rows, TOPK, width) * gates[:, :, None], axis=1
    )
    grad_table = jnp.concatenate([back_grad.reshape(num_exp * capacity, width), zero_row], axis=0)
    grad_moe_part = jnp.sum(grad_table[dest_rows].reshape(tok_rows, TOPK, width), axis=1)
    moe_sum, grad_moe_in = (
        lax.psum(combined.astype(jnp.bfloat16), "tensor").astype(jnp.float32),
        lax.psum(grad_moe_part.astype(jnp.bfloat16), "tensor").astype(jnp.float32),
    )
    output = (residual + moe_sum).astype(bf16)
    query_full, key_full, value_full, output_full = (
        lax.all_gather(query_weight, "dp", axis=0, tiled=True),
        lax.all_gather(key_weight, "dp", axis=0, tiled=True),
        lax.all_gather(value_weight, "dp", axis=0, tiled=True),
        lax.all_gather(output_weight, "dp", axis=0, tiled=True),
    )
    grad_norm_moe, grad_moe_gain = norm_back(residual, moe_gain, grad_moe_in)
    grad_resid = grad_out + grad_norm_moe
    grad_resid_low = grad_resid.astype(bf16)
    grad_output_w = contract_first(grad_resid_low, attended_low)
    grad_att_low = (
        jnp.dot(grad_resid_low, output_full, preferred_element_type=f32)
        .astype(bf16)
        .reshape(tok_rows, head_local, HD)
    )
    delta_rows = jnp.sum(grad_att_low.astype(f32) * attended, axis=2).T
    key_piece = lax.all_gather(key_rows, "dp", axis=0, tiled=True)
    value_piece = lax.all_gather(value_rows, "dp", axis=0, tiled=True)
    anchor_piece = lax.all_gather(anchor, "dp", axis=0, tiled=True)
    piece_docs, unused = locate(anchor_piece, lengths)
    allowed = pair_allowed(anchor, docs, anchor_piece, piece_docs)
    scores = score_scale * jnp.einsum(
        "qhd,khd->hqk", query_rows, key_piece, preferred_element_type=f32
    )
    attn_probs = jnp.where(allowed, jnp.exp(scores - log_total[:, :, None]), 0.0)
    grad_probs = jnp.einsum("qhd,khd->hqk", grad_att_low, value_piece, preferred_element_type=f32)
    grad_scores = (attn_probs * (grad_probs - delta_rows[:, :, None])).astype(bf16)
    grad_query_rot = score_scale * jnp.einsum(
        "hqk,khd->qhd", grad_scores, key_piece, preferred_element_type=f32
    )
    query_wide = lax.all_gather(
        query_rows.astype(f32).astype(jnp.bfloat16), "dp", axis=0, tiled=True
    ).astype(jnp.float32)
    gradatt_wide = lax.all_gather(
        grad_att_low.astype(f32).astype(jnp.bfloat16), "dp", axis=0, tiled=True
    ).astype(jnp.float32)
    logtot_piece = lax.all_gather(
        log_total.T.astype(jnp.bfloat16), "dp", axis=0, tiled=True
    ).astype(jnp.float32)
    delta_piece = lax.all_gather(
        delta_rows.T.astype(jnp.bfloat16), "dp", axis=0, tiled=True
    ).astype(jnp.float32)
    anchor_piece = lax.all_gather(anchor, "dp", axis=0, tiled=True)
    query_piece = query_wide.astype(bf16)
    gradatt_piece = gradatt_wide.astype(bf16)
    piece_docs, unused = locate(anchor_piece, lengths)
    allowed = pair_allowed(anchor_piece, piece_docs, anchor, docs)
    scores = score_scale * jnp.einsum(
        "qhd,khd->hqk", query_piece, key_rows, preferred_element_type=f32
    )
    attn_probs = jnp.where(allowed, jnp.exp(scores - logtot_piece.T[:, :, None]), 0.0)
    grad_value = jnp.einsum(
        "hqk,qhd->khd", attn_probs.astype(bf16), gradatt_piece, preferred_element_type=f32
    )
    grad_probs = jnp.einsum("qhd,khd->hqk", gradatt_piece, value_rows, preferred_element_type=f32)
    grad_scores = (attn_probs * (grad_probs - delta_piece.T[:, :, None])).astype(bf16)
    grad_key = score_scale * jnp.einsum(
        "hqk,qhd->khd", grad_scores, query_piece, preferred_element_type=f32
    )
    grad_query_hat = rotary(grad_query_rot, -positions).reshape(tok_rows, -1)
    grad_key_hat = rotary(grad_key, -positions).reshape(tok_rows, -1)
    weighted_query = grad_query_hat * query_gain
    weighted_key = grad_key_hat * key_gain
    quarter = query_gain.shape[0]
    gain_offset = lax.axis_index("tensor") * quarter
    query_gain_part = jnp.sum(grad_query_hat * query_raw * query_inv, axis=0)
    key_gain_part = jnp.sum(grad_key_hat * key_raw * key_inv, axis=0)
    query_gain_wide = lax.dynamic_update_slice_in_dim(
        jnp.zeros((D,), f32), query_gain_part, gain_offset, 0
    )
    key_gain_wide = lax.dynamic_update_slice_in_dim(
        jnp.zeros((D,), f32), key_gain_part, gain_offset, 0
    )
    cross = lax.psum(
        (
            jnp.sum(weighted_query * query_raw, axis=1),
            jnp.sum(weighted_key * key_raw, axis=1),
            query_gain_wide,
            key_gain_wide,
        ),
        "tensor",
    )
    grad_query_raw = (
        query_inv * weighted_query - query_raw * query_inv**3 * cross[0][:, None] / D
    ).astype(bf16)
    grad_key_raw = (key_inv * weighted_key - key_raw * key_inv**3 * cross[1][:, None] / D).astype(
        bf16
    )
    grad_value_low = grad_value.reshape(tok_rows, -1).astype(bf16)
    grad_query_w = contract_first(normed, grad_query_raw)
    grad_key_w = contract_first(normed, grad_key_raw)
    grad_value_w = contract_first(normed, grad_value_low)
    grad_normed = (
        contract_last(grad_query_raw, query_full)
        + contract_last(grad_key_raw, key_full)
        + contract_last(grad_value_low, value_full)
    )
    grad_normed_sum = lax.psum(grad_normed.astype(jnp.bfloat16), "tensor").astype(jnp.float32)
    grad_norm_attn, grad_attn_gain = norm_back(inputs, attn_gain, grad_normed_sum)
    input_grad = grad_resid + grad_norm_attn
    summed = (
        lax.psum_scatter(
            grad_query_w.astype(jnp.bfloat16), "dp", scatter_dimension=0, tiled=True
        ).astype(jnp.float32),
        lax.psum_scatter(
            grad_key_w.astype(jnp.bfloat16), "dp", scatter_dimension=0, tiled=True
        ).astype(jnp.float32),
        lax.psum_scatter(
            grad_value_w.astype(jnp.bfloat16), "dp", scatter_dimension=0, tiled=True
        ).astype(jnp.float32),
        lax.psum_scatter(
            grad_output_w.astype(jnp.bfloat16), "dp", scatter_dimension=0, tiled=True
        ).astype(jnp.float32),
        lax.psum_scatter(
            grad_attn_gain.astype(jnp.bfloat16), "dp", scatter_dimension=0, tiled=True
        ).astype(jnp.float32),
        lax.psum_scatter(
            cross[2].astype(jnp.bfloat16), "dp", scatter_dimension=0, tiled=True
        ).astype(jnp.float32),
        lax.psum_scatter(
            cross[3].astype(jnp.bfloat16), "dp", scatter_dimension=0, tiled=True
        ).astype(jnp.float32),
        lax.psum_scatter(
            grad_moe_gain.astype(jnp.bfloat16), "dp", scatter_dimension=0, tiled=True
        ).astype(jnp.float32),
    )
    return (
        output,
        input_grad,
        summed[0],
        summed[1],
        summed[2],
        summed[3],
        grad_gateup_w,
        grad_down,
        summed[4],
        summed[5],
        summed[6],
        summed[7],
    )


def solution(mesh):
    in_specs = (
        P("dp", None),
        P(),
        P("dp", "tensor"),
        P("dp", "tensor"),
        P("dp", "tensor"),
        P("dp", "tensor"),
        P("tensor"),
        P("tensor"),
        P(),
        P(None, "dp", None, "tensor"),
        P(None, "dp", "tensor"),
        P("dp", None),
        P("dp", None),
        P("dp"),
        P(),
        P("dp", None),
    )
    out_specs = (
        P("dp", None),
        P("dp", None),
        P("dp", "tensor"),
        P("dp", "tensor"),
        P("dp", "tensor"),
        P("dp", "tensor"),
        P(None, "dp", None, "tensor"),
        P(None, "dp", "tensor"),
        P("dp"),
        P("dp"),
        P("dp"),
        P("dp"),
    )
    return jax.shard_map(shards, mesh=mesh, in_specs=in_specs, out_specs=out_specs, check_vma=False)
```

profile of v0, /device:TPU:0, one launch (start us, length us, event | category | flops | bytes accessed | tf_op | source)
XLA Modules:
  0.0 867.9 jit_solution(12070746928078635573)
XLA Ops:
  15.4 25.0 %all-gather.10.cloned.1.call-done = bf16[2048,512]{1,0:T(8,128)(2,1)} async-done(((bf16[256,512]{1,0:T(8,128)(2,1)}), bf16[2048,512]{1,0:T(8,128)(2,1)}) %all-gather.10.cloned.1.call-update) | async-done | bytes 2097168 | tf_op jit(solution)/shard_map/all_gather | solution.py:121
  42.8 27.3 %all-gather.12.cloned.1.call-done = bf16[2048,512]{1,0:T(8,128)(2,1)} async-done(((bf16[256,512]{1,0:T(8,128)(2,1)}), bf16[2048,512]{1,0:T(8,128)(2,1)}) %all-gather.12.cloned.1.call-update) | async-done | bytes 2097168 | tf_op jit(solution)/shard_map/all_gather | solution.py:122
  72.3 11.7 %all-reduce.7 = (f32[128]{0:T(128)S(1)}, f32[128]{0:T(128)S(1)}) all-reduce(f32[128]{0:T(128)S(1)} %get-tuple-element.131, f32[128]{0:T(128)S(1)} %get-tuple-element.133), channel_id=1, replica_groups=mesh['dp'=8,'tensor'=4] {'tensor'}, use_global_device_ids=true, to_apply=%region_5.6 | all-reduce | flops 256 | bytes 2048 | tf_op jit(solution)/shard_map/psum | solution.py:129
  93.3 6.6 all-gather.16.cloned.1.call-done
  123.3 6.8 gather_fusion.2
  130.1 6.5 multiply_convert_fusion
  141.4 65.4 %all-gather = s32[8,1,128]{2,1,0:T(1,128)S(1)} all-gather(s32[1,1,128]{2,1,0:T(1,128)S(1)} %bitcast.187), channel_id=1, replica_groups=mesh['dp'=8,'tensor'=4] {'dp'}, dimensions={0}, use_global_device_ids=true | all-gather | bytes 4608 | tf_op jit(solution)/shard_map/all_gather | solution.py:145
  218.9 38.4 %all-reduce.14.cloned.1.call-done = bf16[128,2048]{1,0:T(8,128)(2,1)} async-done(((bf16[128,2048]{1,0:T(8,128)(2,1)}), bf16[128,2048]{1,0:T(8,128)(2,1)}) %all-reduce.14.cloned.1.call-update) | async-done | bytes 524304 | tf_op jit(solution)/shard_map/psum | solution.py:162
  260.4 5.9 gather_fusion
  281.0 49.4 %all-to-all-done = bf16[16,72,2048]{2,1,0:T(8,128)(2,1)} async-done(((bf16[16,72,2048]{2,1,0:T(8,128)(2,1)}), bf16[16,72,2048]{2,1,0:T(8,128)(2,1)}, u32[]{:S(2)}, u32[]{:S(2)}) %all-to-all-start) | async-done | bytes 4718624 | tf_op jit(solution)/shard_map/all_to_all | solution.py:177
  344.5 9.4 %copy.183 = bf16[2,576,2048]{2,0,1:T(2,128)(2,1)} copy(bf16[2,576,2048]{2,1,0:T(8,128)(2,1)} %bitcast_convert_fusion) | data formatting | bytes 9437184 | tf_op jit(solution)/shard_map/convert_element_type | solution.py:200
  362.5 9.3 %copy.176 = bf16[2,576,2048]{2,0,1:T(2,128)(2,1)} copy(bf16[2,576,2048]{2,1,0:T(8,128)(2,1)} %convolution_convert_fusion) | data formatting | bytes 9437184 | tf_op jit(solution)/shard_map/convert_element_type | solution.py:197
  371.8 41.7 %all-to-all-done.3 = bf16[2,576,2048]{2,0,1:T(2,128)(2,1)} async-done(((bf16[2,576,2048]{2,0,1:T(2,128)(2,1)}), bf16[2,576,2048]{2,0,1:T(2,128)(2,1)}, u32[]{:S(2)}, u32[]{:S(2)}) %all-to-all-start.3) | async-done | bytes 4718624 | tf_op jit(solution)/shard_map/all_to_all | solution.py:199
  419.4 60.7 %all_gather.49 = bf16[1024,4]{0,1:T(4,128)(2,1)S(1)} all-gather(bf16[128,4]{0,1:T(4,128)(2,1)S(1)} %copy-done.64), channel_id=1, replica_groups=mesh['dp'=8,'tensor'=4] {'dp'}, dimensions={0}, use_global_device_ids=true | all-gather | bytes 9216 | tf_op jit(solution)/shard_map/all_gather | solution.py:252
  489.5 12.6 %gather_fusion.3 = f32[1024,2048]{1,0:T(8,128)} fusion(f32[1153,2048]{1,0:T(8,128)} %pad_convert_fusion, s32[1024]{0:T(1024)S(1)} %broadcast_clamp_fusion), kind=kCustom, calls=%fused_computation.3 | custom fusion | bytes 16781312 | tf_op jit(solution)/shard_map/gather | solution.py:210
  502.1 6.2 bitcast_reduce_fusion
  511.7 6.7 copy.177
  518.5 26.7 %all-reduce.16.cloned.1.call-done = bf16[128,2048]{1,0:T(8,128)(2,1)} async-done(((bf16[128,2048]{1,0:T(8,128)(2,1)}), bf16[128,2048]{1,0:T(8,128)(2,1)}) %all-reduce.16.cloned.1.call-update) | async-done | bytes 524304 | tf_op jit(solution)/shard_map/psum | solution.py:213
  550.7 7.3 pad_convert_fusion.1
  557.9 12.6 %gather_fusion.1 = f32[1024,2048]{1,0:T(8,128)} fusion(f32[1153,2048]{1,0:T(8,128)} %pad_convert_fusion.1, s32[1024]{0:T(1024)S(1)} %broadcast_clamp_fusion), kind=kCustom, calls=%fused_computation.1 | custom fusion | bytes 16781312 | tf_op jit(solution)/shard_map/gather | solution.py:207
  570.5 7.5 fusion
  578.1 8.9 %all_gather.51 = bf16[1024,4]{0,1:T(4,128)(2,1)S(1)} all-gather(bf16[128,4]{0,1:T(4,128)(2,1)S(1)} %convert_element_type.256), channel_id=1, replica_groups=mesh['dp'=8,'tensor'=4] {'dp'}, dimensions={0}, use_global_device_ids=true | all-gather | bytes 9216 | tf_op jit(solution)/shard_map/all_gather | solution.py:255
  605.2 19.0 %all-reduce.6 = (f32[128]{0:T(128)}, f32[128]{0:T(128)S(1)}, bf16[2048]{0:T(1024)(128)(2,1)}, bf16[2048]{0:T(1024)(128)(2,1)}) all-reduce(f32[128]{0:T(128)S(1)} %get-tuple-element.79, f32[128]{0:T(128)} %get-tuple-element.77, f32[2048]{0:T(1024)S(1)} %dynamic_update_slice.6, ...), channel_id=1, replica_groups=mesh['dp'=8,'tensor'=4] {'tensor'}, use_global_device_ids=true, to_apply=%region_26.27 | all-reduce | flops 4352 | bytes 26624 | tf_op jit(solution)/shard_map/psum | solution.py:289
  645.2 8.2 convolution_bitcast_fusion
  653.4 13.3 %copy.195 = f32[2048,2,2,256]{3,2,1,0:T(2,128)} copy(f32[2048,2,2,256]{0,3,2,1:T(8,128)} %convolution_bitcast_fusion) | data formatting | bytes 16777216
  666.6 6.2 convolution_bitcast_fusion.1
  672.9 7.2 copy.196
  684.0 24.2 %all-reduce.8 = (bf16[2048]{0:T(1024)(128)(2,1)S(1)}, bf16[2048]{0:T(1024)(128)(2,1)S(1)}, bf16[2048]{0:T(1024)(128)(2,1)S(1)}, bf16[2048]{0:T(1024)(128)(2,1)S(1)}) all-reduce(bf16[2048]{0:T(1024)(128)(2,1)S(1)} %get-tuple-element.74, bf16[2048]{0:T(1024)(128)(2,1)S(1)} %copy-done.65, ...), channel_id=6, replica_groups=mesh['dp'=8,'tensor'=4] {'dp'}, use_global_device_ids=true, to_apply=%region_36.37.clone | all-reduce | flops 8192 | bytes 32768
  714.5 11.6 %reduce-scatter.11.cloned.1.call-done = bf16[256,512]{1,0:T(8,128)(2,1)} async-done(((bf16[2048,512]{1,0:T(8,128)(2,1)}), bf16[256,512]{1,0:T(8,128)(2,1)}) %reduce-scatter.11.cloned.1.call-update) | async-done | bytes 262160 | tf_op jit(solution)/shard_map/reduce_scatter | solution.py:326
  727.9 42.6 %reduce-scatter.9.cloned.1.call-done = bf16[256,512]{1,0:T(8,128)(2,1)} async-done(((bf16[2048,512]{1,0:T(8,128)(2,1)}), bf16[256,512]{1,0:T(8,128)(2,1)}) %reduce-scatter.9.cloned.1.call-update) | async-done | bytes 262160 | tf_op jit(solution)/shard_map/reduce_scatter | solution.py:323
  772.4 42.5 %reduce-scatter.7.cloned.1.call-done = bf16[256,512]{1,0:T(8,128)(2,1)} async-done(((bf16[2048,512]{1,0:T(8,128)(2,1)}), bf16[256,512]{1,0:T(8,128)(2,1)}) %reduce-scatter.7.cloned.1.call-update) | async-done | bytes 262160 | tf_op jit(solution)/shard_map/reduce_scatter | solution.py:320
  816.7 42.5 %reduce-scatter.5.cloned.1.call-done = bf16[256,512]{1,0:T(8,128)(2,1)} async-done(((bf16[2048,512]{1,0:T(8,128)(2,1)}), bf16[256,512]{1,0:T(8,128)(2,1)}) %reduce-scatter.5.cloned.1.call-update) | async-done | bytes 262160 | tf_op jit(solution)/shard_map/reduce_scatter | solution.py:317
  (337 shorter events, 181.8 us)
Async XLA Ops:
  7.2 329.5 %copy-start = (bf16[2048,2,256]{2,1,0:T(2,128)(2,1)S(1)}, bf16[2048,2,256]{2,1,0:T(2,128)(2,1)}, u32[]{:S(2)}) copy-start(bf16[2048,2,256]{2,1,0:T(2,128)(2,1)} %param.26) | copy-start | bytes 6291460
  7.2 33.2 %all-gather.10.cloned.1.call-start = ((), (), s32[]{:S(2)}) async-start(), calls=%async_computation.8 | async-start | bytes 2359296 | tf_op jit(solution)/shard_map/all_gather | solution.py:121
  7.9 62.2 %all-gather.12.cloned.1.call-start = ((), (), s32[]{:S(2)}) async-start(), calls=%async_computation.9 | async-start | bytes 2359296 | tf_op jit(solution)/shard_map/all_gather | solution.py:122
  8.7 61.4 %copy-start.2 = (bf16[128,2048]{1,0:T(8,128)(2,1)S(1)}, bf16[128,2048]{1,0:T(8,128)(2,1)}, u32[]{:S(2)}) copy-start(bf16[128,2048]{1,0:T(8,128)(2,1)} %param.16) | copy-start | bytes 1572868
  8.7 61.4 %copy-start.32 = (f32[2048]{0:T(1024)S(1)}, f32[2048]{0:T(1024)}, u32[]{:S(2)}) copy-start(f32[2048]{0:T(1024)} %param.17) | copy-start | bytes 24580
  8.7 91.1 %all-gather.16.cloned.1.call-start = ((), (), s32[]{:S(2)}) async-start(), calls=%async_computation.11 | async-start | bytes 2359296 | tf_op jit(solution)/shard_map/all_gather | solution.py:123
  9.4 198.1 %all-gather.14.cloned.1.call-start = ((), (), s32[]{:S(2)}) async-start(), calls=%async_computation.10 | async-start | bytes 1179648 | tf_op jit(solution)/shard_map/all_gather | solution.py:143
  15.4 84.4 %copy-start.53 = (f32[128]{0:T(128)}, f32[128]{0:T(128)S(1)}, u32[]{:S(2)}) copy-start(f32[128]{0:T(128)S(1)} %get-tuple-element.122) | copy-start | bytes 1540
  93.2 118.8 %all-gather.18.cloned.1.call-start = ((), (), s32[]{:S(2)}) async-start(), calls=%async_computation.12 | async-start | bytes 1179648 | tf_op jit(solution)/shard_map/all_gather | solution.py:144
  102.7 112.7 %all-gather.20.cloned.1.call-start = ((), (), s32[]{:S(2)}) async-start(), calls=%async_computation.13 | async-start | bytes 2359296 | tf_op jit(solution)/shard_map/all_gather | solution.py:124
  136.5 70.3 %copy-start.77 = (s32[4,1]{0,1:T(1,128)S(1)}, s32[4,1]{0,1:T(1,128)}, u32[]{:S(2)}) copy-start(s32[4,1]{0,1:T(1,128)} %copy-done.76) | copy-start | bytes 52
  136.5 70.4 %copy-start.71 = (s32[128]{0:T(128)S(1)}, s32[128]{0:T(128)}, u32[]{:S(2)}) copy-start(s32[128]{0:T(128)} %copy-done.70) | copy-start | bytes 1540
  136.5 70.9 %copy-start.26 = (bf16[128,4,64]{2,0,1:T(8,128)(2,1)S(1)}, bf16[128,4,64]{2,0,1:T(8,128)(2,1)}, u32[]{:S(2)}) copy-start(bf16[128,4,64]{2,0,1:T(8,128)(2,1)} %get-tuple-element.109) | copy-start | bytes 196612
  136.5 70.9 %copy-start.27 = (bf16[128,4,64]{2,0,1:T(8,128)(2,1)S(1)}, bf16[128,4,64]{2,0,1:T(8,128)(2,1)}, u32[]{:S(2)}) copy-start(bf16[128,4,64]{2,0,1:T(8,128)(2,1)} %get-tuple-element.110) | copy-start | bytes 196612
  136.6 134.6 %all-to-all-start.2 = ((bf16[16,72,2048]{2,1,0:T(8,128)(2,1)}), bf16[16,72,2048]{2,1,0:T(8,128)(2,1)}, u32[]{:S(2)}, u32[]{:S(2)}) async-start(bf16[16,72,2048]{2,1,0:T(8,128)(2,1)} %multiply_convert_fusion), calls=%async_computation.2 | async-start | bytes 9437184 | tf_op jit(solution)/shard_map/all_to_all | solution.py:178
  141.3 115.9 %all-reduce.14.cloned.1.call-start = ((), (), s32[]{:S(2)}) async-start(), calls=%async_computation.14 | async-start | bytes 1048576 | tf_op jit(solution)/shard_map/psum | solution.py:162
  271.2 59.3 %all-to-all-start = ((bf16[16,72,2048]{2,1,0:T(8,128)(2,1)}), bf16[16,72,2048]{2,1,0:T(8,128)(2,1)}, u32[]{:S(2)}, u32[]{:S(2)}) async-start(bf16[16,72,2048]{2,1,0:T(8,128)(2,1)} %broadcast_multiply_fusion), calls=%async_computation | async-start | bytes 9437184 | tf_op jit(solution)/shard_map/all_to_all | solution.py:177
  353.8 59.8 %all-to-all-start.3 = ((bf16[2,576,2048]{2,0,1:T(2,128)(2,1)}), bf16[2,576,2048]{2,0,1:T(2,128)(2,1)}, u32[]{:S(2)}, u32[]{:S(2)}) async-start(bf16[2,576,2048]{2,0,1:T(2,128)(2,1)} %copy.183), calls=%async_computation.3 | async-start | bytes 9437184 | tf_op jit(solution)/shard_map/all_to_all | solution.py:199
  371.8 47.2 %copy-start.40 = (s32[1024]{0:T(1024)S(1)}, s32[1024]{0:T(1024)}, u32[]{:S(2)}) copy-start(s32[1024]{0:T(1024)} %copy-done.39) | copy-start | bytes 12292
  371.8 47.3 %copy-start.61 = (s32[128]{0:T(128)S(1)}, s32[128]{0:T(128)}, u32[]{:S(2)}) copy-start(s32[128]{0:T(128)} %param.29) | copy-start | bytes 1540
  371.8 47.3 %copy-start.72 = (s32[128]{0:T(128)S(1)}, s32[128]{0:T(128)}, u32[]{:S(2)}) copy-start(s32[128]{0:T(128)} %copy-done.70) | copy-start | bytes 1540
  371.8 47.6 %copy-start.64 = (bf16[128,4]{0,1:T(4,128)(2,1)S(1)}, bf16[128,4]{0,1:T(4,128)(2,1)}, u32[]{:S(2)}) copy-start(bf16[128,4]{0,1:T(4,128)(2,1)} %get-tuple-element.113) | copy-start | bytes 3076
  413.6 98.2 %all-to-all-start.1 = ((bf16[2,576,2048]{2,0,1:T(2,128)(2,1)}), bf16[2,576,2048]{2,0,1:T(2,128)(2,1)}, u32[]{:S(2)}, u32[]{:S(2)}) async-start(bf16[2,576,2048]{2,0,1:T(2,128)(2,1)} %copy.176), calls=%async_computation.1 | async-start | bytes 9437184 | tf_op jit(solution)/shard_map/all_to_all | solution.py:196
  418.2 90.2 %all-gather.22.cloned.1.call-start = ((), (), s32[]{:S(2)}) async-start(), calls=%async_computation.16 | async-start | bytes 1179648 | tf_op jit(solution)/shard_map/all_gather | solution.py:246
  419.0 126.2 %all-reduce.16.cloned.1.call-start = ((), (), s32[]{:S(2)}) async-start(), calls=%async_computation.15 | async-start | bytes 1048576 | tf_op jit(solution)/shard_map/psum | solution.py:213
  508.3 82.3 %all-gather.24.cloned.1.call-start = ((), (), s32[]{:S(2)}) async-start(), calls=%async_computation.17 | async-start | bytes 1179648 | tf_op jit(solution)/shard_map/all_gather | solution.py:249
  550.4 132.2 %all-reduce.18.cloned.1.call-start = ((), (), s32[]{:S(2)}) async-start(), calls=%async_computation.22 | async-start | bytes 2097152 | tf_op jit(solution)/shard_map/psum | solution.py:212
  633.2 92.9 %reduce-scatter.11.cloned.1.call-start = ((), (), s32[]{:S(2)}) async-start(), calls=%async_computation.21 | async-start | bytes 2359296 | tf_op jit(solution)/shard_map/reduce_scatter | solution.py:326
  636.5 134.1 %reduce-scatter.9.cloned.1.call-start = ((), (), s32[]{:S(2)}) async-start(), calls=%async_computation.20 | async-start | bytes 2359296 | tf_op jit(solution)/shard_map/reduce_scatter | solution.py:323
  639.4 175.5 %reduce-scatter.7.cloned.1.call-start = ((), (), s32[]{:S(2)}) async-start(), calls=%async_computation.19 | async-start | bytes 2359296 | tf_op jit(solution)/shard_map/reduce_scatter | solution.py:320
  641.7 217.5 %reduce-scatter.5.cloned.1.call-start = ((), (), s32[]{:S(2)}) async-start(), calls=%async_computation.18 | async-start | bytes 2359296 | tf_op jit(solution)/shard_map/reduce_scatter | solution.py:317
  710.8 150.1 %copy-start.1 = (bf16[2048,2,256]{2,1,0:T(2,128)(2,1)S(1)}, bf16[2048,2,256]{2,1,0:T(2,128)(2,1)}, u32[]{:S(2)}) copy-start(bf16[2048,2,256]{2,1,0:T(2,128)(2,1)} %param.26) | copy-start | bytes 6291460
  (73 other events, 1012.0 us)
Sparse Core Ops, SparseCore 0:
  9.9 30.4 all-gather.9
  42.3 27.7 all-gather.11
  72.0 27.7 all-gather.15
  102.2 23.3 all-gather.13
  127.9 26.3 all-gather.17
  156.0 52.6 all-gather.19
  218.9 38.3 all-reduce.13
  420.9 35.1 all-gather.21
  508.5 36.7 all-reduce.15
  550.5 23.2 all-gather.23
  633.3 49.2 all-reduce.17
  685.8 40.3 reduce-scatter.10
  729.4 41.1 reduce-scatter.8
  773.7 41.1 reduce-scatter.6
  818.0 41.1 reduce-scatter.4
where the time goes:
time: 877 us; the launch traced here: 868 us
  waiting for transfers between devices  360 us (41%)
  blocking collectives  190 us (22%)
  local copies, waits for them, and re-layouts  129 us (15%)
  other arithmetic  83.5 us (10%)
  matrix products  69.1 us (8%)
  starting transfers between devices  20.1 us (2%)
  between operations  16.2 us (2%)
    all_gather x1, blocking collectives, shards(): anchor_piece = lax.all_gather(anchor, 'dp', axis=0, tiled=True)  65.4 us
    all_gather x1, blocking collectives, shards(): lax.all_gather(log_total.T.astype(jnp.bfloat16), 'dp', axis=0, tiled=True)  60.7 us
    all_to_all x1, waiting for transfers between devices, shards(): lax.all_to_all(buffer_rows, 'dp', split_axis=0, concat_axis=1, tiled=True)  49.4 us
    reduce_scatter x1, waiting for transfers between devices, shards(): lax.psum_scatter(grad_value_w.astype(jnp.bfloat16), 'dp', scatter_dimensi...  42.6 us
    reduce_scatter x1, waiting for transfers between devices, shards(): lax.psum_scatter(grad_key_w.astype(jnp.bfloat16), 'dp', scatter_dimension...  42.5 us
    reduce_scatter x1, waiting for transfers between devices, shards(): lax.psum_scatter(grad_query_w.astype(jnp.bfloat16), 'dp', scatter_dimensi...  42.5 us
    all_to_all x1, waiting for transfers between devices, shards(): lax.all_to_all(grad_buffer.astype(jnp.bfloat16), 'dp', split_axis=1, conc...  41.7 us
    psum x1, waiting for transfers between devices, shards(): lax.psum(contract_last(attended_low, output_full).astype(jnp.bfloat16), '...  38.4 us
  transfers between devices with their start and end apart: 19, of which 12 were waited for; matrix products, arithmetic and copies ran while one was open for 26% of the time, Pallas kernels for 0%

commit v1 on v0

v1 whole, which is shorter than its diff:
```python
import functools
import jax
import jax.numpy as jnp
from jax import lax
from jax.experimental import pallas as pl
from jax.experimental.pallas import tpu as pltpu
from jax.sharding import PartitionSpec as P

MESH = pl.DeviceIdType.MESH
f32 = jnp.float32
bf16 = jnp.bfloat16


def bit_list(n):
    bits, b = [], 1
    while b < n:
        bits.append(b)
        b *= 2
    return bits


def flip(i, m):
    for b in bit_list(m + 1):
        if m & b:
            i = i + b - 2 * b * ((i // b) % 2)
    return i


def span(bits):
    out = [0]
    for b in bits:
        out = out + [m | b for m in out]
    return out


def orders(n):
    bits = bit_list(n)
    outer = bits[1:]
    return (outer + bits[:1], outer[::-1] + bits[:1])


def hello(peers):
    barrier = pltpu.get_barrier_semaphore()
    for peer in peers:
        pl.semaphore_signal(barrier, inc=1, device_id=peer, device_id_type=MESH)
    pl.semaphore_wait(barrier, len(peers))


def rdma(src, dst, send_sem, recv_sem, peer):
    return pltpu.make_async_remote_copy(
        src_ref=src, dst_ref=dst, send_sem=send_sem, recv_sem=recv_sem,
        device_id=peer, device_id_type=MESH,
    )


class Gather:
    def __init__(self, n, me, src, dst, send_sems, recv_sems):
        self.n, self.me, self.src, self.dst = n, me, src, dst
        self.send_sems, self.recv_sems = send_sems, recv_sems
        self.half = src.shape[0] // 2
        self.sent = []

    def push(self, h, m, bit):
        rows = pl.ds(h * self.half, self.half)
        place = self.dst(flip(self.me, m)).at[rows]
        copy = rdma(self.src.at[rows] if m == 0 else place, place, self.send_sems.at[h, m | bit],
                    self.recv_sems.at[h, m | bit], {"dp": flip(self.me, bit)})
        copy.start()
        self.sent.append(copy)

    def start(self):
        o = orders(self.n)
        for j in range(len(o[0])):
            for h in (0, 1):
                self.push(h, 0, o[h][j])

    def stage(self, j):
        o = orders(self.n)
        for i in range(2**j):
            for h in (0, 1):
                m = span(o[h][:j])[i] | o[h][j]
                place = self.dst(flip(self.me, m)).at[pl.ds(h * self.half, self.half)]
                rdma(place, place, self.send_sems.at[h, m], self.recv_sems.at[h, m],
                     {"dp": flip(self.me, o[h][j])}).wait_recv()
                for bit in o[h][j + 1:]:
                    self.push(h, m, bit)

    def finish(self):
        for copy in self.sent:
            copy.wait_send()


def dp_peers(n, me):
    return [{"dp": flip(me, b)} for b in bit_list(n)]


def all_peers(axis, n, me):
    return [{axis: flip(me, m)} for m in range(1, n)]


def call(kernel, name, cid, outs, out_space, in_space, scratch, *args):
    single = not isinstance(outs, (list, tuple))
    spec = pl.BlockSpec(memory_space=out_space)
    return pl.pallas_call(
        kernel,
        out_shape=outs,
        in_specs=[pl.BlockSpec(memory_space=in_space)] * len(args),
        out_specs=spec if single else [spec] * len(outs),
        scratch_shapes=scratch,
        compiler_params=pltpu.CompilerParams(collective_id=cid, has_side_effects=True),
        name=name,
    )(*args)


def gather_kernel(n, count, *refs):
    srcs, dsts, sems = refs[:count], refs[count:2 * count], refs[2 * count:]
    me = lax.axis_index("dp")
    own = [pltpu.make_async_copy(srcs[i], dsts[i].at[me], sems[2 * count].at[i]) for i in range(count)]
    hello(dp_peers(n, me))
    gathers = [Gather(n, me, srcs[i], (lambda o, i=i: dsts[i].at[o]), sems[2 * i], sems[2 * i + 1]) for i in range(count)]
    for g in gathers:
        g.start()
    for c in own:
        c.start()
    for j in range(len(bit_list(n))):
        for g in gathers:
            g.stage(j)
    for g in gathers:
        g.finish()
    for c in own:
        c.wait()


def gather_dp(n, arrs, cid):
    arrs = list(arrs)
    scratch = [pltpu.SemaphoreType.DMA((2, n))] * (2 * len(arrs)) + [pltpu.SemaphoreType.DMA((len(arrs),))]
    outs = [jax.ShapeDtypeStruct((n,) + a.shape, a.dtype) for a in arrs]
    return call(functools.partial(gather_kernel, n, len(arrs)), "gather_dp", cid, outs, pl.ANY, pl.ANY, scratch, *arrs)


def spread_kernel(n, nt, src, dst, zs, zr, gs, gr, loc):
    d, t = lax.axis_index("dp"), lax.axis_index("tensor")
    own = pltpu.make_async_copy(src, dst.at[d, t], loc)
    hello(dp_peers(n, d) + all_peers("tensor", nt, t))
    sent = []
    for m in range(1, nt):
        c = rdma(src, dst.at[d, t], zs.at[m], zr.at[m], {"tensor": flip(t, m)})
        c.start()
        sent.append(c)
    gathers = []
    for m in range(nt):
        tm = flip(t, m)
        gathers.append(Gather(n, d, src if m == 0 else dst.at[d, tm], (lambda o, tm=tm: dst.at[o, tm]), gs.at[m], gr.at[m]))
    gathers[0].start()
    own.start()
    for m in range(1, nt):
        place = dst.at[d, flip(t, m)]
        rdma(place, place, zs.at[m], zr.at[m], {"tensor": flip(t, m)}).wait_recv()
        gathers[m].start()
        gathers[m - 1].stage(0)
        if m > 1:
            gathers[m - 2].stage(1)
    steps = len(bit_list(n))
    done = [0] * nt
    for m in range(nt):
        done[m] = 0 if m == nt - 1 else 1 if m == nt - 2 else 2
    for j in range(steps):
        for m in range(nt):
            if done[m] == j:
                gathers[m].stage(j)
                done[m] = j + 1
    for g in gathers:
        g.finish()
    for c in sent:
        c.wait_send()
    own.wait()


def spread(n, nt, x, cid):
    scratch = [pltpu.SemaphoreType.DMA((nt,))] * 2 + [pltpu.SemaphoreType.DMA((nt, 2, n))] * 2 + [pltpu.SemaphoreType.DMA]
    out = jax.ShapeDtypeStruct((n, nt) + x.shape, x.dtype)
    return call(functools.partial(spread_kernel, n, nt), "spread", cid, out, pl.ANY, pl.ANY, scratch, x)


def reduce_dp(n, me, p_ref, acc, got, send_sems, recv_sems, put):
    half = p_ref.shape[1] // 2
    bits = bit_list(n)
    o = [x[::-1] for x in orders(n)]
    sent = []
    base = 0
    for j in range(len(bits)):
        keeps = [span(o[h][j + 1:]) for h in (0, 1)]
        for i in range(len(keeps[0])):
            for h in (0, 1):
                m, b = keeps[h][i], o[h][j]
                src = p_ref.at[flip(me, m | b), pl.ds(h * half, half)] if j == 0 else acc.at[h, m | b]
                c = rdma(src, got.at[h, base + i], send_sems.at[h, base + i], recv_sems.at[h, base + i], {"dp": flip(me, b)})
                c.start()
                sent.append(c)
        for i in range(len(keeps[0]))[::-1]:
            for h in (0, 1):
                m, b = keeps[h][i], o[h][j]
                rows = pl.ds(h * half, half)
                view = got.at[h, base + i]
                rdma(view, view, send_sems.at[h, base + i], recv_sems.at[h, base + i], {"dp": flip(me, b)}).wait_recv()
                mine = p_ref[flip(me, m), rows] if j == 0 else acc[h, m]
                total = mine.astype(f32) + view[...].astype(f32)
                if j == len(bits) - 1:
                    put(rows, total)
                else:
                    acc[h, m] = total.astype(bf16)
        base += len(keeps[0])
    return sent


def fold_kernel(n, nt, p_ref, out_ref, acc, got, part, zgot, send_sems, recv_sems, zs, zr):
    d, t = lax.axis_index("dp"), lax.axis_index("tensor")
    hello(dp_peers(n, d) + all_peers("tensor", nt, t))
    share = out_ref.shape[0]

    def put(rows, total):
        part[rows, :] = total.astype(bf16)

    sent = reduce_dp(n, d, p_ref, acc, got, send_sems, recv_sems, put)
    for m in range(1, nt):
        c = rdma(part.at[pl.ds(flip(t, m) * share, share)], zgot.at[m], zs.at[m], zr.at[m], {"tensor": flip(t, m)})
        c.start()
        sent.append(c)
    total = part[pl.ds(t * share, share), :].astype(f32)
    for m in range(1, nt):
        rdma(zgot.at[m], zgot.at[m], zs.at[m], zr.at[m], {"tensor": flip(t, m)}).wait_recv()
        total = total + zgot[m].astype(f32)
    out_ref[...] = total
    for c in sent:
        c.wait_send()


def fold(n, nt, p, cid):
    _, rows, cols = p.shape
    scratch = [
        pltpu.VMEM((2, n, rows // 2, cols), bf16),
        pltpu.VMEM((2, n, rows // 2, cols), bf16),
        pltpu.VMEM((rows, cols), bf16),
        pltpu.VMEM((nt, rows // nt, cols), bf16),
    ] + [pltpu.SemaphoreType.DMA((2, n))] * 2 + [pltpu.SemaphoreType.DMA((nt,))] * 2
    out = jax.ShapeDtypeStruct((rows // nt, cols), f32)
    return call(functools.partial(fold_kernel, n, nt), "fold", cid, out, pltpu.VMEM, pltpu.VMEM, scratch, p)


def zsum_kernel(nt, x_ref, out_ref, zgot, zs, zr):
    t = lax.axis_index("tensor")
    hello(all_peers("tensor", nt, t))
    share = out_ref.shape[0]
    sent = []
    for m in range(1, nt):
        c = rdma(x_ref.at[pl.ds(flip(t, m) * share, share)], zgot.at[m], zs.at[m], zr.at[m], {"tensor": flip(t, m)})
        c.start()
        sent.append(c)
    total = x_ref[pl.ds(t * share, share), :].astype(f32)
    for m in range(1, nt):
        rdma(zgot.at[m], zgot.at[m], zs.at[m], zr.at[m], {"tensor": flip(t, m)}).wait_recv()
        total = total + zgot[m].astype(f32)
    out_ref[...] = total
    for c in sent:
        c.wait_send()


def zsum(nt, x, cid):
    rows, cols = x.shape
    scratch = [pltpu.VMEM((nt, rows // nt, cols), x.dtype)] + [pltpu.SemaphoreType.DMA((nt,))] * 2
    out = jax.ShapeDtypeStruct((rows // nt, cols), f32)
    return call(functools.partial(zsum_kernel, nt), "zsum", cid, out, pltpu.VMEM, pltpu.VMEM, scratch, x)


def direct_kernel(axis, n, split, count, *refs):
    srcs, dsts, ss, rs, loc = refs[:count], refs[count:2 * count], *refs[2 * count:]
    me = lax.axis_index(axis)
    own = [pltpu.make_async_copy(srcs[i].at[me] if split else srcs[i], dsts[i].at[me], loc.at[i]) for i in range(count)]
    hello(all_peers(axis, n, me))
    sent = []
    for m in range(1, n):
        for i in range(count):
            peer = flip(me, m)
            c = rdma(srcs[i].at[peer] if split else srcs[i], dsts[i].at[me], ss.at[i, m], rs.at[i, m], {axis: peer})
            c.start()
            sent.append(c)
    for c in own:
        c.start()
    for m in range(1, n):
        for i in range(count):
            place = dsts[i].at[flip(me, m)]
            rdma(place, place, ss.at[i, m], rs.at[i, m], {axis: flip(me, m)}).wait_recv()
    for c in sent:
        c.wait_send()
    for c in own:
        c.wait()


def direct(axis, n, arrs, cid, split=False):
    arrs = list(arrs)
    scratch = [pltpu.SemaphoreType.DMA((len(arrs), n))] * 2 + [pltpu.SemaphoreType.DMA((len(arrs),))]
    outs = [jax.ShapeDtypeStruct(a.shape if split else (n,) + a.shape, a.dtype) for a in arrs]
    return call(functools.partial(direct_kernel, axis, n, split, len(arrs)), "direct_" + axis, cid, outs, pltpu.VMEM, pltpu.VMEM, scratch, *arrs)


D = 2048
HD = 128
TOPK = 8
EPSILON = 1e-05
ROPE_BASE = 10000.0
NEG_FILL = -1e30


def norm_back(values, gain, grad_out):
    inv_rms = lax.rsqrt(jnp.mean(values * values, axis=-1, keepdims=True) + EPSILON)
    weighted = grad_out * gain
    grad_in = inv_rms * weighted - values * inv_rms**3 * jnp.mean(weighted * values, axis=-1, keepdims=True)
    return grad_in, jnp.sum(grad_out * values * inv_rms, axis=0)


def locate(anchor, lengths):
    ends = jnp.cumsum(lengths)
    starts = ends - lengths
    docs = jnp.sum((anchor[:, None] >= ends[None, :]).astype(jnp.int32), axis=1)
    which = docs[:, None] == jnp.arange(lengths.shape[0], dtype=jnp.int32)[None, :]
    begins = jnp.sum(jnp.where(which, starts[None, :], 0), axis=1)
    return docs, (anchor - begins).astype(jnp.int32)


def rope_tables(positions):
    half_dim = HD // 2
    freqs = ROPE_BASE ** (-2.0 * jnp.arange(half_dim, dtype=f32) / HD)
    angles = positions.astype(f32)[:, None] * freqs[None, :]
    cosine, sine = jnp.cos(angles), jnp.sin(angles)
    return jnp.concatenate([cosine, cosine], axis=1)[:, None, :], jnp.concatenate([-sine, sine], axis=1)[:, None, :]


def turn(x, cosine, sine):
    return x * cosine + jnp.roll(x, HD // 2, axis=-1) * sine


def pair_allowed(query_anchor, query_docs, key_anchor, key_docs):
    return ((query_docs[:, None] == key_docs[None, :]) & (key_anchor[None, :] <= query_anchor[:, None]))[None]


def contract(left, right, l, r):
    return lax.dot_general(left, right, (((l,), (r,)), ((), ())), preferred_element_type=f32)


def routing(experts, gates, num_exp, capacity):
    toks = experts.shape[0]
    chosen = experts[:, :, None] == jnp.arange(num_exp, dtype=jnp.int32)[None, None, :]
    mask = jnp.any(chosen, axis=1)
    gate = jnp.sum(jnp.where(chosen, gates[:, :, None], 0.0), axis=1)
    index = jnp.arange(toks, dtype=jnp.int32)
    before = (index[:, None] > index[None, :]).astype(bf16)
    slot = contract(before, mask.astype(bf16), 1, 0)
    return jnp.where(mask & (slot < capacity), gate, 0.0)


def small(rows):
    rows = jnp.stack(rows)
    return jnp.pad(rows, ((0, -rows.shape[0] % 8), (0, 0)))


def shards(hidden_in, attn_gain, query_weight, key_weight, value_weight, output_weight, query_gain, key_gain,
           moe_gain, expert_gate_up, expert_down, experts, gates, anchor, lengths, cotangent):
    n, nt = lax.axis_size("dp"), lax.axis_size("tensor")
    d, t = lax.axis_index("dp"), lax.axis_index("tensor")
    toks = hidden_in.shape[0]
    share = toks // nt
    cols = query_weight.shape[1]
    heads = cols // HD
    scale = HD ** (-0.5)
    exp_local = expert_down.shape[1]
    num_exp = exp_local * n
    capacity = 9 * toks * TOPK // (8 * num_exp)
    hidden = hidden_in.astype(f32)

    def mine(a):
        return lax.dynamic_slice_in_dim(a, t * share, share, 0)

    coef = routing(experts, gates, num_exp, capacity).T
    place = jnp.broadcast_to(anchor[None, :], (16, toks))
    wq, wk, wv, wo, dy_all, coef_all, anchor_all = gather_dp(
        n, (query_weight, key_weight, value_weight, output_weight, cotangent, coef, place), 1)
    wq, wk, wv, wo = (w.reshape(D, cols) for w in (wq, wk, wv, wo))
    dy_all = dy_all.reshape(n * toks, D)
    coef_all = lax.dynamic_slice_in_dim(coef_all, d * exp_local, exp_local, 1)
    coef_all = coef_all.transpose(0, 2, 1).reshape(n * toks, exp_local)
    anchor_all = anchor_all[:, 0].reshape(n * toks)

    docs, positions = locate(anchor, lengths)
    docs_all, _ = locate(anchor_all, lengths)
    cosine, sine = rope_tables(positions)
    allowed = pair_allowed(anchor, docs, anchor_all, docs_all)
    allowed_back = pair_allowed(anchor_all, docs_all, anchor, docs)

    inv = lax.rsqrt(jnp.mean(hidden * hidden, axis=-1, keepdims=True) + EPSILON)
    normed = (hidden * inv * attn_gain).astype(bf16)
    q_raw, k_raw, v_raw = (contract(normed, w, 1, 0) for w in (wq, wk, wv))
    (sq,) = direct("tensor", nt, [small([jnp.sum(q_raw * q_raw, axis=1), jnp.sum(k_raw * k_raw, axis=1)])], 2)
    sq = jnp.sum(sq, axis=0)
    q_inv = lax.rsqrt(sq[0] / D + EPSILON)[:, None]
    k_inv = lax.rsqrt(sq[1] / D + EPSILON)[:, None]
    q = turn((q_raw * q_inv * query_gain).reshape(toks, heads, HD), cosine, sine).astype(bf16)
    k = turn((k_raw * k_inv * key_gain).reshape(toks, heads, HD), cosine, sine).astype(bf16)
    v = v_raw.astype(bf16)
    k_all, v_all = gather_dp(n, (k.reshape(toks, cols), v), 3)
    k_all, v_all = (a.reshape(n * toks, heads, HD) for a in (k_all, v_all))
    v = v.reshape(toks, heads, HD)

    scores = scale * jnp.einsum("qhd,khd->hqk", q, k_all, preferred_element_type=f32)
    top = jnp.max(jnp.where(allowed, scores, NEG_FILL), axis=2)
    probs = jnp.where(allowed, jnp.exp(scores - top[:, :, None]), 0.0)
    total = jnp.sum(probs, axis=2)
    lse = top + jnp.log(total)
    attended = jnp.einsum("hqk,khd->qhd", probs.astype(bf16), v_all, preferred_element_type=f32)
    attended = attended / total.T[:, :, None]
    o = attended.reshape(toks, cols).astype(bf16)
    h1 = mine(hidden) + zsum(nt, contract(o, wo, 1, 1).astype(bf16), 4)
    n2 = (h1 * lax.rsqrt(jnp.mean(h1 * h1, axis=-1, keepdims=True) + EPSILON) * moe_gain).astype(bf16)
    n2_all = spread(n, nt, n2, 5).reshape(n * toks, D)

    gu = jnp.einsum("td,dezf->tezf", n2_all, expert_gate_up, preferred_element_type=f32)
    g, u = gu[:, :, 0], gu[:, :, 1]
    sig = jax.nn.sigmoid(g)
    act = (coef_all[:, :, None] * (g * sig * u)).astype(bf16)
    dact = coef_all[:, :, None] * jnp.einsum("td,def->tef", dy_all, expert_down, preferred_element_type=f32)
    dgu = jnp.stack([dact * u * sig * (1.0 + g * (1.0 - sig)), dact * (g * sig)], axis=2).astype(bf16)
    dn2 = jnp.einsum("tezf,dezf->td", dgu, expert_gate_up, preferred_element_type=f32).astype(bf16)
    moe = jnp.einsum("tef,def->td", act, expert_down, preferred_element_type=f32).astype(bf16)
    down_grad = jnp.einsum("td,tef->def", dy_all, act, preferred_element_type=f32)
    gate_up_grad = jnp.einsum("td,tezf->dezf", n2_all, dgu, preferred_element_type=f32)

    dn2 = fold(n, nt, dn2.reshape(n, toks, D), 6)
    dres, moe_gain_part = norm_back(h1, moe_gain, dn2)
    dh1 = mine(cotangent).astype(f32) + dres
    moe = fold(n, nt, moe.reshape(n, toks, D), 7)
    out_share = (h1 + moe).astype(bf16)
    dh1r, output = direct("tensor", nt, [dh1.astype(bf16), out_share], 8)
    dh1r = dh1r.reshape(toks, D)
    output = output.reshape(toks, D)

    do = contract(dh1r, wo, 1, 0).astype(bf16)
    delta = jnp.sum(do.reshape(toks, heads, HD).astype(f32) * attended, axis=2).T
    stats = small(list(lse) + list(delta))
    if stats.shape[0] % 16:
        stats = jnp.pad(stats, ((0, 8), (0, 0)))
    q_all, do_all, o_all, stats_all = gather_dp(n, (q.reshape(toks, cols), do, o, stats), 9)
    slices, = direct("dp", n, [jnp.concatenate([normed, dh1r], axis=0).reshape(2 * toks, n, D // n).transpose(1, 0, 2)], 10, True)
    normed_all = slices[:, :toks].reshape(n * toks, D // n)
    dh1r_all = slices[:, toks:].reshape(n * toks, D // n)
    output_grad = contract(dh1r_all, o_all.reshape(n * toks, cols), 0, 0)

    do = do.reshape(toks, heads, HD)
    q_all, do_all = (a.reshape(n * toks, heads, HD) for a in (q_all, do_all))
    lse_all = stats_all[:, :heads].transpose(1, 0, 2).reshape(heads, n * toks)
    delta_all = stats_all[:, heads:2 * heads].transpose(1, 0, 2).reshape(heads, n * toks)
    probs = jnp.where(allowed, jnp.exp(scores - lse[:, :, None]), 0.0)
    dprobs = jnp.einsum("qhd,khd->hqk", do, v_all, preferred_element_type=f32)
    ds = (probs * (dprobs - delta[:, :, None])).astype(bf16)
    dq = scale * jnp.einsum("hqk,khd->qhd", ds, k_all, preferred_element_type=f32)
    scores_b = scale * jnp.einsum("qhd,khd->hqk", q_all, k, preferred_element_type=f32)
    probs_b = jnp.where(allowed_back, jnp.exp(scores_b - lse_all[:, :, None]), 0.0)
    dv = jnp.einsum("hqk,qhd->khd", probs_b.astype(bf16), do_all, preferred_element_type=f32)
    dprobs_b = jnp.einsum("qhd,khd->hqk", do_all, v, preferred_element_type=f32)
    ds_b = (probs_b * (dprobs_b - delta_all[:, :, None])).astype(bf16)
    dk = scale * jnp.einsum("hqk,qhd->khd", ds_b, q_all, preferred_element_type=f32)
    dq_hat = turn(dq, cosine, -sine).reshape(toks, cols)
    dk_hat = turn(dk, cosine, -sine).reshape(toks, cols)
    dv = dv.reshape(toks, cols).astype(bf16)

    wdq, wdk = dq_hat * query_gain, dk_hat * key_gain
    q_gain_part = jnp.sum(dq_hat * q_raw * q_inv, axis=0)
    k_gain_part = jnp.sum(dk_hat * k_raw * k_inv, axis=0)
    (cross,) = direct("tensor", nt, [small([jnp.sum(wdq * q_raw, axis=1), jnp.sum(wdk * k_raw, axis=1)])], 11)
    cross = jnp.sum(cross, axis=0)
    dq_raw = (q_inv * wdq - q_raw * q_inv**3 * cross[0][:, None] / D).astype(bf16)
    dk_raw = (k_inv * wdk - k_raw * k_inv**3 * cross[1][:, None] / D).astype(bf16)
    dnormed = contract(dq_raw, wq, 1, 1) + contract(dk_raw, wk, 1, 1) + contract(dv, wv, 1, 1)
    dnormed = zsum(nt, dnormed.astype(bf16), 12)
    dx, attn_gain_part = norm_back(mine(hidden), attn_gain, dnormed)

    def wide(part):
        return lax.dynamic_update_slice_in_dim(jnp.zeros((D,), f32), part, t * cols, 0)

    gains = small([attn_gain_part, wide(q_gain_part), wide(k_gain_part), moe_gain_part])
    gains = jnp.concatenate([gains, jnp.zeros_like(gains)], axis=0)
    dq_all, dk_all, dv_all, gains_all = gather_dp(n, (dq_raw, dk_raw, dv, gains), 13)
    query_grad, key_grad, value_grad = (
        contract(normed_all, a.reshape(n * toks, cols), 0, 0) for a in (dq_all, dk_all, dv_all))
    gains = lax.dynamic_slice_in_dim(jnp.sum(gains_all[:, :8], axis=0), d * (D // n), D // n, 1)
    input_grad, gains = direct("tensor", nt, [(dh1 + dx).astype(bf16), gains], 14)
    input_grad = input_grad.reshape(toks, D).astype(f32)
    gains = jnp.sum(gains, axis=0)
    return (output, input_grad, query_grad, key_grad, value_grad, output_grad, gate_up_grad, down_grad,
            gains[0], gains[1], gains[2], gains[3])


def solution(mesh):
    in_specs = (
        P("dp", None),
        P(),
        P("dp", "tensor"),
        P("dp", "tensor"),
        P("dp", "tensor"),
        P("dp", "tensor"),
        P("tensor"),
        P("tensor"),
        P(),
        P(None, "dp", None, "tensor"),
        P(None, "dp", "tensor"),
        P("dp", None),
        P("dp", None),
        P("dp"),
        P(),
        P("dp", None),
    )
    out_specs = (
        P("dp", None),
        P("dp", None),
        P("dp", "tensor"),
        P("dp", "tensor"),
        P("dp", "tensor"),
        P("dp", "tensor"),
        P(None, "dp", None, "tensor"),
        P(None, "dp", "tensor"),
        P("dp"),
        P("dp"),
        P("dp"),
        P("dp"),
    )
    return jax.shard_map(shards, mesh=mesh, in_specs=in_specs, out_specs=out_specs, check_vma=False)
```

time: 877 us -> 518 us (0.59)
  waiting for transfers between devices: 360 us -> 0 us
  Pallas kernels: 0 us -> 332 us
  blocking collectives: 190 us -> 0 us
  local copies, waits for them, and re-layouts: 129 us -> 64.2 us
  other arithmetic: 83.5 us -> 40.2 us
  starting transfers between devices: 20.1 us -> 0 us
  between operations: 16.2 us -> 2.04 us
    pallas_call x0 -> x14, Pallas kernels: none -> 332 us  [call(): pl.pallas_call(kernel, out_shape=outs, in_specs=[pl.BlockSpec(memory_spac...]
    reduce_scatter x4 -> x0, waiting for transfers between devices: 139 us -> none  [the longest x1 42.6 us: shards(): lax.psum_scatter(grad_value_w.astype(jnp.bfloat16), 'dp', scatter_dimensi...]
    all_gather x3 -> x0, blocking collectives: 135 us -> none  [the longest x1 65.4 us: shards(): anchor_piece = lax.all_gather(anchor, 'dp', axis=0, tiled=True)]
    all_to_all x4 -> x0, waiting for transfers between devices: 91.2 us -> none  [the longest x1 49.4 us: shards(): lax.all_to_all(buffer_rows, 'dp', split_axis=0, concat_axis=1, tiled=True)]
    psum x3 -> x0, waiting for transfers between devices: 67.6 us -> none  [the longest x1 38.4 us: shards(): lax.psum(contract_last(attended_low, output_full).astype(jnp.bfloat16), '...]
    all_gather x8 -> x0, waiting for transfers between devices: 58.9 us -> none  [the longest x1 27.3 us: shards(): lax.all_gather(key_weight, 'dp', axis=0, tiled=True)]
    gather x4 -> x0, local copies, waits for them, and re-layouts: 37.8 us -> none  [the longest x1 12.6 us: shards(): table_rows[dest_rows].reshape(tok_rows, TOPK, width) * gates[:, :, None]]
    psum x2 -> x0, blocking collectives: 30.7 us -> none  [the longest x1 19 us: shards(): lax.psum((jnp.sum(weighted_query * query_raw, axis=1), jnp.sum(weighted_k...]
  transfers between devices with their start and end apart: 19 -> 0, of which waited for: 12 -> 0; matrix products, arithmetic and copies ran while one was open for 26% -> 0% of each run, Pallas kernels for 0% -> 0%
where the time goes in v1:
time: 518 us; the launch traced here: 514 us
  Pallas kernels  332 us (64%)
  matrix products  75.7 us (15%)
  local copies, waits for them, and re-layouts  64.2 us (12%)
  other arithmetic  40.2 us (8%)
    pallas_call x14, Pallas kernels, call(): pl.pallas_call(kernel, out_shape=outs, in_specs=[pl.BlockSpec(memory_spac...  332 us
    unnamed x163, local copies, waits for them, and re-layouts  37.9 us
    dot_general x13, matrix products, contract(): lax.dot_general(left, right, (((l,), (r,)), ((), ())), preferred_element_...  22.5 us

profile of v1, /device:TPU:0, one launch (start us, length us, event | category | flops | bytes accessed | tf_op | source)
XLA Modules:
  0.0 513.7 jit_solution(7122687600952411717)
XLA Ops:
  4.3 60.2 %gather_dp.4 = (bf16[8,256,512]{2,1,0:T(8,128)(2,1)}, bf16[8,256,512]{2,1,0:T(8,128)(2,1)}, bf16[8,256,512]{2,1,0:T(8,128)(2,1)}, bf16[8,256,512]{2,1,0:T(8,128)...) custom-call(bf16[256,512]{1,0:T(8,128)(2,1)} %refs_0_.1, ...), custom_call_target="tpu_custom_call" | custom-call | tf_op jit(solution)/shard_map/gather_dp/pallas_call | solution.py:104
  75.3 7.2 %direct_tensor.4 = f32[4,8,128]{2,1,0:T(8,128)} custom-call(f32[8,128]{1,0:T(8,128)} %select_maximum_fusion.5.refs_0_), custom_call_target="tpu_custom_call" | custom-call | tf_op jit(solution)/shard_map/direct_tensor/pallas_call | solution.py:104
  93.7 2.7 convolution_convert_fusion.2.refs_1_
  96.4 13.5 %gather_dp.5 = (bf16[8,128,512]{2,1,0:T(8,128)(2,1)}, bf16[8,128,512]{2,1,0:T(8,128)(2,1)}) custom-call(bf16[128,512]{1,0:T(8,128)(2,1)} %fusion.55.refs_0_, bf16[128,512]{1,0:T(8,128)(2,1)} %convolution_convert_fusion.2.refs_1_), custom_call_target="tpu_custom_call" | custom-call | tf_op jit(solution)/shard_map/gather_dp/pallas_call | solution.py:104
  112.1 2.5 copy.133
  121.0 3.5 fusion.88
  126.8 15.7 %zsum.2 = f32[32,2048]{1,0:T(8,128)} custom-call(bf16[128,2048]{1,0:T(8,128)(2,1)} %convolution_convert_fusion.x_ref), custom_call_target="tpu_custom_call" | custom-call | tf_op jit(solution)/shard_map/zsum/pallas_call | solution.py:104
  146.7 28.9 %spread.1 = bf16[8,4,32,2048]{3,2,1,0:T(8,128)(2,1)} custom-call(bf16[32,2048]{1,0:T(8,128)(2,1)} %multiply_convert_fusion.6.src), custom_call_target="tpu_custom_call" | custom-call | tf_op jit(solution)/shard_map/spread/pallas_call | solution.py:104
  175.6 10.0 %fusion = f32[1024,2,2,256]{3,0,1,2:T(8,128)} fusion(bf16[1024,2048,1,1]{1,0,2,3:T(8,128)(2,1)} %bitcast.237, bf16[2048,2,2,256]{3,2,1,0:T(2,128)(2,1)} %param.25), kind=kOutput, calls=%fused_computation.2 | convolution fusion | flops 4294967296 | bytes 12582912 | tf_op jit(solution)/shard_map/td,dezf->tezf/dot_general | solution.py:425
  186.4 6.1 %fusion.46 = (bf16[1024,2,1,256]{3,0,1,2:T(8,128)(2,1)S(1)}, bf16[1024,2,1,256]{3,0,1,2:T(8,128)(2,1)S(1)}) fusion(f32[1024,2,2,256]{3,0,1,2:T(8,128)} %fusion, f32[1024,2]{0,1:T(2,128)S(1)} %dynamic-slice_bitcast_fusion, bf16[1024,2048,1]{1,0,2:T(8,128)(2,1)} %bitcast.277, bf16[2048,2,256]{2,1,0:T(2,128)(2,1)S(1)} %copy-done), kind=kOutput, calls=%fused_computation.74 | convolution fusion | flops 2154823680 | bytes 12591104 | tf_op jit(solution)/shard_map/td,def->tef/dot_general | solution.py:429
  192.5 6.5 %bitcast_convert_fusion = bf16[1024,2048]{1,0:T(8,128)(2,1)} fusion(bf16[2048,2,2,256]{3,2,1,0:T(2,128)(2,1)S(1)} %copy-done.70, bf16[1024,2,1,256]{3,0,1,2:T(8,128)(2,1)S(1)} %get-tuple-element.107, bf16[1024,2,1,256]{3,0,1,2:T(8,128)(2,1)S(1)} %get-tuple-element.106), kind=kOutput, calls=%fused_computation | convolution fusion | flops 4298113024 | bytes 10485760 | tf_op jit(solution)/shard_map/tezf,dezf->td/dot_general | solution.py:431
  199.0 41.7 %fold.2 = f32[32,2048]{1,0:T(8,128)} custom-call(bf16[8,128,2048]{2,1,0:T(8,128)(2,1)} %bitcast.239), custom_call_target="tpu_custom_call" | custom-call | tf_op jit(solution)/shard_map/fold/pallas_call | solution.py:104
  240.7 6.7 %bitcast_convert_fusion.1 = bf16[1024,2048]{1,0:T(8,128)(2,1)} fusion(bf16[2048,2,256]{2,1,0:T(2,128)(2,1)S(1)} %copy-done, f32[1024,2,2,256]{3,0,1,2:T(8,128)} %fusion, f32[1024,2]{0,1:T(2,128)S(1)} %dynamic-slice_bitcast_fusion), kind=kOutput, calls=%fused_computation.1 | convolution fusion | flops 2153250816 | bytes 10493952 | tf_op jit(solution)/shard_map/tef,def->td/dot_general | solution.py:432
  247.4 42.2 %fold.3 = f32[32,2048]{1,0:T(8,128)} custom-call(bf16[8,128,2048]{2,1,0:T(8,128)(2,1)} %bitcast.240), custom_call_target="tpu_custom_call" | custom-call | tf_op jit(solution)/shard_map/fold/pallas_call | solution.py:104
  293.9 24.3 %direct_tensor.5 = (bf16[4,32,2048]{2,1,0:T(8,128)(2,1)}, bf16[4,32,2048]{2,1,0:T(8,128)(2,1)}) custom-call(bf16[32,2048]{1,0:T(8,128)(2,1)} %get-tuple-element.102.refs_0_, bf16[32,2048]{1,0:T(8,128)(2,1)} %get-tuple-element.114.refs_1_), custom_call_target="tpu_custom_call" | custom-call | tf_op jit(solution)/shard_map/direct_tensor/pallas_call | solution.py:104
  320.9 3.5 broadcast_multiply_fusion.1
  328.3 18.2 %gather_dp.6 = (bf16[8,128,512]{2,1,0:T(8,128)(2,1)}, bf16[8,128,512]{2,1,0:T(8,128)(2,1)}, bf16[8,128,512]{2,1,0:T(8,128)(2,1)}, f32[8,16,128]{2,1,0:T(8,128)}) custom-call(bf16[128,512]{1,0:T(8,128)(2,1)} %get-tuple-element.109.refs_0_, bf16[128,512]{1,0:T(8,128)(2,1)} %copy-done.28, bf16[128,512]{1,0:T(8,128)(2,1)} %copy.165.refs_2_, ...), custom_call_target="tpu_custom_call" | custom-call | tf_op jit(solution)/shard_map/gather_dp/pallas_call | solution.py:104
  350.4 2.5 exponential_select_fusion
  355.1 2.8 copy.142
  358.0 3.3 broadcast_multiply_fusion
  367.6 9.7 %direct_tensor.6 = f32[4,8,128]{2,1,0:T(8,128)} custom-call(f32[8,128]{1,0:T(8,128)} %select_maximum_fusion.4.refs_0_), custom_call_target="tpu_custom_call" | custom-call | tf_op jit(solution)/shard_map/direct_tensor/pallas_call | solution.py:104
  379.2 2.5 fusion.95
  387.0 14.6 %zsum.3 = f32[32,2048]{1,0:T(8,128)} custom-call(bf16[128,2048]{1,0:T(8,128)(2,1)} %fusion.3.x_ref), custom_call_target="tpu_custom_call" | custom-call | tf_op jit(solution)/shard_map/zsum/pallas_call | solution.py:104
  406.2 22.0 %gather_dp.7 = (bf16[8,128,512]{2,1,0:T(8,128)(2,1)}, bf16[8,128,512]{2,1,0:T(8,128)(2,1)}, bf16[8,128,512]{2,1,0:T(8,128)(2,1)}, f32[8,16,2048]{2,1,0:T(8,128)}) custom-call(bf16[128,512]{1,0:T(8,128)(2,1)} %copy-done.25, bf16[128,512]{1,0:T(8,128)(2,1)} %copy-done.26, bf16[128,512]{1,0:T(8,128)(2,1)} %copy.169.refs_2_, f32[16,2048]{1,0:T(8,128)} %concatenate.40.refs_3_), custom_call_target="tpu_custom_call" | custom-call | tf_op jit(solution)/shard_map/gather_dp/pallas_call | solution.py:104
  429.9 16.3 %direct_tensor.7 = (bf16[4,32,2048]{2,1,0:T(8,128)(2,1)}, f32[4,8,256]{2,1,0:T(8,128)}) custom-call(bf16[32,2048]{1,0:T(8,128)(2,1)} %add_convert_fusion.refs_0_, f32[8,256]{1,0:T(8,128)} %constant_dynamic-slice_fusion.refs_1_), custom_call_target="tpu_custom_call" | custom-call | tf_op jit(solution)/shard_map/direct_tensor/pallas_call | solution.py:104
  450.1 17.0 %direct_dp.1 = bf16[8,256,256]{2,1,0:T(8,128)(2,1)} custom-call(bf16[8,256,256]{2,1,0:T(8,128)(2,1)} %maximum_bitcast_fusion.refs_0_), custom_call_target="tpu_custom_call" | custom-call | tf_op jit(solution)/shard_map/direct_dp/pallas_call | solution.py:104
  467.1 2.4 convolution_bitcast_fusion.3
  469.6 2.6 convolution_bitcast_fusion.2
  474.7 5.8 %fusion.13 = f32[2048,2,2,256]{3,0,2,1:T(8,128)S(1)} fusion(bf16[1024,2048,1,1]{1,0,3,2:T(8,128)(2,1)S(1)} %bitcast.238, bf16[1024,2,1,256]{3,0,1,2:T(8,128)(2,1)} %copy-done.78, bf16[1024,2,1,256]{3,0,1,2:T(8,128)(2,1)S(1)} %copy-done.77), kind=kOutput, calls=%fused_computation.31 | convolution fusion | flops 4296015872 | bytes 14680064 | tf_op jit(solution)/shard_map/td,tezf->dezf/dot_general | solution.py:434
  480.5 16.7 %copy.154 = f32[2048,2,2,256]{3,2,1,0:T(2,128)} copy(f32[2048,2,2,256]{3,0,2,1:T(8,128)S(1)} %fusion.13) | data formatting | bytes 16777216
  497.2 2.6 fusion.31
  499.9 12.2 %copy.155 = f32[2048,2,256]{2,1,0:T(2,128)} copy(f32[2048,2,256]{2,0,1:T(8,128)S(1)} %fusion.31) | data formatting | bytes 8388608
  (255 shorter events, 85.1 us)
Async XLA Ops:
  0.6 185.7 %copy-start = (bf16[2048,2,256]{2,1,0:T(2,128)(2,1)S(1)}, bf16[2048,2,256]{2,1,0:T(2,128)(2,1)}, u32[]{:S(2)}) copy-start(bf16[2048,2,256]{2,1,0:T(2,128)(2,1)} %param.26) | copy-start | bytes 6291460
  0.7 70.4 %copy-start.40 = (f32[2048]{0:T(1024)S(1)}, f32[2048]{0:T(1024)}, u32[]{:S(2)}) copy-start(f32[2048]{0:T(1024)} %param.17) | copy-start | bytes 24580
  0.7 70.2 %copy-start.9 = (bf16[128,2048]{1,0:T(8,128)(2,1)S(1)}, bf16[128,2048]{1,0:T(8,128)(2,1)}, u32[]{:S(2)}) copy-start(bf16[128,2048]{1,0:T(8,128)(2,1)} %param.16) | copy-start | bytes 1572868
  73.5 11.6 %copy-start.46 = (f32[512]{0:T(512)S(1)}, f32[512]{0:T(512)}, u32[]{:S(2)}) copy-start(f32[512]{0:T(512)} %param.23) | copy-start | bytes 6148
  73.5 11.6 %copy-start.50 = (f32[512]{0:T(512)S(1)}, f32[512]{0:T(512)}, u32[]{:S(2)}) copy-start(f32[512]{0:T(512)} %param.22) | copy-start | bytes 6148
  118.8 5.7 %copy-start.63 = (f32[4,128]{1,0:T(4,128)}, f32[4,128]{1,0:T(4,128)S(1)}, u32[]{:S(2)}) copy-start(f32[4,128]{1,0:T(4,128)S(1)} %fusion.19) | copy-start | bytes 6148
  126.8 19.2 %copy-start.41 = (f32[2048]{0:T(1024)S(1)}, f32[2048]{0:T(1024)}, u32[]{:S(2)}) copy-start(f32[2048]{0:T(1024)} %param.24) | copy-start | bytes 24580
  145.9 29.7 %copy-start.65 = (f32[32]{0:T(128)}, f32[32]{0:T(128)S(1)}, u32[]{:S(2)}) copy-start(f32[32]{0:T(128)S(1)} %get-tuple-element.141) | copy-start | bytes 388
  186.4 54.4 %copy-start.61 = (f32[1024,2]{0,1:T(2,128)}, f32[1024,2]{0,1:T(2,128)S(1)}, u32[]{:S(2)}) copy-start(f32[1024,2]{0,1:T(2,128)S(1)} %dynamic-slice_bitcast_fusion) | copy-start | bytes 24580
  186.4 6.1 %copy-start.70 = (bf16[2048,2,2,256]{3,2,1,0:T(2,128)(2,1)S(1)}, bf16[2048,2,2,256]{3,2,1,0:T(2,128)(2,1)}, u32[]{:S(2)}) copy-start(bf16[2048,2,2,256]{3,2,1,0:T(2,128)(2,1)} %param.25) | copy-start | bytes 12582916
  192.5 6.5 %copy-start.76 = (bf16[1024,2,1,256]{3,0,1,2:T(8,128)(2,1)}, bf16[1024,2,1,256]{3,0,1,2:T(8,128)(2,1)S(1)}, u32[]{:S(2)}) copy-start(bf16[1024,2,1,256]{3,0,1,2:T(8,128)(2,1)S(1)} %get-tuple-element.106) | copy-start | bytes 3145732
  192.5 6.5 %copy-start.78 = (bf16[1024,2,1,256]{3,0,1,2:T(8,128)(2,1)}, bf16[1024,2,1,256]{3,0,1,2:T(8,128)(2,1)S(1)}, u32[]{:S(2)}) copy-start(bf16[1024,2,1,256]{3,0,1,2:T(8,128)(2,1)S(1)} %get-tuple-element.107) | copy-start | bytes 3145732
  247.4 42.3 %copy-start.19 = (f32[32,2048]{1,0:T(8,128)S(1)}, f32[32,2048]{1,0:T(8,128)}, u32[]{:S(2)}) copy-start(f32[32,2048]{1,0:T(8,128)} %fold.2) | copy-start | bytes 786436
  289.7 28.5 %copy-start.7 = (bf16[8,256,512]{2,1,0:T(8,128)(2,1)S(1)}, bf16[8,256,512]{2,1,0:T(8,128)(2,1)}, u32[]{:S(2)}) copy-start(bf16[8,256,512]{2,1,0:T(8,128)(2,1)} %get-tuple-element.39) | copy-start | bytes 6291460
  293.9 27.0 %copy-start.53 = (f32[4,128]{1,0:T(4,128)S(1)}, f32[4,128]{1,0:T(4,128)}, u32[]{:S(2)}) copy-start(f32[4,128]{1,0:T(4,128)} %copy-done.52) | copy-start | bytes 6148
  293.9 27.0 %copy-start.64 = (f32[4,128]{1,0:T(4,128)S(1)}, f32[4,128]{1,0:T(4,128)}, u32[]{:S(2)}) copy-start(f32[4,128]{1,0:T(4,128)} %copy-done.63) | copy-start | bytes 6148
  324.7 21.8 %copy-start.20 = (f32[128,512]{1,0:T(8,128)}, f32[128,512]{1,0:T(8,128)S(1)}, u32[]{:S(2)}) copy-start(f32[128,512]{1,0:T(8,128)S(1)} %copy.167) | copy-start | bytes 786436
  357.9 7.0 %copy-start.47 = (f32[512]{0:T(512)S(1)}, f32[512]{0:T(512)}, u32[]{:S(2)}) copy-start(f32[512]{0:T(512)} %param.23) | copy-start | bytes 6148
  385.4 16.2 %copy-start.69 = (f32[32]{0:T(128)S(1)}, f32[32]{0:T(128)}, u32[]{:S(2)}) copy-start(f32[32]{0:T(128)} %get-tuple-element.108) | copy-start | bytes 388
  385.4 16.2 %copy-start.12 = (f32[128,2048]{1,0:T(8,128)S(1)}, f32[128,2048]{1,0:T(8,128)}, u32[]{:S(2)}) copy-start(f32[128,2048]{1,0:T(8,128)} %convert_element_type.118) | copy-start | bytes 3145732
  385.4 17.4 %copy-start.33 = (f32[32,2048]{1,0:T(8,128)S(1)}, f32[32,2048]{1,0:T(8,128)}, u32[]{:S(2)}) copy-start(f32[32,2048]{1,0:T(8,128)} %get-tuple-element.103) | copy-start | bytes 786436
  387.0 18.4 %copy-start.60 = (f32[512]{0:T(512)S(1)}, f32[512]{0:T(512)}, u32[]{:S(2)}) copy-start(f32[512]{0:T(512)} %get-tuple-element.94) | copy-start | bytes 6148
  387.0 18.4 %copy-start.59 = (f32[512]{0:T(512)S(1)}, f32[512]{0:T(512)}, u32[]{:S(2)}) copy-start(f32[512]{0:T(512)} %get-tuple-element.92) | copy-start | bytes 6148
  387.0 18.4 %copy-start.48 = (f32[2048]{0:T(1024)S(1)}, f32[2048]{0:T(1024)}, u32[]{:S(2)}) copy-start(f32[2048]{0:T(1024)} %get-tuple-element.96) | copy-start | bytes 24580
  402.8 45.5 %copy-start.24 = (bf16[4,32,2048]{2,1,0:T(8,128)(2,1)S(1)}, bf16[4,32,2048]{2,1,0:T(8,128)(2,1)}, u32[]{:S(2)}) copy-start(bf16[4,32,2048]{2,1,0:T(8,128)(2,1)} %get-tuple-element.43) | copy-start | bytes 1572868
  449.1 18.0 %copy-start.74 = (bf16[8,128,512]{2,1,0:T(8,128)(2,1)S(1)}, bf16[8,128,512]{2,1,0:T(8,128)(2,1)}, u32[]{:S(2)}) copy-start(bf16[8,128,512]{2,1,0:T(8,128)(2,1)} %get-tuple-element.49) | copy-start | bytes 3145732
  480.5 16.7 %copy-start.62 = (f32[1024,2]{0,1:T(2,128)S(1)}, f32[1024,2]{0,1:T(2,128)}, u32[]{:S(2)}) copy-start(f32[1024,2]{0,1:T(2,128)} %copy-done.61) | copy-start | bytes 24580
  480.5 16.7 %copy-start.71 = (bf16[8,128,2048]{2,1,0:T(8,128)(2,1)S(1)}, bf16[8,128,2048]{2,1,0:T(8,128)(2,1)}, u32[]{:S(2)}) copy-start(bf16[8,128,2048]{2,1,0:T(8,128)(2,1)} %get-tuple-element.41) | copy-start | bytes 12582916
  480.5 16.7 %copy-start.75 = (f32[1024,2,2,256]{3,0,1,2:T(8,128)S(1)}, f32[1024,2,2,256]{3,0,1,2:T(8,128)}, u32[]{:S(2)}) copy-start(f32[1024,2,2,256]{3,0,1,2:T(8,128)} %fusion) | copy-start | bytes 12582916
  499.8 12.2 %copy-start.49 = (f32[4,8,256]{2,1,0:T(8,128)S(1)}, f32[4,8,256]{2,1,0:T(8,128)}, u32[]{:S(2)}) copy-start(f32[4,8,256]{2,1,0:T(8,128)} %get-tuple-element.53) | copy-start | bytes 98308
  499.8 12.8 %copy-start.37 = (bf16[4,32,2048]{2,1,0:T(8,128)(2,1)S(1)}, bf16[4,32,2048]{2,1,0:T(8,128)(2,1)}, u32[]{:S(2)}) copy-start(bf16[4,32,2048]{2,1,0:T(8,128)(2,1)} %get-tuple-element.42) | copy-start | bytes 1572868
  499.9 13.6 %copy-start.1 = (bf16[2048,2,256]{2,1,0:T(2,128)(2,1)S(1)}, bf16[2048,2,256]{2,1,0:T(2,128)(2,1)}, u32[]{:S(2)}) copy-start(bf16[2048,2,256]{2,1,0:T(2,128)(2,1)} %param.26) | copy-start | bytes 6291460
  (47 other events, 131.9 us)

commit v2 on v1

--- a/solution.py
+++ b/solution.py
@@ -138,138 +138,461 @@
     return call(functools.partial(gather_kernel, n, len(arrs)), "gather_dp", cid, outs, pl.ANY, pl.ANY, scratch, *arrs)
 
 
-def spread_kernel(n, nt, src, dst, zs, zr, gs, gr, loc):
+class Spread:
+    def __init__(self, n, nt, d, t, src, dst, zs, zr, gs, gr):
+        self.nt, self.t, self.d, self.src, self.dst, self.zs, self.zr = nt, t, d, src, dst, zs, zr
+        self.steps = len(bit_list(n))
+        self.gathers = []
+        for m in range(nt):
+            tm = flip(t, m)
+            own = src if m == 0 else dst.at[d, tm]
+            self.gathers.append(Gather(n, d, own, (lambda o, tm=tm: dst.at[o, tm]), gs.at[m], gr.at[m]))
+        self.sent = []
+
+    def start(self):
+        for m in range(1, self.nt):
+            c = rdma(self.src, self.dst.at[self.d, self.t], self.zs.at[m], self.zr.at[m], {"tensor": flip(self.t, m)})
+            c.start()
+            self.sent.append(c)
+        self.gathers[0].start()
+
+    def run(self):
+        done = [0] * self.nt
+        for m in range(1, self.nt):
+            place = self.dst.at[self.d, flip(self.t, m)]
+            rdma(place, place, self.zs.at[m], self.zr.at[m], {"tensor": flip(self.t, m)}).wait_recv()
+            self.gathers[m].start()
+            for k in range(m):
+                if done[k] < self.steps and k + done[k] < m:
+                    self.gathers[k].stage(done[k])
+                    done[k] += 1
+        for j in range(self.steps):
+            for m in range(self.nt):
+                if done[m] == j:
+                    self.gathers[m].stage(j)
+                    done[m] = j + 1
+
+    def finish(self):
+        for g in self.gathers:
+            g.finish()
+        for c in self.sent:
+            c.wait_send()
+
+
+class Reduce:
+    def __init__(self, n, me, p, got, send_sems, recv_sems):
+        self.n, self.me, self.p, self.got, self.ss, self.rs = n, me, p, got, send_sems, recv_sems
+        self.half = p.shape[1] // 2
+        self.bits = len(bit_list(n))
+        self.o = [x[::-1] for x in orders(n)]
+        self.keeps = [[span(self.o[h][j + 1:]) for h in (0, 1)] for j in range(self.bits)]
+        self.base = [sum(len(self.keeps[k][0]) for k in range(j)) for j in range(self.bits)]
+        self.sent = []
+
+    def piece(self, j, h, m):
+        if j == 0:
+            return self.p.at[flip(self.me, m), pl.ds(h * self.half, self.half)]
+        return self.got.at[h, self.base[j - 1] + self.keeps[j - 1][h].index(m)]
+
+    def each(self, j):
+        for i in range(len(self.keeps[j][0])):
+            for h in (0, 1):
+                yield h, self.keeps[j][h][i], self.o[h][j], self.base[j] + i
+
+    def send(self, j):
+        for h, m, b, k in self.each(j):
+            c = rdma(self.piece(j, h, m | b), self.got.at[h, k], self.ss.at[h, k], self.rs.at[h, k], {"dp": flip(self.me, b)})
+            c.start()
+            self.sent.append(c)
+
+    def recv(self, j, put=None):
+        for h, m, b, k in self.each(j):
+            view = self.got.at[h, k]
+            rdma(view, view, self.ss.at[h, k], self.rs.at[h, k], {"dp": flip(self.me, b)}).wait_recv()
+            total = self.piece(j, h, m)[...].astype(f32) + view[...].astype(f32)
+            if j == self.bits - 1:
+                put(pl.ds(h * self.half, self.half), total)
+            else:
+                view[...] = total.astype(bf16)
+
+    def finish(self):
+        for c in self.sent:
+            c.wait_send()
+
+
+class ZSum:
+    def __init__(self, nt, t, src, got, zs, zr):
+        self.nt, self.t, self.src, self.got, self.zs, self.zr = nt, t, src, got, zs, zr
+        self.share = src.shape[0] // nt
+        self.sent = []
+
+    def start(self):
+        for m in range(1, self.nt):
+            peer = flip(self.t, m)
+            c = rdma(self.src.at[pl.ds(peer * self.share, self.share)], self.got.at[m], self.zs.at[m], self.zr.at[m], {"tensor": peer})
+            c.start()
+            self.sent.append(c)
+
+    def total(self):
+        total = self.src[pl.ds(self.t * self.share, self.share), :].astype(f32)
+        for m in range(1, self.nt):
+            v = self.got.at[m]
+            rdma(v, v, self.zs.at[m], self.zr.at[m], {"tensor": flip(self.t, m)}).wait_recv()
+            total = total + v[...].astype(f32)
+        return total
+
+    def finish(self):
+        for c in self.sent:
+            c.wait_send()
+
+
+class Direct:
+    def __init__(self, axis, n, me, src, dst, ss, rs, split=False):
+        self.axis, self.n, self.me, self.src, self.dst, self.ss, self.rs, self.split = axis, n, me, src, dst, ss, rs, split
+        self.sent = []
+
+    def start(self):
+        for m in range(1, self.n):
+            peer = flip(self.me, m)
+            c = rdma(self.src.at[peer] if self.split else self.src, self.dst.at[self.me], self.ss.at[m], self.rs.at[m], {self.axis: peer})
+            c.start()
+            self.sent.append(c)
+
+    def wait(self):
+        for m in range(1, self.n):
+            place = self.dst.at[flip(self.me, m)]
+            rdma(place, place, self.ss.at[m], self.rs.at[m], {self.axis: flip(self.me, m)}).wait_recv()
+
+    def finish(self):
+        for c in self.sent:
+            c.wait_send()
+
+
+def greet(n, nt, d, t, every_dp=False):
+    hello((all_peers("dp", n, d) if every_dp else dp_peers(n, d)) + all_peers("tensor", nt, t))
+
+
+def inv_rms(v):
+    return lax.rsqrt(jnp.mean(v * v, axis=-1, keepdims=True) + EPSILON)
+
+
+VM = pl.BlockSpec(memory_space=pltpu.VMEM)
+HB = pl.BlockSpec(memory_space=pl.ANY)
+DMA = pltpu.SemaphoreType.DMA
+
+
+def kernel_call(kernel, name, cid, in_specs, outs, out_specs, scratch, args):
+    return pl.pallas_call(
+        kernel, out_shape=outs, in_specs=in_specs, out_specs=out_specs, scratch_shapes=scratch,
+        compiler_params=pltpu.CompilerParams(collective_id=cid, has_side_effects=True), name=name,
+    )(*args)
+
+
+def stats_kernel(n, nt, sq, wo, sq_all, wo_all, ss, rs, gs, gr, loc):
     d, t = lax.axis_index("dp"), lax.axis_index("tensor")
-    own = pltpu.make_async_copy(src, dst.at[d, t], loc)
-    hello(dp_peers(n, d) + all_peers("tensor", nt, t))
-    sent = []
-    for m in range(1, nt):
-        c = rdma(src, dst.at[d, t], zs.at[m], zr.at[m], {"tensor": flip(t, m)})
+    greet(n, nt, d, t)
+    x = Direct("tensor", nt, t, sq, sq_all, ss, rs)
+    g = Gather(n, d, wo, lambda o: wo_all.at[o], gs, gr)
+    own = pltpu.make_async_copy(wo, wo_all.at[d], loc)
+    x.start()
+    g.start()
+    own.start()
+    sq_all[t] = sq[...]
+    x.wait()
+    for j in range(len(bit_list(n))):
+        g.stage(j)
+    g.finish()
+    x.finish()
+    own.wait()
+
+
+def stats(n, nt, sq, wo, cid):
+    return kernel_call(
+        functools.partial(stats_kernel, n, nt), "stats", cid, [VM, HB],
+        [jax.ShapeDtypeStruct((nt,) + sq.shape, sq.dtype), jax.ShapeDtypeStruct((n,) + wo.shape, wo.dtype)], [VM, HB],
+        [DMA((nt,)), DMA((nt,)), DMA((2, n)), DMA((2, n)), DMA], (sq, wo))
+
+
+def enter_kernel(n, nt, part, hidden, gain, dy, coef, n2_all, h1, dy_all, coef_all,
+                 zgot, n2, zs, zr, ps, pr, gs, gr, ys, yr, cs, cr, loc):
+    d, t = lax.axis_index("dp"), lax.axis_index("tensor")
+    greet(n, nt, d, t)
+    z = ZSum(nt, t, part, zgot, zs, zr)
+    z.start()
+    gy = Gather(n, d, dy, lambda o: dy_all.at[o], ys, yr)
+    gc = Gather(n, d, coef, lambda o: coef_all.at[o], cs, cr)
+    gc.start()
+    gy.start()
+    own_y = pltpu.make_async_copy(dy, dy_all.at[d], loc.at[0])
+    own_c = pltpu.make_async_copy(coef, coef_all.at[d], loc.at[1])
+    own_y.start()
+    own_c.start()
+    value = hidden[pl.ds(t * z.share, z.share), :].astype(f32) + z.total()
+    h1[...] = value
+    n2[...] = (value * inv_rms(value) * gain[...]).astype(bf16)
+    s = Spread(n, nt, d, t, n2, n2_all, ps, pr, gs, gr)
+    own_n = pltpu.make_async_copy(n2, n2_all.at[d, t], loc.at[2])
+    s.start()
+    own_n.start()
+    for j in range(len(bit_list(n))):
+        gc.stage(j)
+        gy.stage(j)
+    s.run()
+    s.finish()
+    gy.finish()
+    gc.finish()
+    z.finish()
+    own_y.wait()
+    own_c.wait()
+    own_n.wait()
+
+
+def enter(n, nt, part, hidden, gain, dy, coef, cid):
+    rows, cols = part.shape
+    share = rows // nt
+    sds = jax.ShapeDtypeStruct
+    return kernel_call(
+        functools.partial(enter_kernel, n, nt), "enter", cid, [VM, VM, VM, HB, HB],
+        [sds((n, nt, share, cols), bf16), sds((share, cols), f32), sds((n,) + dy.shape, dy.dtype), sds((n,) + coef.shape, coef.dtype)],
+        [HB, VM, HB, HB],
+        [pltpu.VMEM((nt, share, cols), bf16), pltpu.VMEM((share, cols), bf16), DMA((nt,)), DMA((nt,)), DMA((nt,)), DMA((nt,)),
+         DMA((nt, 2, n)), DMA((nt, 2, n)), DMA((2, n)), DMA((2, n)), DMA((2, n)), DMA((2, n)), DMA((3,))],
+        (part, hidden, gain, dy, coef))
+
+
+def leave_kernel(n, nt, both, *refs):
+    if both:
+        (dn2, moe, h1, cot, gain, dh1, dh1r_all, gain_part, moe_part,
+         got, got2, part, zgot, low, ss, rs, ss2, rs2, zs, zr, xs, xr) = refs
+    else:
+        dn2, h1, cot, gain, dh1, dh1r_all, gain_part, got, part, zgot, low, ss, rs, zs, zr, xs, xr = refs
+    d, t = lax.axis_index("dp"), lax.axis_index("tensor")
+    greet(n, nt, d, t)
+    steps = len(bit_list(n))
+
+    def put(rows, total):
+        part[rows, :] = total.astype(bf16)
+
+    a = Reduce(n, d, dn2, got, ss, rs)
+    z = ZSum(nt, t, part, zgot, zs, zr)
+    if both:
+        b = Reduce(n, d, moe, got2, ss2, rs2)
+
+        def put2(rows, total):
+            moe_part[rows, :] = total.astype(bf16)
+
+    a.send(0)
+    a.recv(0, put)
+    for j in range(1, steps):
+        a.send(j)
+        if both and j == 1:
+            b.send(0)
+        a.recv(j, put)
+    z.start()
+    if both:
+        b.recv(0, put2)
+        b.send(1)
+    value = h1[...]
+    dz = z.total()
+    r = inv_rms(value)
+    weighted = dz * gain[...]
+    grad = r * weighted - value * (r * r * r) * jnp.mean(weighted * value, axis=-1, keepdims=True)
+    grad = cot[pl.ds(t * z.share, z.share), :].astype(f32) + grad
+    dh1[...] = grad
+    low[...] = grad.astype(bf16)
+    dh1r_all[t] = grad.astype(bf16)
+    gain_part[...] = jnp.broadcast_to(jnp.sum(dz * value * r, axis=0, keepdims=True), gain_part.shape)
+    x = Direct("tensor", nt, t, low, dh1r_all, xs, xr)
+    x.start()
+    if both:
+        for j in range(1, steps):
+            b.recv(j, put2)
+            if j + 1 < steps:
+                b.send(j + 1)
+        b.finish()
+    x.wait()
+    a.finish()
+    z.finish()
+    x.finish()
+
+
+def leave(n, nt, dn2, moe, h1, cot, gain, cid):
+    _, rows, cols = dn2.shape
+    share = rows // nt
+    sds, vm = jax.ShapeDtypeStruct, pltpu.VMEM
+    both = moe is not None
+    outs = [sds((share, cols), f32), sds((nt, share, cols), bf16), sds((8, cols), f32)]
+    if both:
+        outs.append(sds((rows, cols), bf16))
+    got = [vm((2, n, rows // 2, cols), bf16)] * (2 if both else 1)
+    sems = [DMA((2, n))] * (4 if both else 2) + [DMA((nt,))] * 4
+    args = (dn2, moe, h1, cot, gain) if both else (dn2, h1, cot, gain)
+    return kernel_call(
+        functools.partial(leave_kernel, n, nt, both), "leave", cid, [VM] * len(args), outs, [VM] * len(outs),
+        got + [vm((rows, cols), bf16), vm((nt, share, cols), bf16), vm((share, cols), bf16)] + sems, args)
+
+
+def fold_kernel(n, nt, p, out, got, ss, rs):
+    d = lax.axis_index("dp")
+    hello(dp_peers(n, d))
+
+    def put(rows, total):
+        out[rows, :] = total.astype(bf16)
+
+    a = Reduce(n, d, p, got, ss, rs)
+    for j in range(len(bit_list(n))):
+        a.send(j)
+        a.recv(j, put)
+    a.finish()
+
+
+def fold(n, nt, p, cid):
+    _, rows, cols = p.shape
+    return kernel_call(functools.partial(fold_kernel, n, nt), "fold", cid, [VM], jax.ShapeDtypeStruct((rows, cols), bf16), VM,
+                       [pltpu.VMEM((2, n, rows // 2, cols), bf16), DMA((2, n)), DMA((2, n))], (p,))
+
+
+def back_kernel(n, nt, count, *refs):
+    moe, h1, srcs = refs[0], refs[1], refs[2:2 + count]
+    out_all, dsts = refs[2 + count], refs[3 + count:3 + 2 * count]
+    zgot, low, zs, zr, xs, xr, gs, gr, loc = refs[3 + 2 * count:]
+    d, t = lax.axis_index("dp"), lax.axis_index("tensor")
+    greet(n, nt, d, t)
+    z = ZSum(nt, t, moe, zgot, zs, zr)
+    gathers = [Gather(n, d, srcs[i], (lambda o, i=i: dsts[i].at[o]), gs.at[i], gr.at[i]) for i in range(count)]
+    own = [pltpu.make_async_copy(srcs[i], dsts[i].at[d], loc.at[i]) for i in range(count)]
+    for g in gathers:
+        g.start()
+    z.start()
+    for c in own:
         c.start()
-        sent.append(c)
-    gathers = []
-    for m in range(nt):
-        tm = flip(t, m)
-        gathers.append(Gather(n, d, src if m == 0 else dst.at[d, tm], (lambda o, tm=tm: dst.at[o, tm]), gs.at[m], gr.at[m]))
-    gathers[0].start()
-    own.start()
-    for m in range(1, nt):
-        place = dst.at[d, flip(t, m)]
-        rdma(place, place, zs.at[m], zr.at[m], {"tensor": flip(t, m)}).wait_recv()
-        gathers[m].start()
-        gathers[m - 1].stage(0)
-        if m > 1:
-            gathers[m - 2].stage(1)
-    steps = len(bit_list(n))
-    done = [0] * nt
-    for m in range(nt):
-        done[m] = 0 if m == nt - 1 else 1 if m == nt - 2 else 2
-    for j in range(steps):
-        for m in range(nt):
-            if done[m] == j:
-                gathers[m].stage(j)
-                done[m] = j + 1
+    for g in gathers:
+        g.stage(0)
+    value = (h1[...] + z.total()).astype(bf16)
+    low[...] = value
+    out_all[t] = value
+    x = Direct("tensor", nt, t, low, out_all, xs, xr)
+    x.start()
+    for j in range(1, len(bit_list(n))):
+        for g in gathers:
+            g.stage(j)
+    x.wait()
     for g in gathers:
         g.finish()
-    for c in sent:
-        c.wait_send()
-    own.wait()
-
-
-def spread(n, nt, x, cid):
-    scratch = [pltpu.SemaphoreType.DMA((nt,))] * 2 + [pltpu.SemaphoreType.DMA((nt, 2, n))] * 2 + [pltpu.SemaphoreType.DMA]
-    out = jax.ShapeDtypeStruct((n, nt) + x.shape, x.dtype)
-    return call(functools.partial(spread_kernel, n, nt), "spread", cid, out, pl.ANY, pl.ANY, scratch, x)
-
-
-def reduce_dp(n, me, p_ref, acc, got, send_sems, recv_sems, put):
-    half = p_ref.shape[1] // 2
-    bits = bit_list(n)
-    o = [x[::-1] for x in orders(n)]
-    sent = []
-    base = 0
-    for j in range(len(bits)):
-        keeps = [span(o[h][j + 1:]) for h in (0, 1)]
-        for i in range(len(keeps[0])):
-            for h in (0, 1):
-                m, b = keeps[h][i], o[h][j]
-                src = p_ref.at[flip(me, m | b), pl.ds(h * half, half)] if j == 0 else acc.at[h, m | b]
-                c = rdma(src, got.at[h, base + i], send_sems.at[h, base + i], recv_sems.at[h, base + i], {"dp": flip(me, b)})
-                c.start()
-                sent.append(c)
-        for i in range(len(keeps[0]))[::-1]:
-            for h in (0, 1):
-                m, b = keeps[h][i], o[h][j]
-                rows = pl.ds(h * half, half)
-                view = got.at[h, base + i]
-                rdma(view, view, send_sems.at[h, base + i], recv_sems.at[h, base + i], {"dp": flip(me, b)}).wait_recv()
-                mine = p_ref[flip(me, m), rows] if j == 0 else acc[h, m]
-                total = mine.astype(f32) + view[...].astype(f32)
-                if j == len(bits) - 1:
-                    put(rows, total)
-                else:
-                    acc[h, m] = total.astype(bf16)
-        base += len(keeps[0])
-    return sent
-
-
-def fold_kernel(n, nt, p_ref, out_ref, acc, got, part, zgot, send_sems, recv_sems, zs, zr):
+    for c in own:
+        c.wait()
+    z.finish()
+    x.finish()
+
+
+def back(n, nt, moe, h1, arrs, cid):
+    rows, cols = moe.shape
+    share = rows // nt
+    sds = jax.ShapeDtypeStruct
+    k = len(arrs)
+    return kernel_call(
+        functools.partial(back_kernel, n, nt, k), "back", cid, [VM, VM] + [HB] * k,
+        [sds((nt, share, cols), bf16)] + [sds((n,) + a.shape, a.dtype) for a in arrs], [VM] + [HB] * k,
+        [pltpu.VMEM((nt, share, cols), bf16), pltpu.VMEM((share, cols), bf16)] + [DMA((nt,))] * 4 + [DMA((k, 2, n))] * 2 + [DMA((k,))],
+        (moe, h1, *arrs))
+
+
+def last_kernel(n, nt, count, *refs):
+    dnormed, hidden, gain, dh1, gains, slices, srcs = *refs[:6], refs[6:6 + count]
+    grad_all, gains_out, slices_all, dsts = *refs[6 + count:9 + count], refs[9 + count:9 + 2 * count]
+    (zgot, low, gpart, ggot, gsum, gall, zs, zr, xs, xr, gs, gr, bs, br, ps, pr, qs, qr, loc) = refs[9 + 2 * count:]
     d, t = lax.axis_index("dp"), lax.axis_index("tensor")
-    hello(dp_peers(n, d) + all_peers("tensor", nt, t))
-    share = out_ref.shape[0]
-
-    def put(rows, total):
-        part[rows, :] = total.astype(bf16)
-
-    sent = reduce_dp(n, d, p_ref, acc, got, send_sems, recv_sems, put)
-    for m in range(1, nt):
-        c = rdma(part.at[pl.ds(flip(t, m) * share, share)], zgot.at[m], zs.at[m], zr.at[m], {"tensor": flip(t, m)})
+    greet(n, nt, d, t, True)
+    z = ZSum(nt, t, dnormed, zgot, zs, zr)
+    z.start()
+    gathers = [Gather(n, d, srcs[i], (lambda o, i=i: dsts[i].at[o]), gs.at[i], gr.at[i]) for i in range(count)]
+    own = [pltpu.make_async_copy(srcs[i], dsts[i].at[d], loc.at[i]) for i in range(count)]
+    own.append(pltpu.make_async_copy(slices.at[d], slices_all.at[d], loc.at[count]))
+    for g in gathers:
+        g.start()
+    b = Direct("dp", n, d, slices, slices_all, bs, br, True)
+    b.start()
+    for c in own:
         c.start()
-        sent.append(c)
-    total = part[pl.ds(t * share, share), :].astype(f32)
-    for m in range(1, nt):
-        rdma(zgot.at[m], zgot.at[m], zs.at[m], zr.at[m], {"tensor": flip(t, m)}).wait_recv()
-        total = total + zgot[m].astype(f32)
-    out_ref[...] = total
-    for c in sent:
-        c.wait_send()
-
-
-def fold(n, nt, p, cid):
-    _, rows, cols = p.shape
-    scratch = [
-        pltpu.VMEM((2, n, rows // 2, cols), bf16),
-        pltpu.VMEM((2, n, rows // 2, cols), bf16),
-        pltpu.VMEM((rows, cols), bf16),
-        pltpu.VMEM((nt, rows // nt, cols), bf16),
-    ] + [pltpu.SemaphoreType.DMA((2, n))] * 2 + [pltpu.SemaphoreType.DMA((nt,))] * 2
-    out = jax.ShapeDtypeStruct((rows // nt, cols), f32)
-    return call(functools.partial(fold_kernel, n, nt), "fold", cid, out, pltpu.VMEM, pltpu.VMEM, scratch, p)
-
-
-def zsum_kernel(nt, x_ref, out_ref, zgot, zs, zr):
-    t = lax.axis_index("tensor")
-    hello(all_peers("tensor", nt, t))
-    share = out_ref.shape[0]
-    sent = []
-    for m in range(1, nt):
-        c = rdma(x_ref.at[pl.ds(flip(t, m) * share, share)], zgot.at[m], zs.at[m], zr.at[m], {"tensor": flip(t, m)})
-        c.start()
-        sent.append(c)
-    total = x_ref[pl.ds(t * share, share), :].astype(f32)
-    for m in range(1, nt):
-        rdma(zgot.at[m], zgot.at[m], zs.at[m], zr.at[m], {"tensor": flip(t, m)}).wait_recv()
-        total = total + zgot[m].astype(f32)
-    out_ref[...] = total
-    for c in sent:
-        c.wait_send()
-
-
-def zsum(nt, x, cid):
-    rows, cols = x.shape
-    scratch = [pltpu.VMEM((nt, rows // nt, cols), x.dtype)] + [pltpu.SemaphoreType.DMA((nt,))] * 2
-    out = jax.ShapeDtypeStruct((rows // nt, cols), f32)
-    return call(functools.partial(zsum_kernel, nt), "zsum", cid, out, pltpu.VMEM, pltpu.VMEM, scratch, x)
+    for g in gathers:
+        g.stage(0)
+    dz = z.total()
+    value = hidden[pl.ds(t * z.share, z.share), :].astype(f32)
+    r = inv_rms(value)
+    weighted = dz * gain[...]
+    grad = r * weighted - value * (r * r * r) * jnp.mean(weighted * value, axis=-1, keepdims=True)
+    grad = (dh1[...] + grad).astype(bf16)
+    low[...] = grad
+    grad_all[t] = grad
+    x = Direct("tensor", nt, t, low, grad_all, xs, xr)
+    x.start()
+    row = jnp.sum(dz * value * r, axis=0, keepdims=True)
+    first = lax.broadcasted_iota(jnp.int32, gains.shape, 0) == 0
+    whole = jnp.where(first, row, gains[...])
+    width = gpart.shape[2]
+    for i in range(n):
+        gpart[i] = whole[:, i * width:(i + 1) * width]
+    p = Direct("dp", n, d, gpart, ggot, ps, pr, True)
+    p.start()
+    for j in range(1, len(bit_list(n))):
+        for g in gathers:
+            g.stage(j)
+    p.wait()
+    total = gpart[d]
+    for m in range(1, n):
+        total = total + ggot[flip(d, m)]
+    gsum[...] = total
+    gall[t] = total
+    q = Direct("tensor", nt, t, gsum, gall, qs, qr)
+    q.start()
+    b.wait()
+    x.wait()
+    q.wait()
+    total = gall[0]
+    for i in range(1, nt):
+        total = total + gall[i]
+    gains_out[...] = total
+    for g in gathers:
+        g.finish()
+    for c in own:
+        c.wait()
+    for e in (z, x, b, p, q):
+        e.finish()
+
+
+def last(n, nt, dnormed, hidden, gain, dh1, gains, slices, arrs, cid):
+    rows, cols = dnormed.shape
+    share = rows // nt
+    width = cols // n
+    sds, vm = jax.ShapeDtypeStruct, pltpu.VMEM
+    k = len(arrs)
+    return kernel_call(
+        functools.partial(last_kernel, n, nt, k), "last", cid, [VM] * 5 + [HB] * (k + 1),
+        [sds((nt, share, cols), bf16), sds((8, width), f32), sds(slices.shape, bf16)] + [sds((n,) + a.shape, a.dtype) for a in arrs],
+        [VM, VM, HB] + [HB] * k,
+        [vm((nt, share, cols), bf16), vm((share, cols), bf16), vm((n, 8, width), f32), vm((n, 8, width), f32), vm((8, width), f32),
+         vm((nt, 8, width), f32)] + [DMA((nt,))] * 4 + [DMA((k, 2, n))] * 2 + [DMA((n,))] * 4 + [DMA((nt,))] * 2 + [DMA((k + 1,))],
+        (dnormed, hidden, gain, dh1, gains, slices, *arrs))
+
+
+def weight_grad_kernel(order, a_ref, b_ref, out_ref):
+    res = contract(a_ref[...], b_ref[...], 0, 0)
+    rows = res.shape[0]
+    for c, j in enumerate(order):
+        out_ref[pl.ds(j, rows, stride=len(order)), :] = res[:, c * 128:(c + 1) * 128]
+
+
+def weight_grad(a, b, order):
+    toks, rows = a.shape
+    block = 256
+    return pl.pallas_call(
+        functools.partial(weight_grad_kernel, order),
+        grid=(rows // block,),
+        in_specs=[pl.BlockSpec((toks, block), lambda i: (0, i)), pl.BlockSpec((toks, b.shape[1]), lambda i: (0, 0))],
+        out_specs=pl.BlockSpec((block * len(order), 128), lambda i: (i, 0)),
+        out_shape=jax.ShapeDtypeStruct((rows * len(order), 128), f32),
+        name="weight_grad",
+    )(a, b)
 
 
 def direct_kernel(axis, n, split, count, *refs):
@@ -382,12 +705,8 @@
 
     coef = routing(experts, gates, num_exp, capacity).T
     place = jnp.broadcast_to(anchor[None, :], (16, toks))
-    wq, wk, wv, wo, dy_all, coef_all, anchor_all = gather_dp(
-        n, (query_weight, key_weight, value_weight, output_weight, cotangent, coef, place), 1)
-    wq, wk, wv, wo = (w.reshape(D, cols) for w in (wq, wk, wv, wo))
-    dy_all = dy_all.reshape(n * toks, D)
-    coef_all = lax.dynamic_slice_in_dim(coef_all, d * exp_local, exp_local, 1)
-    coef_all = coef_all.transpose(0, 2, 1).reshape(n * toks, exp_local)
+    wq, wk, wv, anchor_all = gather_dp(n, (query_weight, key_weight, value_weight, place), 1)
+    wq, wk, wv = (w.reshape(D, cols) for w in (wq, wk, wv))
     anchor_all = anchor_all[:, 0].reshape(n * toks)
 
     docs, positions = locate(anchor, lengths)
@@ -399,7 +718,9 @@
     inv = lax.rsqrt(jnp.mean(hidden * hidden, axis=-1, keepdims=True) + EPSILON)
     normed = (hidden * inv * attn_gain).astype(bf16)
     q_raw, k_raw, v_raw = (contract(normed, w, 1, 0) for w in (wq, wk, wv))
-    (sq,) = direct("tensor", nt, [small([jnp.sum(q_raw * q_raw, axis=1), jnp.sum(k_raw * k_raw, axis=1)])], 2)
+    sq = small([jnp.sum(q_raw * q_raw, axis=1), jnp.sum(k_raw * k_raw, axis=1)])
+    sq, wo = stats(n, nt, sq, output_weight, 2)
+    wo = wo.reshape(D, cols)
     sq = jnp.sum(sq, axis=0)
     q_inv = lax.rsqrt(sq[0] / D + EPSILON)[:, None]
     k_inv = lax.rsqrt(sq[1] / D + EPSILON)[:, None]
@@ -418,9 +739,11 @@
     attended = jnp.einsum("hqk,khd->qhd", probs.astype(bf16), v_all, preferred_element_type=f32)
     attended = attended / total.T[:, :, None]
     o = attended.reshape(toks, cols).astype(bf16)
-    h1 = mine(hidden) + zsum(nt, contract(o, wo, 1, 1).astype(bf16), 4)
-    n2 = (h1 * lax.rsqrt(jnp.mean(h1 * h1, axis=-1, keepdims=True) + EPSILON) * moe_gain).astype(bf16)
-    n2_all = spread(n, nt, n2, 5).reshape(n * toks, D)
+    n2_all, h1, dy_all, coef_all = enter(
+        n, nt, contract(o, wo, 1, 1).astype(bf16), hidden_in, moe_gain[None, :], cotangent, coef, 4)
+    n2_all, dy_all = n2_all.reshape(n * toks, D), dy_all.reshape(n * toks, D)
+    coef_all = lax.dynamic_slice_in_dim(coef_all, d * exp_local, exp_local, 1)
+    coef_all = coef_all.transpose(0, 2, 1).reshape(n * toks, exp_local)
 
     gu = jnp.einsum("td,dezf->tezf", n2_all, expert_gate_up, preferred_element_type=f32)
     g, u = gu[:, :, 0], gu[:, :, 1]
@@ -430,28 +753,26 @@
     dgu = jnp.stack([dact * u * sig * (1.0 + g * (1.0 - sig)), dact * (g * sig)], axis=2).astype(bf16)
     dn2 = jnp.einsum("tezf,dezf->td", dgu, expert_gate_up, preferred_element_type=f32).astype(bf16)
     moe = jnp.einsum("tef,def->td", act, expert_down, preferred_element_type=f32).astype(bf16)
-    down_grad = jnp.einsum("td,tef->def", dy_all, act, preferred_element_type=f32)
-    gate_up_grad = jnp.einsum("td,tezf->dezf", n2_all, dgu, preferred_element_type=f32)
-
-    dn2 = fold(n, nt, dn2.reshape(n, toks, D), 6)
-    dres, moe_gain_part = norm_back(h1, moe_gain, dn2)
-    dh1 = mine(cotangent).astype(f32) + dres
-    moe = fold(n, nt, moe.reshape(n, toks, D), 7)
-    out_share = (h1 + moe).astype(bf16)
-    dh1r, output = direct("tensor", nt, [dh1.astype(bf16), out_share], 8)
+    half = expert_down.shape[2] // 128
+    down_grad = weight_grad(dy_all, act.reshape(n * toks, -1), [f * exp_local + e for e in range(exp_local) for f in range(half)])
+    down_grad = down_grad.reshape(D, half, exp_local, 128).transpose(0, 2, 1, 3).reshape(expert_down.shape)
+    gate_up_grad = weight_grad(n2_all, dgu.reshape(n * toks, -1),
+                               [(e * half + f) * 2 + z for e in range(exp_local) for z in (0, 1) for f in range(half)])
+    gate_up_grad = gate_up_grad.reshape(D, exp_local, half, 2, 128).transpose(0, 1, 3, 2, 4).reshape(expert_gate_up.shape)
+
+    dn2, moe = dn2.reshape(n, toks, D), moe.reshape(n, toks, D)
+    together = 16 * n * toks * D <= 48 * 2**20
+    dh1, dh1r, moe_gain_part, *rest = leave(n, nt, dn2, moe if together else None, h1, cotangent, moe_gain[None, :], 6)
+    moe = rest[0] if together else fold(n, nt, moe, 7)
     dh1r = dh1r.reshape(toks, D)
-    output = output.reshape(toks, D)
 
     do = contract(dh1r, wo, 1, 0).astype(bf16)
     delta = jnp.sum(do.reshape(toks, heads, HD).astype(f32) * attended, axis=2).T
-    stats = small(list(lse) + list(delta))
-    if stats.shape[0] % 16:
-        stats = jnp.pad(stats, ((0, 8), (0, 0)))
-    q_all, do_all, o_all, stats_all = gather_dp(n, (q.reshape(toks, cols), do, o, stats), 9)
-    slices, = direct("dp", n, [jnp.concatenate([normed, dh1r], axis=0).reshape(2 * toks, n, D // n).transpose(1, 0, 2)], 10, True)
-    normed_all = slices[:, :toks].reshape(n * toks, D // n)
-    dh1r_all = slices[:, toks:].reshape(n * toks, D // n)
-    output_grad = contract(dh1r_all, o_all.reshape(n * toks, cols), 0, 0)
+    terms = small(list(lse) + list(delta))
+    if terms.shape[0] % 16:
+        terms = jnp.pad(terms, ((0, 8), (0, 0)))
+    output, q_all, do_all, o_all, stats_all = back(n, nt, moe, h1, (q.reshape(toks, cols), do, o, terms), 9)
+    output = output.reshape(toks, D)
 
     do = do.reshape(toks, heads, HD)
     q_all, do_all = (a.reshape(n * toks, heads, HD) for a in (q_all, do_all))
@@ -479,21 +800,20 @@
     dq_raw = (q_inv * wdq - q_raw * q_inv**3 * cross[0][:, None] / D).astype(bf16)
     dk_raw = (k_inv * wdk - k_raw * k_inv**3 * cross[1][:, None] / D).astype(bf16)
     dnormed = contract(dq_raw, wq, 1, 1) + contract(dk_raw, wk, 1, 1) + contract(dv, wv, 1, 1)
-    dnormed = zsum(nt, dnormed.astype(bf16), 12)
-    dx, attn_gain_part = norm_back(mine(hidden), attn_gain, dnormed)
 
     def wide(part):
         return lax.dynamic_update_slice_in_dim(jnp.zeros((D,), f32), part, t * cols, 0)
 
-    gains = small([attn_gain_part, wide(q_gain_part), wide(k_gain_part), moe_gain_part])
-    gains = jnp.concatenate([gains, jnp.zeros_like(gains)], axis=0)
-    dq_all, dk_all, dv_all, gains_all = gather_dp(n, (dq_raw, dk_raw, dv, gains), 13)
+    gains = small([jnp.zeros((D,), f32), wide(q_gain_part), wide(k_gain_part), moe_gain_part[0]])
+    slices = jnp.concatenate([normed, dh1r], axis=0).reshape(2 * toks, n, D // n).transpose(1, 0, 2)
+    input_grad, gains, slices, dq_all, dk_all, dv_all = last(
+        n, nt, dnormed.astype(bf16), hidden_in, attn_gain[None, :], dh1, gains, slices, (dq_raw, dk_raw, dv), 12)
+    normed_all = slices[:, :toks].reshape(n * toks, D // n)
+    dh1r_all = slices[:, toks:].reshape(n * toks, D // n)
+    output_grad = contract(dh1r_all, o_all.reshape(n * toks, cols), 0, 0)
     query_grad, key_grad, value_grad = (
         contract(normed_all, a.reshape(n * toks, cols), 0, 0) for a in (dq_all, dk_all, dv_all))
-    gains = lax.dynamic_slice_in_dim(jnp.sum(gains_all[:, :8], axis=0), d * (D // n), D // n, 1)
-    input_grad, gains = direct("tensor", nt, [(dh1 + dx).astype(bf16), gains], 14)
     input_grad = input_grad.reshape(toks, D).astype(f32)
-    gains = jnp.sum(gains, axis=0)
     return (output, input_grad, query_grad, key_grad, value_grad, output_grad, gate_up_grad, down_grad,
             gains[0], gains[1], gains[2], gains[3])
 

time: 518 us -> 414 us (0.80)
  Pallas kernels: 332 us -> 260 us
  matrix products: 75.7 us -> 58.7 us
  other arithmetic: 40.2 us -> 30 us
  local copies, waits for them, and re-layouts: 64.2 us -> 57.6 us
    pallas_call x14 -> x3, Pallas kernels: 332 us -> 55.8 us  [call(): pl.pallas_call(kernel, out_shape=outs, in_specs=[pl.BlockSpec(memory_spac...]
    pallas_call x0 -> x7, Pallas kernels: none -> 204 us  [the longest x5 184 us: kernel_call(): pl.pallas_call(kernel, out_shape=outs, in_specs=in_specs, out_specs=out_s...]
    unnamed x163 -> x140, local copies, waits for them, and re-layouts: 37.9 us -> 10 us
    dot_general x2 -> x0, matrix products: 8.4 us -> none  [the longest x1 5.8 us: shards(): jnp.einsum('td,tezf->dezf', n2_all, dgu, preferred_element_type=f32)]
    convert_element_type x1 -> x2, local copies, waits for them, and re-layouts: 0.27 us -> 8.49 us  [shards(): jnp.stack([dact * u * sig * (1.0 + g * (1.0 - sig)), dact * (g * sig)], a...]
    reduce_sum x5 -> x0, other arithmetic: 6.35 us -> none  [the longest x2 3.58 us: norm_back(): return (grad_in, jnp.sum(grad_out * values * inv_rms, axis=0))]
    squeeze x0 -> x2, local copies, waits for them, and re-layouts: none -> 5.93 us  [shards(): g, u = (gu[:, :, 0], gu[:, :, 1])]
    slice x0 -> x2, local copies, waits for them, and re-layouts: none -> 5.75 us  [the longest x1 4.91 us: shards(): g, u = (gu[:, :, 0], gu[:, :, 1])]
where the time goes in v2:
time: 414 us; the launch traced here: 408 us
  Pallas kernels  260 us (63%)
  matrix products  58.7 us (14%)
  local copies, waits for them, and re-layouts  57.6 us (14%)
  other arithmetic  30 us (7%)
    pallas_call x5, Pallas kernels, kernel_call(): pl.pallas_call(kernel, out_shape=outs, in_specs=in_specs, out_specs=out_s...  184 us
    pallas_call x3, Pallas kernels, call(): pl.pallas_call(kernel, out_shape=outs, in_specs=[pl.BlockSpec(memory_spac...  55.8 us
    dot_general x13, matrix products, contract(): lax.dot_general(left, right, (((l,), (r,)), ((), ())), preferred_element_...  20.9 us
    pallas_call x2, Pallas kernels, weight_grad(): pl.pallas_call(functools.partial(weight_grad_kernel, order), grid=(rows /...  19.8 us
    unnamed x140, local copies, waits for them, and re-layouts  10 us
    convert_element_type x2, local copies, waits for them, and re-layouts, shards(): jnp.stack([dact * u * sig * (1.0 + g * (1.0 - sig)), dact * (g * sig)], a...  8.49 us

profile of v2, /device:TPU:0, one launch (start us, length us, event | category | flops | bytes accessed | tf_op | source)
XLA Modules:
  0.0 408.3 jit_solution(12384834661183536343)
XLA Ops:
  2.1 33.4 %gather_dp.2 = (bf16[8,256,512]{2,1,0:T(8,128)(2,1)}, bf16[8,256,512]{2,1,0:T(8,128)(2,1)}, bf16[8,256,512]{2,1,0:T(8,128)(2,1)}, s32[8,16,128]{2,1,0:T(8,128)}) custom-call(bf16[256,512]{1,0:T(8,128)(2,1)} %refs_0_.1, bf16[256,512]{1,0:T(8,128)(2,1)} %refs_1_.2, bf16[256,512]{1,0:T(8,128)(2,1)} %refs_2_.1, s32[16,128]{1,0:T(8,128)} %broadcast_in_dim.64.refs_3_), custom_call_target="tpu_custom_call" | custom-call | tf_op jit(solution)/shard_map/gather_dp/pallas_call | solution.py:104
  43.8 2.3 multiply_reduce_fusion.5
  47.4 17.3 %stats.1 = (f32[4,8,128]{2,1,0:T(8,128)}, bf16[8,256,512]{2,1,0:T(8,128)(2,1)}) custom-call(f32[8,128]{1,0:T(8,128)} %select_maximum_fusion.5.sq, bf16[256,512]{1,0:T(8,128)(2,1)} %wo.1), custom_call_target="tpu_custom_call" | custom-call | tf_op jit(solution)/shard_map/stats/pallas_call | solution.py:285
  73.3 2.7 convolution_convert_fusion.2.refs_1_
  76.1 13.8 %gather_dp.3 = (bf16[8,128,512]{2,1,0:T(8,128)(2,1)}, bf16[8,128,512]{2,1,0:T(8,128)(2,1)}) custom-call(bf16[128,512]{1,0:T(8,128)(2,1)} %fusion.51.refs_0_, bf16[128,512]{1,0:T(8,128)(2,1)} %convolution_convert_fusion.2.refs_1_), custom_call_target="tpu_custom_call" | custom-call | tf_op jit(solution)/shard_map/gather_dp/pallas_call | solution.py:104
  89.9 2.3 reshape.387
  92.2 2.4 copy.140
  101.0 3.5 fusion.85
  107.0 46.4 %enter.1 = (bf16[8,4,32,2048]{3,2,1,0:T(8,128)(2,1)}, f32[32,2048]{1,0:T(8,128)}, bf16[8,128,2048]{2,1,0:T(8,128)(2,1)}, f32[8,16,128]{2,1,0:T(8,128)}) custom-call(bf16[128,2048]{1,0:T(8,128)(2,1)} %convolution_convert_fusion.part, bf16[128,2048]{1,0:T(8,128)(2,1)} %refs_1_.3, f32[1,2048]{1,0:T(1,128)} %bitcast.269, bf16[128,2048]{1,0:T(8,128)(2,1)} %refs_3_.1, ...), custom_call_target="tpu_custom_call" | custom-call | tf_op jit(solution)/shard_map/enter/pallas_call | solution.py:285
  154.2 7.8 %fusion = f32[1024,2,2,256]{0,3,1,2:T(8,128)S(1)} fusion(bf16[1024,2048,1,1]{1,0,2,3:T(8,128)(2,1)} %bitcast.243, bf16[2048,2,2,256]{3,2,1,0:T(2,128)(2,1)} %param.25), kind=kOutput, calls=%fused_computation.3 | convolution fusion | flops 4294967296 | bytes 12582912 | tf_op jit(solution)/shard_map/td,dezf->tezf/dot_general | solution.py:748
  162.1 3.1 fusion.10
  165.7 6.5 %bitcast_convert_fusion = bf16[1024,2048]{1,0:T(8,128)(2,1)} fusion(bf16[2048,2,2,256]{3,2,1,0:T(2,128)(2,1)S(1)} %copy-done.63, bf16[1024,2,1,256]{0,3,1,2:T(8,128)(2,1)S(1)} %get-tuple-element.75, bf16[1024,2,1,256]{0,3,1,2:T(8,128)(2,1)S(1)} %get-tuple-element.74), kind=kOutput, calls=%fused_computation | convolution fusion | flops 4298113024 | bytes 10485760 | tf_op jit(solution)/shard_map/tezf,dezf->td/dot_general | solution.py:754
  172.2 4.6 %bitcast_convert_fusion.1 = bf16[1024,2048]{1,0:T(8,128)(2,1)} fusion(bf16[2048,2,256]{2,1,0:T(2,128)(2,1)S(1)} %copy-done, f32[1024,2]{0,1:T(2,128)S(1)} %dynamic-slice_bitcast_fusion, f32[1024,2,2,256]{0,3,1,2:T(8,128)S(1)} %fusion), kind=kOutput, calls=%fused_computation.1 | convolution fusion | flops 2153250816 | bytes 10493952 | tf_op jit(solution)/shard_map/tef,def->td/dot_general | solution.py:755
  176.9 55.4 %leave.1 = (f32[32,2048]{1,0:T(8,128)}, bf16[4,32,2048]{2,1,0:T(8,128)(2,1)}, f32[8,2048]{1,0:T(8,128)}, bf16[128,2048]{1,0:T(8,128)(2,1)}) custom-call(bf16[8,128,2048]{2,1,0:T(8,128)(2,1)} %bitcast.248, bf16[8,128,2048]{2,1,0:T(8,128)(2,1)} %bitcast.249, f32[32,2048]{1,0:T(8,128)} %get-tuple-element.50.refs_2_.refs_1_, bf16[128,2048]{1,0:T(8,128)(2,1)} %refs_3_.1, ...), custom_call_target="tpu_custom_call" | custom-call | tf_op jit(solution)/shard_map/leave/pallas_call | solution.py:285
  235.6 3.5 broadcast_multiply_fusion.1
  242.9 29.1 %back.1 = (bf16[4,32,2048]{2,1,0:T(8,128)(2,1)}, bf16[8,128,512]{2,1,0:T(8,128)(2,1)}, bf16[8,128,512]{2,1,0:T(8,128)(2,1)}, bf16[8,128,512]{2,1,0:T(8,128)(2,1)}, f32[8,16,128]{2,1,0:T(8,128)}) custom-call(bf16[128,2048]{1,0:T(8,128)(2,1)} %get-tuple-element.51.refs_0_, f32[32,2048]{1,0:T(8,128)} %get-tuple-element.50.refs_2_.refs_1_, ...), custom_call_target="tpu_custom_call" | custom-call | tf_op jit(solution)/shard_map/back/pallas_call | solution.py:285
  275.4 2.8 exponential_select_fusion
  280.4 2.4 copy.148
  282.8 3.3 broadcast_multiply_fusion
  292.5 8.6 %direct_tensor.1 = f32[4,8,128]{2,1,0:T(8,128)} custom-call(f32[8,128]{1,0:T(8,128)} %select_maximum_fusion.4.refs_0_), custom_call_target="tpu_custom_call" | custom-call | tf_op jit(solution)/shard_map/direct_tensor/pallas_call | solution.py:104
  302.9 2.5 fusion.92
  314.7 36.2 %last.1 = (bf16[4,32,2048]{2,1,0:T(8,128)(2,1)}, f32[8,256]{1,0:T(8,128)}, bf16[8,256,256]{2,1,0:T(8,128)(2,1)}, bf16[8,128,512]{2,1,0:T(8,128)(2,1)}, bf16[8,12...) custom-call(bf16[128,2048]{1,0:T(8,128)(2,1)} %fusion.3.refs_0_, bf16[128,2048]{1,0:T(8,128)(2,1)} %refs_1_.3, ...), custom_call_target="tpu_custom_call" | custom-call | tf_op jit(solution)/shard_map/last/pallas_call | solution.py:285
  350.9 2.3 bitcast_convert_fusion.2
  353.2 2.7 convolution_bitcast_fusion.3
  359.9 4.0 copy.156
  363.9 4.4 %convert_element_type.137.b_ref = bf16[1024,1024]{1,0:T(8,128)(2,1)} reshape(bf16[1024,2,2,256]{3,2,1,0:T(2,128)(2,1)} %copy.156) | data formatting | bytes 4194304 | tf_op jit(solution)/shard_map/convert_element_type | solution.py:753
  368.4 11.2 %weight_grad.2 = f32[16384,128]{1,0:T(8,128)} custom-call(bf16[1024,2048]{1,0:T(8,128)(2,1)} %bitcast.244, bf16[1024,1024]{1,0:T(8,128)(2,1)} %convert_element_type.137.b_ref), custom_call_target="tpu_custom_call" | custom-call | tf_op jit(solution)/shard_map/weight_grad/pallas_call | solution.py:588
  383.0 4.9 %fusion.79 = (f32[1024,2,1,256]{0,3,1,2:T(8,128)}, f32[1024,2,1,256]{0,3,1,2:T(8,128)}) fusion(f32[1024,2,2,256]{0,3,1,2:T(8,128)} %copy-done.10), kind=kLoop, calls=%fused_computation.167 | loop fusion | bytes 8388608 | tf_op jit(solution)/shard_map/slice | solution.py:749
  387.9 2.9 copy.179
  390.9 3.0 copy.178
  393.8 4.0 multiply_convert_fusion.b_ref
  397.9 8.6 %weight_grad.3 = f32[8192,128]{1,0:T(8,128)} custom-call(bf16[1024,2048]{1,0:T(8,128)(2,1)} %bitcast.245, bf16[1024,512]{1,0:T(8,128)(2,1)} %multiply_convert_fusion.b_ref), custom_call_target="tpu_custom_call" | custom-call | tf_op jit(solution)/shard_map/weight_grad/pallas_call | solution.py:588
  (221 shorter events, 68.1 us)
Async XLA Ops:
  0.6 161.4 %copy-start = (bf16[2048,2,256]{2,1,0:T(2,128)(2,1)S(1)}, bf16[2048,2,256]{2,1,0:T(2,128)(2,1)}, u32[]{:S(2)}) copy-start(bf16[2048,2,256]{2,1,0:T(2,128)(2,1)} %param.26) | copy-start | bytes 6291460
  0.7 42.8 %copy-start.42 = (f32[2048]{0:T(1024)S(1)}, f32[2048]{0:T(1024)}, u32[]{:S(2)}) copy-start(f32[2048]{0:T(1024)} %param.17) | copy-start | bytes 24580
  36.3 4.2 %copy-start.38 = (s32[8,1,128]{2,1,0:T(1,128)}, s32[8,1,128]{2,1,0:T(1,128)S(1)}, u32[]{:S(2)}) copy-start(s32[8,1,128]{2,1,0:T(1,128)S(1)} %slice.79) | copy-start | bytes 12292
  37.9 8.2 %copy-start.60 = (s32[128]{0:T(128)}, s32[128]{0:T(128)S(1)}, u32[]{:S(2)}) copy-start(s32[128]{0:T(128)S(1)} %convert_reduce_fusion.1) | copy-start | bytes 1540
  38.8 62.3 %copy-start.24 = (pred[128,1024]{1,0:T(8,128)(4,1)}, pred[128,1024]{1,0:T(8,128)(4,1)S(1)}, u32[]{:S(2)}) copy-start(pred[128,1024]{1,0:T(8,128)(4,1)S(1)} %compare_and_fusion.1) | copy-start | bytes 393220
  46.2 19.8 %copy-start.43 = (f32[512]{0:T(512)S(1)}, f32[512]{0:T(512)}, u32[]{:S(2)}) copy-start(f32[512]{0:T(512)} %param.23) | copy-start | bytes 6148
  46.2 19.8 %copy-start.47 = (f32[512]{0:T(512)S(1)}, f32[512]{0:T(512)}, u32[]{:S(2)}) copy-start(f32[512]{0:T(512)} %param.22) | copy-start | bytes 6148
  65.9 5.0 %copy-start.51 = (f32[128]{0:T(128)}, f32[128]{0:T(128)S(1)}, u32[]{:S(2)}) copy-start(f32[128]{0:T(128)S(1)} %get-tuple-element.102) | copy-start | bytes 1540
  65.9 173.4 %copy-start.53 = (f32[128]{0:T(128)}, f32[128]{0:T(128)S(1)}, u32[]{:S(2)}) copy-start(f32[128]{0:T(128)S(1)} %get-tuple-element.73) | copy-start | bytes 1540
  98.9 5.7 %copy-start.57 = (f32[4,128]{1,0:T(4,128)}, f32[4,128]{1,0:T(4,128)S(1)}, u32[]{:S(2)}) copy-start(f32[4,128]{1,0:T(4,128)S(1)} %fusion.17) | copy-start | bytes 6148
  154.2 18.1 %copy-start.45 = (f32[1024,2]{0,1:T(2,128)}, f32[1024,2]{0,1:T(2,128)S(1)}, u32[]{:S(2)}) copy-start(f32[1024,2]{0,1:T(2,128)S(1)} %dynamic-slice_bitcast_fusion) | copy-start | bytes 24580
  154.2 7.9 %copy-start.9 = (bf16[8,128,2048]{2,1,0:T(8,128)(2,1)S(1)}, bf16[8,128,2048]{2,1,0:T(8,128)(2,1)}, u32[]{:S(2)}) copy-start(bf16[8,128,2048]{2,1,0:T(8,128)(2,1)} %get-tuple-element.48) | copy-start | bytes 12582916
  162.0 10.2 %copy-start.10 = (f32[1024,2,2,256]{0,3,1,2:T(8,128)}, f32[1024,2,2,256]{0,3,1,2:T(8,128)S(1)}, u32[]{:S(2)}) copy-start(f32[1024,2,2,256]{0,3,1,2:T(8,128)S(1)} %fusion) | copy-start | bytes 12582916
  165.1 7.1 %copy-start.29 = (bf16[1024,2,1,256]{0,3,1,2:T(8,128)(2,1)}, bf16[1024,2,1,256]{0,3,1,2:T(8,128)(2,1)S(1)}, u32[]{:S(2)}) copy-start(bf16[1024,2,1,256]{0,3,1,2:T(8,128)(2,1)S(1)} %get-tuple-element.74) | copy-start | bytes 3145732
  165.1 7.1 %copy-start.31 = (bf16[1024,2,1,256]{0,3,1,2:T(8,128)(2,1)}, bf16[1024,2,1,256]{0,3,1,2:T(8,128)(2,1)S(1)}, u32[]{:S(2)}) copy-start(bf16[1024,2,1,256]{0,3,1,2:T(8,128)(2,1)S(1)} %get-tuple-element.75) | copy-start | bytes 3145732
  176.9 55.4 %copy-start.7 = (bf16[8,256,512]{2,1,0:T(8,128)(2,1)S(1)}, bf16[8,256,512]{2,1,0:T(8,128)(2,1)}, u32[]{:S(2)}) copy-start(bf16[8,256,512]{2,1,0:T(8,128)(2,1)} %get-tuple-element.46) | copy-start | bytes 6291460
  233.8 5.3 %copy-start.23 = (bf16[128,512]{1,0:T(8,128)(2,1)}, bf16[128,512]{1,0:T(8,128)(2,1)S(1)}, u32[]{:S(2)}) copy-start(bf16[128,512]{1,0:T(8,128)(2,1)S(1)} %convolution_convert_fusion.1.refs_3_) | copy-start | bytes 393220
  239.4 32.7 %copy-start.15 = (f32[128,512]{1,0:T(8,128)}, f32[128,512]{1,0:T(8,128)S(1)}, u32[]{:S(2)}) copy-start(f32[128,512]{1,0:T(8,128)S(1)} %copy.174) | copy-start | bytes 786436
  278.2 4.6 %copy-start.22 = (bf16[128,512]{1,0:T(8,128)(2,1)S(1)}, bf16[128,512]{1,0:T(8,128)(2,1)}, u32[]{:S(2)}) copy-start(bf16[128,512]{1,0:T(8,128)(2,1)} %convolution_convert_fusion.2.refs_1_) | copy-start | bytes 393220
  286.1 15.7 %copy-start.48 = (f32[512]{0:T(512)S(1)}, f32[512]{0:T(512)}, u32[]{:S(2)}) copy-start(f32[512]{0:T(512)} %param.22) | copy-start | bytes 6148
  286.1 15.7 %copy-start.54 = (f32[128]{0:T(128)S(1)}, f32[128]{0:T(128)}, u32[]{:S(2)}) copy-start(f32[128]{0:T(128)} %copy-done.53) | copy-start | bytes 1540
  291.2 14.3 %copy-start.44 = (f32[512]{0:T(512)S(1)}, f32[512]{0:T(512)}, u32[]{:S(2)}) copy-start(f32[512]{0:T(512)} %param.23) | copy-start | bytes 6148
  291.2 14.3 %copy-start.52 = (f32[128]{0:T(128)S(1)}, f32[128]{0:T(128)}, u32[]{:S(2)}) copy-start(f32[128]{0:T(128)} %copy-done.51) | copy-start | bytes 1540
  302.9 4.2 %copy-start.20 = (bf16[128,512]{1,0:T(8,128)(2,1)}, bf16[128,512]{1,0:T(8,128)(2,1)S(1)}, u32[]{:S(2)}) copy-start(bf16[128,512]{1,0:T(8,128)(2,1)S(1)} %subtract_convert_fusion.1.refs_6_) | copy-start | bytes 393220
  308.1 4.3 %copy-start.19 = (bf16[4,32,2048]{2,1,0:T(8,128)(2,1)S(1)}, bf16[4,32,2048]{2,1,0:T(8,128)(2,1)}, u32[]{:S(2)}) copy-start(bf16[4,32,2048]{2,1,0:T(8,128)(2,1)} %get-tuple-element.52) | copy-start | bytes 1572868
  350.9 5.0 %copy-start.65 = (bf16[8,256,256]{2,1,0:T(8,128)(2,1)S(1)}, bf16[8,256,256]{2,1,0:T(8,128)(2,1)}, u32[]{:S(2)}) copy-start(bf16[8,256,256]{2,1,0:T(8,128)(2,1)} %get-tuple-element.60) | copy-start | bytes 3145732
  350.9 5.0 %copy-start.67 = (bf16[8,128,512]{2,1,0:T(8,128)(2,1)S(1)}, bf16[8,128,512]{2,1,0:T(8,128)(2,1)}, u32[]{:S(2)}) copy-start(bf16[8,128,512]{2,1,0:T(8,128)(2,1)} %get-tuple-element.62) | copy-start | bytes 3145732
  353.2 4.0 copy-start.66
  368.3 11.2 %copy-start.46 = (f32[1024,2]{0,1:T(2,128)S(1)}, f32[1024,2]{0,1:T(2,128)}, u32[]{:S(2)}) copy-start(f32[1024,2]{0,1:T(2,128)} %copy-done.45) | copy-start | bytes 24580
  397.9 8.6 %copy-start.62 = (f32[8,256]{1,0:T(8,128)S(1)}, f32[8,256]{1,0:T(8,128)}, u32[]{:S(2)}) copy-start(f32[8,256]{1,0:T(8,128)} %get-tuple-element.65) | copy-start | bytes 24580
  397.9 9.2 %copy-start.35 = (bf16[4,32,2048]{2,1,0:T(8,128)(2,1)S(1)}, bf16[4,32,2048]{2,1,0:T(8,128)(2,1)}, u32[]{:S(2)}) copy-start(bf16[4,32,2048]{2,1,0:T(8,128)(2,1)} %get-tuple-element.53) | copy-start | bytes 1572868
  397.9 10.0 %copy-start.1 = (bf16[2048,2,256]{2,1,0:T(2,128)(2,1)S(1)}, bf16[2048,2,256]{2,1,0:T(2,128)(2,1)}, u32[]{:S(2)}) copy-start(bf16[2048,2,256]{2,1,0:T(2,128)(2,1)} %param.26) | copy-start | bytes 6291460
  (36 other events, 83.9 us)

commit v3 on v2

--- a/solution.py
+++ b/solution.py
@@ -288,29 +288,64 @@
     )(*args)
 
 
-def stats_kernel(n, nt, sq, wo, sq_all, wo_all, ss, rs, gs, gr, loc):
+def across(column, lanes):
+    return jnp.transpose(jnp.broadcast_to(column, (column.shape[0], lanes)))
+
+
+def mix_kernel(n, nt, q_raw, k_raw, v, cosine, sine, q_gain, k_gain, wo, q, k, k_all, v_all, wo_all, sums,
+               sq, sq_all, ss, rs, ws, wr, ks, kr, vs, vr, loc):
     d, t = lax.axis_index("dp"), lax.axis_index("tensor")
     greet(n, nt, d, t)
+    row = lax.broadcasted_iota(jnp.int32, sq.shape, 0)
+    part_q, part_k = (across(jnp.sum(a[...] * a[...], axis=1, keepdims=True), HD)[:8] for a in (q_raw, k_raw))
+    part = jnp.where(row == 0, part_q, jnp.where(row == 1, part_k, 0.0))
+    sq[...] = part
+    sq_all[t] = part
     x = Direct("tensor", nt, t, sq, sq_all, ss, rs)
-    g = Gather(n, d, wo, lambda o: wo_all.at[o], gs, gr)
-    own = pltpu.make_async_copy(wo, wo_all.at[d], loc)
     x.start()
-    g.start()
-    own.start()
-    sq_all[t] = sq[...]
+    gv = Gather(n, d, v, lambda o: v_all.at[o], vs, vr)
+    gv.start()
+    own = [pltpu.make_async_copy(v, v_all.at[d], loc.at[0]), pltpu.make_async_copy(wo, wo_all.at[d], loc.at[1])]
+    for c in own:
+        c.start()
     x.wait()
+    total = sq_all[0]
+    for i in range(1, nt):
+        total = total + sq_all[i]
+    sums[...] = total
+    inv = lax.rsqrt(total / D + EPSILON)
+    for i, (raw, gain, out) in enumerate(((k_raw, k_gain, k), (q_raw, q_gain, q))):
+        scale = jnp.transpose(jnp.broadcast_to(inv[i ^ 1:(i ^ 1) + 1], (HD, inv.shape[1])))
+        for h in range(raw.shape[1] // HD):
+            at = slice(h * HD, (h + 1) * HD)
+            y = raw[:, at] * scale * gain[:, at]
+            out[:, at] = (y * cosine[...] + pltpu.roll(y, HD // 2, 1) * sine[...]).astype(bf16)
+        if i == 0:
+            gk = Gather(n, d, k, lambda o: k_all.at[o], ks, kr)
+            gk.start()
+            gw = Gather(n, d, wo, lambda o: wo_all.at[o], ws, wr)
+            gw.start()
+            own_k = pltpu.make_async_copy(k, k_all.at[d], loc.at[2])
+            own_k.start()
     for j in range(len(bit_list(n))):
-        g.stage(j)
-    g.finish()
-    x.finish()
-    own.wait()
-
-
-def stats(n, nt, sq, wo, cid):
+        for g in (gv, gk, gw):
+            g.stage(j)
+    for e in (x, gv, gk, gw):
+        e.finish()
+    for c in own:
+        c.wait()
+    own_k.wait()
+
+
+def mix(n, nt, q_raw, k_raw, v, cosine, sine, q_gain, k_gain, wo, cid):
+    toks, cols = v.shape
+    sds, vm = jax.ShapeDtypeStruct, pltpu.VMEM
+    wide = sds((n, toks, cols), bf16)
     return kernel_call(
-        functools.partial(stats_kernel, n, nt), "stats", cid, [VM, HB],
-        [jax.ShapeDtypeStruct((nt,) + sq.shape, sq.dtype), jax.ShapeDtypeStruct((n,) + wo.shape, wo.dtype)], [VM, HB],
-        [DMA((nt,)), DMA((nt,)), DMA((2, n)), DMA((2, n)), DMA], (sq, wo))
+        functools.partial(mix_kernel, n, nt), "mix", cid, [VM] * 7 + [HB],
+        [sds((toks, cols), bf16)] * 2 + [wide, wide, sds((n,) + wo.shape, bf16), sds((8, toks), f32)], [VM] * 2 + [HB] * 3 + [VM],
+        [vm((8, toks), f32), vm((nt, 8, toks), f32), DMA((nt,)), DMA((nt,))] + [DMA((2, n))] * 6 + [DMA((3,))],
+        (q_raw, k_raw, v, cosine, sine, q_gain, k_gain, wo))
 
 
 def enter_kernel(n, nt, part, hidden, gain, dy, coef, n2_all, h1, dy_all, coef_all,
@@ -362,10 +397,11 @@
 
 def leave_kernel(n, nt, both, *refs):
     if both:
-        (dn2, moe, h1, cot, gain, dh1, dh1r_all, gain_part, moe_part,
-         got, got2, part, zgot, low, ss, rs, ss2, rs2, zs, zr, xs, xr) = refs
+        (dn2, h1, cot, gain, q, o, moe, dh1, dh1r_all, gain_part, q_all, o_all, moe_part,
+         got, got2, part, zgot, low, ss, rs, ss2, rs2, zs, zr, xs, xr, qs, qr, os, orr, loc) = refs
     else:
-        dn2, h1, cot, gain, dh1, dh1r_all, gain_part, got, part, zgot, low, ss, rs, zs, zr, xs, xr = refs
+        (dn2, h1, cot, gain, q, o, dh1, dh1r_all, gain_part, q_all, o_all,
+         got, part, zgot, low, ss, rs, zs, zr, xs, xr, qs, qr, os, orr, loc) = refs
     d, t = lax.axis_index("dp"), lax.axis_index("tensor")
     greet(n, nt, d, t)
     steps = len(bit_list(n))
@@ -382,6 +418,12 @@
             moe_part[rows, :] = total.astype(bf16)
 
     a.send(0)
+    gathers = [Gather(n, d, q, lambda i: q_all.at[i], qs, qr), Gather(n, d, o, lambda i: o_all.at[i], os, orr)]
+    own = [pltpu.make_async_copy(q, q_all.at[d], loc.at[0]), pltpu.make_async_copy(o, o_all.at[d], loc.at[1])]
+    for g in gathers:
+        g.start()
+    for c in own:
+        c.start()
     a.recv(0, put)
     for j in range(1, steps):
         a.send(j)
@@ -404,6 +446,9 @@
     gain_part[...] = jnp.broadcast_to(jnp.sum(dz * value * r, axis=0, keepdims=True), gain_part.shape)
     x = Direct("tensor", nt, t, low, dh1r_all, xs, xr)
     x.start()
+    for j in range(steps):
+        for g in gathers:
+            g.stage(j)
     if both:
         for j in range(1, steps):
             b.recv(j, put2)
@@ -411,24 +456,25 @@
                 b.send(j + 1)
         b.finish()
     x.wait()
-    a.finish()
-    z.finish()
-    x.finish()
-
-
-def leave(n, nt, dn2, moe, h1, cot, gain, cid):
+    for e in (a, z, x, *gathers):
+        e.finish()
+    for c in own:
+        c.wait()
+
+
+def leave(n, nt, dn2, moe, h1, cot, gain, q, o, cid):
     _, rows, cols = dn2.shape
     share = rows // nt
     sds, vm = jax.ShapeDtypeStruct, pltpu.VMEM
     both = moe is not None
-    outs = [sds((share, cols), f32), sds((nt, share, cols), bf16), sds((8, cols), f32)]
+    outs = [sds((share, cols), f32), sds((nt, share, cols), bf16), sds((8, cols), f32)] + [sds((n,) + q.shape, bf16)] * 2
     if both:
         outs.append(sds((rows, cols), bf16))
     got = [vm((2, n, rows // 2, cols), bf16)] * (2 if both else 1)
-    sems = [DMA((2, n))] * (4 if both else 2) + [DMA((nt,))] * 4
-    args = (dn2, moe, h1, cot, gain) if both else (dn2, h1, cot, gain)
+    sems = [DMA((2, n))] * (4 if both else 2) + [DMA((nt,))] * 4 + [DMA((2, n))] * 4 + [DMA((2,))]
+    args = (dn2, h1, cot, gain, q, o) + ((moe,) if both else ())
     return kernel_call(
-        functools.partial(leave_kernel, n, nt, both), "leave", cid, [VM] * len(args), outs, [VM] * len(outs),
+        functools.partial(leave_kernel, n, nt, both), "leave", cid, [VM] * 4 + [HB] * 2 + [VM] * both, outs, [VM] * 3 + [HB] * 2 + [VM] * both,
         got + [vm((rows, cols), bf16), vm((nt, share, cols), bf16), vm((share, cols), bf16)] + sems, args)
 
 
@@ -453,17 +499,20 @@
 
 
 def back_kernel(n, nt, count, *refs):
-    moe, h1, srcs = refs[0], refs[1], refs[2:2 + count]
-    out_all, dsts = refs[2 + count], refs[3 + count:3 + 2 * count]
-    zgot, low, zs, zr, xs, xr, gs, gr, loc = refs[3 + 2 * count:]
+    moe, h1, slices, srcs = *refs[:3], refs[3:3 + count]
+    out_all, slices_all, dsts = *refs[3 + count:5 + count], refs[5 + count:5 + 2 * count]
+    zgot, low, zs, zr, xs, xr, gs, gr, bs, br, loc = refs[5 + 2 * count:]
     d, t = lax.axis_index("dp"), lax.axis_index("tensor")
-    greet(n, nt, d, t)
+    greet(n, nt, d, t, True)
     z = ZSum(nt, t, moe, zgot, zs, zr)
     gathers = [Gather(n, d, srcs[i], (lambda o, i=i: dsts[i].at[o]), gs.at[i], gr.at[i]) for i in range(count)]
     own = [pltpu.make_async_copy(srcs[i], dsts[i].at[d], loc.at[i]) for i in range(count)]
+    own.append(pltpu.make_async_copy(slices.at[d], slices_all.at[d], loc.at[count]))
     for g in gathers:
         g.start()
     z.start()
+    b = Direct("dp", n, d, slices, slices_all, bs, br, True)
+    b.start()
     for c in own:
         c.start()
     for g in gathers:
@@ -477,41 +526,39 @@
         for g in gathers:
             g.stage(j)
     x.wait()
+    b.wait()
     for g in gathers:
         g.finish()
     for c in own:
         c.wait()
-    z.finish()
-    x.finish()
-
-
-def back(n, nt, moe, h1, arrs, cid):
+    for e in (z, x, b):
+        e.finish()
+
+
+def back(n, nt, moe, h1, slices, arrs, cid):
     rows, cols = moe.shape
     share = rows // nt
     sds = jax.ShapeDtypeStruct
     k = len(arrs)
     return kernel_call(
-        functools.partial(back_kernel, n, nt, k), "back", cid, [VM, VM] + [HB] * k,
-        [sds((nt, share, cols), bf16)] + [sds((n,) + a.shape, a.dtype) for a in arrs], [VM] + [HB] * k,
-        [pltpu.VMEM((nt, share, cols), bf16), pltpu.VMEM((share, cols), bf16)] + [DMA((nt,))] * 4 + [DMA((k, 2, n))] * 2 + [DMA((k,))],
-        (moe, h1, *arrs))
+        functools.partial(back_kernel, n, nt, k), "back", cid, [VM, VM] + [HB] * (k + 1),
+        [sds((nt, share, cols), bf16), sds(slices.shape, bf16)] + [sds((n,) + a.shape, a.dtype) for a in arrs], [VM] + [HB] * (k + 1),
+        [pltpu.VMEM((nt, share, cols), bf16), pltpu.VMEM((share, cols), bf16)] + [DMA((nt,))] * 4 + [DMA((k, 2, n))] * 2 + [DMA((n,))] * 2 + [DMA((k + 1,))],
+        (moe, h1, slices, *arrs))
 
 
 def last_kernel(n, nt, count, *refs):
-    dnormed, hidden, gain, dh1, gains, slices, srcs = *refs[:6], refs[6:6 + count]
-    grad_all, gains_out, slices_all, dsts = *refs[6 + count:9 + count], refs[9 + count:9 + 2 * count]
-    (zgot, low, gpart, ggot, gsum, gall, zs, zr, xs, xr, gs, gr, bs, br, ps, pr, qs, qr, loc) = refs[9 + 2 * count:]
+    dnormed, hidden, gain, dh1, gains, srcs = *refs[:5], refs[5:5 + count]
+    grad_all, gains_out, dsts = *refs[5 + count:7 + count], refs[7 + count:7 + 2 * count]
+    (zgot, low, gpart, ggot, gsum, gall, zs, zr, xs, xr, gs, gr, ps, pr, qs, qr, loc) = refs[7 + 2 * count:]
     d, t = lax.axis_index("dp"), lax.axis_index("tensor")
     greet(n, nt, d, t, True)
     z = ZSum(nt, t, dnormed, zgot, zs, zr)
     z.start()
     gathers = [Gather(n, d, srcs[i], (lambda o, i=i: dsts[i].at[o]), gs.at[i], gr.at[i]) for i in range(count)]
     own = [pltpu.make_async_copy(srcs[i], dsts[i].at[d], loc.at[i]) for i in range(count)]
-    own.append(pltpu.make_async_copy(slices.at[d], slices_all.at[d], loc.at[count]))
     for g in gathers:
         g.start()
-    b = Direct("dp", n, d, slices, slices_all, bs, br, True)
-    b.start()
     for c in own:
         c.start()
     for g in gathers:
@@ -545,7 +592,6 @@
     gall[t] = total
     q = Direct("tensor", nt, t, gsum, gall, qs, qr)
     q.start()
-    b.wait()
     x.wait()
     q.wait()
     total = gall[0]
@@ -556,30 +602,31 @@
         g.finish()
     for c in own:
         c.wait()
-    for e in (z, x, b, p, q):
+    for e in (z, x, p, q):
         e.finish()
 
 
-def last(n, nt, dnormed, hidden, gain, dh1, gains, slices, arrs, cid):
+def last(n, nt, dnormed, hidden, gain, dh1, gains, arrs, cid):
     rows, cols = dnormed.shape
     share = rows // nt
     width = cols // n
     sds, vm = jax.ShapeDtypeStruct, pltpu.VMEM
     k = len(arrs)
     return kernel_call(
-        functools.partial(last_kernel, n, nt, k), "last", cid, [VM] * 5 + [HB] * (k + 1),
-        [sds((nt, share, cols), bf16), sds((8, width), f32), sds(slices.shape, bf16)] + [sds((n,) + a.shape, a.dtype) for a in arrs],
-        [VM, VM, HB] + [HB] * k,
+        functools.partial(last_kernel, n, nt, k), "last", cid, [VM] * 5 + [HB] * k,
+        [sds((nt, share, cols), bf16), sds((8, width), f32)] + [sds((n,) + a.shape, a.dtype) for a in arrs],
+        [VM, VM] + [HB] * k,
         [vm((nt, share, cols), bf16), vm((share, cols), bf16), vm((n, 8, width), f32), vm((n, 8, width), f32), vm((8, width), f32),
-         vm((nt, 8, width), f32)] + [DMA((nt,))] * 4 + [DMA((k, 2, n))] * 2 + [DMA((n,))] * 4 + [DMA((nt,))] * 2 + [DMA((k + 1,))],
-        (dnormed, hidden, gain, dh1, gains, slices, *arrs))
+         vm((nt, 8, width), f32)] + [DMA((nt,))] * 4 + [DMA((k, 2, n))] * 2 + [DMA((n,))] * 2 + [DMA((nt,))] * 2 + [DMA((k,))],
+        (dnormed, hidden, gain, dh1, gains, *arrs))
 
 
 def weight_grad_kernel(order, a_ref, b_ref, out_ref):
-    res = contract(a_ref[...], b_ref[...], 0, 0)
-    rows = res.shape[0]
-    for c, j in enumerate(order):
-        out_ref[pl.ds(j, rows, stride=len(order)), :] = res[:, c * 128:(c + 1) * 128]
+    per = b_ref.shape[2] // 128
+    for i in range(b_ref.shape[0]):
+        res = contract(a_ref[...], b_ref[i], 0, 0)
+        for f in range(per):
+            out_ref[pl.ds(order[i * per + f], res.shape[0], stride=len(order)), :] = res[:, f * 128:(f + 1) * 128]
 
 
 def weight_grad(a, b, order):
@@ -588,7 +635,7 @@
     return pl.pallas_call(
         functools.partial(weight_grad_kernel, order),
         grid=(rows // block,),
-        in_specs=[pl.BlockSpec((toks, block), lambda i: (0, i)), pl.BlockSpec((toks, b.shape[1]), lambda i: (0, 0))],
+        in_specs=[pl.BlockSpec((toks, block), lambda i: (0, i)), pl.BlockSpec(b.shape, lambda i: (0, 0, 0))],
         out_specs=pl.BlockSpec((block * len(order), 128), lambda i: (i, 0)),
         out_shape=jax.ShapeDtypeStruct((rows * len(order), 128), f32),
         name="weight_grad",
@@ -718,18 +765,15 @@
     inv = lax.rsqrt(jnp.mean(hidden * hidden, axis=-1, keepdims=True) + EPSILON)
     normed = (hidden * inv * attn_gain).astype(bf16)
     q_raw, k_raw, v_raw = (contract(normed, w, 1, 0) for w in (wq, wk, wv))
-    sq = small([jnp.sum(q_raw * q_raw, axis=1), jnp.sum(k_raw * k_raw, axis=1)])
-    sq, wo = stats(n, nt, sq, output_weight, 2)
+    v = v_raw.astype(bf16)
+    q, k, k_all, v_all, wo, sq = mix(
+        n, nt, q_raw, k_raw, v, cosine[:, 0], sine[:, 0], query_gain[None, :], key_gain[None, :], output_weight, 2)
     wo = wo.reshape(D, cols)
-    sq = jnp.sum(sq, axis=0)
     q_inv = lax.rsqrt(sq[0] / D + EPSILON)[:, None]
     k_inv = lax.rsqrt(sq[1] / D + EPSILON)[:, None]
-    q = turn((q_raw * q_inv * query_gain).reshape(toks, heads, HD), cosine, sine).astype(bf16)
-    k = turn((k_raw * k_inv * key_gain).reshape(toks, heads, HD), cosine, sine).astype(bf16)
-    v = v_raw.astype(bf16)
-    k_all, v_all = gather_dp(n, (k.reshape(toks, cols), v), 3)
+    q_flat = q
+    q, k, v = (a.reshape(toks, heads, HD) for a in (q, k, v))
     k_all, v_all = (a.reshape(n * toks, heads, HD) for a in (k_all, v_all))
-    v = v.reshape(toks, heads, HD)
 
     scores = scale * jnp.einsum("qhd,khd->hqk", q, k_all, preferred_element_type=f32)
     top = jnp.max(jnp.where(allowed, scores, NEG_FILL), axis=2)
@@ -743,26 +787,28 @@
         n, nt, contract(o, wo, 1, 1).astype(bf16), hidden_in, moe_gain[None, :], cotangent, coef, 4)
     n2_all, dy_all = n2_all.reshape(n * toks, D), dy_all.reshape(n * toks, D)
     coef_all = lax.dynamic_slice_in_dim(coef_all, d * exp_local, exp_local, 1)
-    coef_all = coef_all.transpose(0, 2, 1).reshape(n * toks, exp_local)
-
-    gu = jnp.einsum("td,dezf->tezf", n2_all, expert_gate_up, preferred_element_type=f32)
-    g, u = gu[:, :, 0], gu[:, :, 1]
+    coef_all = coef_all.transpose(1, 0, 2).reshape(exp_local, n * toks, 1)
+
+    gu = jnp.einsum("td,dezf->eztf", n2_all, expert_gate_up, preferred_element_type=f32)
+    g, u = gu[:, 0], gu[:, 1]
     sig = jax.nn.sigmoid(g)
-    act = (coef_all[:, :, None] * (g * sig * u)).astype(bf16)
-    dact = coef_all[:, :, None] * jnp.einsum("td,def->tef", dy_all, expert_down, preferred_element_type=f32)
-    dgu = jnp.stack([dact * u * sig * (1.0 + g * (1.0 - sig)), dact * (g * sig)], axis=2).astype(bf16)
-    dn2 = jnp.einsum("tezf,dezf->td", dgu, expert_gate_up, preferred_element_type=f32).astype(bf16)
-    moe = jnp.einsum("tef,def->td", act, expert_down, preferred_element_type=f32).astype(bf16)
+    act = (coef_all * (g * sig * u)).astype(bf16)
+    dact = coef_all * jnp.einsum("td,def->etf", dy_all, expert_down, preferred_element_type=f32)
+    dgu = jnp.stack([dact * u * sig * (1.0 + g * (1.0 - sig)), dact * (g * sig)], axis=1).astype(bf16)
+    act, dgu = lax.optimization_barrier((act, dgu))
+    dn2 = jnp.einsum("eztf,dezf->td", dgu, expert_gate_up, preferred_element_type=f32).astype(bf16)
+    moe = jnp.einsum("etf,def->td", act, expert_down, preferred_element_type=f32).astype(bf16)
     half = expert_down.shape[2] // 128
-    down_grad = weight_grad(dy_all, act.reshape(n * toks, -1), [f * exp_local + e for e in range(exp_local) for f in range(half)])
+    down_grad = weight_grad(dy_all, act, [f * exp_local + e for e in range(exp_local) for f in range(half)])
     down_grad = down_grad.reshape(D, half, exp_local, 128).transpose(0, 2, 1, 3).reshape(expert_down.shape)
-    gate_up_grad = weight_grad(n2_all, dgu.reshape(n * toks, -1),
+    gate_up_grad = weight_grad(n2_all, dgu.reshape(2 * exp_local, n * toks, -1),
                                [(e * half + f) * 2 + z for e in range(exp_local) for z in (0, 1) for f in range(half)])
     gate_up_grad = gate_up_grad.reshape(D, exp_local, half, 2, 128).transpose(0, 1, 3, 2, 4).reshape(expert_gate_up.shape)
 
     dn2, moe = dn2.reshape(n, toks, D), moe.reshape(n, toks, D)
     together = 16 * n * toks * D <= 48 * 2**20
-    dh1, dh1r, moe_gain_part, *rest = leave(n, nt, dn2, moe if together else None, h1, cotangent, moe_gain[None, :], 6)
+    dh1, dh1r, moe_gain_part, q_all, o_all, *rest = leave(
+        n, nt, dn2, moe if together else None, h1, cotangent, moe_gain[None, :], q_flat, o, 6)
     moe = rest[0] if together else fold(n, nt, moe, 7)
     dh1r = dh1r.reshape(toks, D)
 
@@ -771,7 +817,8 @@
     terms = small(list(lse) + list(delta))
     if terms.shape[0] % 16:
         terms = jnp.pad(terms, ((0, 8), (0, 0)))
-    output, q_all, do_all, o_all, stats_all = back(n, nt, moe, h1, (q.reshape(toks, cols), do, o, terms), 9)
+    slices = jnp.concatenate([normed, dh1r], axis=0).reshape(2 * toks, n, D // n).transpose(1, 0, 2)
+    output, slices, do_all, stats_all = back(n, nt, moe, h1, slices, (do, terms), 9)
     output = output.reshape(toks, D)
 
     do = do.reshape(toks, heads, HD)
@@ -805,9 +852,8 @@
         return lax.dynamic_update_slice_in_dim(jnp.zeros((D,), f32), part, t * cols, 0)
 
     gains = small([jnp.zeros((D,), f32), wide(q_gain_part), wide(k_gain_part), moe_gain_part[0]])
-    slices = jnp.concatenate([normed, dh1r], axis=0).reshape(2 * toks, n, D // n).transpose(1, 0, 2)
-    input_grad, gains, slices, dq_all, dk_all, dv_all = last(
-        n, nt, dnormed.astype(bf16), hidden_in, attn_gain[None, :], dh1, gains, slices, (dq_raw, dk_raw, dv), 12)
+    input_grad, gains, dq_all, dk_all, dv_all = last(
+        n, nt, dnormed.astype(bf16), hidden_in, attn_gain[None, :], dh1, gains, (dq_raw, dk_raw, dv), 12)
     normed_all = slices[:, :toks].reshape(n * toks, D // n)
     dh1r_all = slices[:, toks:].reshape(n * toks, D // n)
     output_grad = contract(dh1r_all, o_all.reshape(n * toks, cols), 0, 0)

time: 414 us -> 389 us (0.940)
  local copies, waits for them, and re-layouts: 57.6 us -> 37.9 us
  other arithmetic: 30 us -> 21.9 us
  matrix products: 58.7 us -> 64.3 us
    pallas_call x5, Pallas kernels: 184 us -> 200 us  [kernel_call(): pl.pallas_call(kernel, out_shape=outs, in_specs=in_specs, out_specs=out_s...]
    pallas_call x3 -> x2, Pallas kernels: 55.8 us -> 41.7 us  [call(): pl.pallas_call(kernel, out_shape=outs, in_specs=[pl.BlockSpec(memory_spac...]
    convert_element_type x2 -> x0, local copies, waits for them, and re-layouts: 8.49 us -> none  [shards(): jnp.stack([dact * u * sig * (1.0 + g * (1.0 - sig)), dact * (g * sig)], a...]
    dot_general x4, matrix products: 22 us -> 28.7 us  [the longest x1 9.97 us: shards(): jnp.einsum('td,dezf->eztf', n2_all, expert_gate_up, preferred_element_typ...]
    convert_element_type x3 -> x0, other arithmetic: 5.95 us -> none  [the longest x1 4.04 us: shards(): act = (coef_all[:, :, None] * (g * sig * u)).astype(bf16)]
    squeeze x2 -> x0, local copies, waits for them, and re-layouts: 5.93 us -> none  [shards(): g, u = (gu[:, :, 0], gu[:, :, 1])]
    slice x1 -> x0, local copies, waits for them, and re-layouts: 4.91 us -> none  [shards(): g, u = (gu[:, :, 0], gu[:, :, 1])]
    unnamed x140 -> x97, local copies, waits for them, and re-layouts: 10 us -> 7.1 us
where the time goes in v3:
time: 389 us; the launch traced here: 387 us
  Pallas kernels  262 us (67%)
  matrix products  64.3 us (17%)
  local copies, waits for them, and re-layouts  37.9 us (10%)
  other arithmetic  21.9 us (6%)
    pallas_call x5, Pallas kernels, kernel_call(): pl.pallas_call(kernel, out_shape=outs, in_specs=in_specs, out_specs=out_s...  200 us
    pallas_call x2, Pallas kernels, call(): pl.pallas_call(kernel, out_shape=outs, in_specs=[pl.BlockSpec(memory_spac...  41.7 us
    pallas_call x2, Pallas kernels, weight_grad(): pl.pallas_call(functools.partial(weight_grad_kernel, order), grid=(rows /...  19.9 us
    dot_general x13, matrix products, contract(): lax.dot_general(left, right, (((l,), (r,)), ((), ())), preferred_element_...  19.4 us
    dot_general x1, matrix products, shards(): jnp.einsum('td,dezf->eztf', n2_all, expert_gate_up, preferred_element_typ...  9.97 us

profile of v3, /device:TPU:0, one launch (start us, length us, event | category | flops | bytes accessed | tf_op | source)
XLA Modules:
  0.0 387.3 jit_solution(8631369330320767975)
XLA Ops:
  2.1 33.4 %gather_dp.1 = (bf16[8,256,512]{2,1,0:T(8,128)(2,1)}, bf16[8,256,512]{2,1,0:T(8,128)(2,1)}, bf16[8,256,512]{2,1,0:T(8,128)(2,1)}, s32[8,16,128]{2,1,0:T(8,128)}) custom-call(bf16[256,512]{1,0:T(8,128)(2,1)} %refs_0_.1, bf16[256,512]{1,0:T(8,128)(2,1)} %refs_1_.2, bf16[256,512]{1,0:T(8,128)(2,1)} %refs_2_.2, s32[16,128]{1,0:T(8,128)} %broadcast_in_dim.68.refs_3_), custom_call_target="tpu_custom_call" | custom-call | tf_op jit(solution)/shard_map/gather_dp/pallas_call | solution.py:104
  40.8 3.0 fusion.73.q_raw
  47.8 26.8 %mix.1 = (bf16[128,512]{1,0:T(8,128)(2,1)}, bf16[128,512]{1,0:T(8,128)(2,1)}, bf16[8,128,512]{2,1,0:T(8,128)(2,1)}, bf16[8,128,512]{2,1,0:T(8,128)(2,1)}, bf16[8...) custom-call(f32[128,512]{1,0:T(8,128)} %fusion.73.q_raw, f32[128,512]{1,0:T(8,128)} %fusion.74.k_raw, ...), custom_call_target="tpu_custom_call" | custom-call | tf_op jit(solution)/shard_map/mix/pallas_call | solution.py:285
  74.6 2.3 reshape.372
  76.9 2.4 copy.106
  79.3 3.1 select_reduce_fusion
  82.4 2.2 fusion.11
  84.7 2.1 reshape.370
  86.8 3.5 fusion.66
  92.8 47.7 %enter.1 = (bf16[8,4,32,2048]{3,2,1,0:T(8,128)(2,1)}, f32[32,2048]{1,0:T(8,128)}, bf16[8,128,2048]{2,1,0:T(8,128)(2,1)}, f32[8,16,128]{2,1,0:T(8,128)}) custom-call(bf16[128,2048]{1,0:T(8,128)(2,1)} %convolution_convert_fusion.part, bf16[128,2048]{1,0:T(8,128)(2,1)} %refs_1_.3, f32[1,2048]{1,0:T(1,128)} %bitcast.235, bf16[128,2048]{1,0:T(8,128)(2,1)} %refs_2_.3, ...), custom_call_target="tpu_custom_call" | custom-call | tf_op jit(solution)/shard_map/enter/pallas_call | solution.py:285
  140.5 10.0 %fusion.4 = f32[2,2,1024,256]{3,2,0,1:T(8,128)} fusion(bf16[1024,2048,1,1]{1,0,2,3:T(8,128)(2,1)} %bitcast.213, bf16[2048,2,2,256]{3,2,1,0:T(2,128)(2,1)} %param.25), kind=kOutput, calls=%fused_computation.9 | convolution fusion | flops 4294967296 | bytes 12582912 | tf_op jit(solution)/shard_map/td,dezf->eztf/dot_general | solution.py:792
  151.3 6.9 %fusion.36 = (bf16[2,1,1024,256]{3,2,0,1:T(8,128)(2,1)S(1)}, bf16[2,1,1024,256]{3,2,0,1:T(8,128)(2,1)S(1)}, bf16[2,1024,256]{2,1,0:T(8,128)(2,1)}) fusion(f32[2,2,1024,256]{3,2,0,1:T(8,128)} %fusion.4, f32[2,1024]{1,0:T(2,128)S(1)} %dynamic-slice_bitcast_fusion, bf16[1024,2048,1]{1,0,2:T(8,128)(2,1)} %bitcast.215, bf16[2048,2,256]{2,1,0:T(2,128)(2,1)S(1)} %copy-done), kind=kOutput, calls=%fused_computation.63 | convolution fusion | flops 2156396544 | bytes 13639680 | tf_op jit(solution)/shard_map/td,def->etf/dot_general | solution.py:796
  158.4 2.0 copy-done.41
  160.4 6.2 %bitcast_convert_fusion = bf16[1024,2048]{1,0:T(8,128)(2,1)} fusion(bf16[2048,2,2,256]{3,2,1,0:T(2,128)(2,1)S(1)} %copy-done.41, bf16[2,2,1024,256]{3,2,0,1:T(8,128)(2,1)S(1)} %pad_maximum_fusion), kind=kOutput, calls=%fused_computation | convolution fusion | flops 4297064448 | bytes 10485760 | tf_op jit(solution)/shard_map/eztf,dezf->td/dot_general | solution.py:799
  167.4 5.6 %bitcast_convert_fusion.1 = bf16[1024,2048]{1,0:T(8,128)(2,1)} fusion(bf16[2,1024,256]{2,1,0:T(8,128)(2,1)} %get-tuple-element.56.b_ref, bf16[2048,2,256]{2,1,0:T(2,128)(2,1)S(1)} %copy-done), kind=kOutput, calls=%fused_computation.1 | convolution fusion | flops 2149580800 | bytes 7340032 | tf_op jit(solution)/shard_map/etf,def->td/dot_general | solution.py:800
  173.0 57.8 %leave.1 = (f32[32,2048]{1,0:T(8,128)}, bf16[4,32,2048]{2,1,0:T(8,128)(2,1)}, f32[8,2048]{1,0:T(8,128)}, bf16[8,128,512]{2,1,0:T(8,128)(2,1)}, bf16[8,128,512]{2,1,0:T(8,128)(2,1)}, /*index=5*/bf16[128,2048]{1,0:T(8,128)(2,1)}) custom-call(bf16[8,128,2048]{2,1,0:T(8,128)(2,1)} %bitcast.218, f32[32,2048]{1,0:T(8,128)} %get-tuple-element.55.refs_1_, ...), custom_call_target="tpu_custom_call" | custom-call | tf_op jit(solution)/shard_map/leave/pallas_call | solution.py:285
  233.9 2.3 maximum_bitcast_fusion.refs_2_
  237.5 36.7 %back.1 = (bf16[4,32,2048]{2,1,0:T(8,128)(2,1)}, bf16[8,256,256]{2,1,0:T(8,128)(2,1)}, bf16[8,128,512]{2,1,0:T(8,128)(2,1)}, f32[8,16,128]{2,1,0:T(8,128)}) custom-call(bf16[128,2048]{1,0:T(8,128)(2,1)} %get-tuple-element.57.refs_0_, f32[32,2048]{1,0:T(8,128)} %get-tuple-element.55.refs_1_, bf16[8,256,256]{2,1,0:T(8,128)(2,1)} %maximum_bitcast_fusion.refs_2_, ...), custom_call_target="tpu_custom_call" | custom-call | tf_op jit(solution)/shard_map/back/pallas_call | solution.py:285
  275.7 1.8 exponential_select_fusion
  277.6 2.2 reshape.384
  279.7 1.9 copy.116
  281.6 3.1 broadcast_multiply_fusion
  289.6 4.2 %broadcast_multiply_fusion.1 = (f32[128,4,128]{0,2,1:T(8,128)}, f32[128,4,128]{0,2,1:T(8,128)}) fusion(bf16[1024,4,128]{0,2,1:T(8,128)(2,1)} %copy.106, f32[4,128,1024]{2,1,0:T(8,128)} %get-tuple-element.109, bf16[128,4,128]{0,2,1:T(8,128)(2,1)S(1)} %bitcast.227, f32[4,128]{1,0:T(4,128)} %bitcast.242, f32[4,128]{1,0:T(4,128)} %copy-done.32, ...), kind=kOutput, calls=%fused_computation.92 | convolution fusion | flops 271646720 | bytes 4984832 | tf_op jit(solution)/shard_map/hqk,khd->qhd/dot_general | solution.py:831
  294.8 2.1 fusion.45
  296.9 1.8 copy.134
  304.7 8.2 %direct_tensor.1 = f32[4,8,128]{2,1,0:T(8,128)} custom-call(f32[8,128]{1,0:T(8,128)} %select_maximum_fusion.4.refs_0_), custom_call_target="tpu_custom_call" | custom-call | tf_op jit(solution)/shard_map/direct_tensor/pallas_call | solution.py:104
  314.9 2.5 fusion.75
  324.8 31.2 %last.1 = (bf16[4,32,2048]{2,1,0:T(8,128)(2,1)}, f32[8,256]{1,0:T(8,128)}, bf16[8,128,512]{2,1,0:T(8,128)(2,1)}, bf16[8,128,512]{2,1,0:T(8,128)(2,1)}, bf16[8,128,512]{2,1,0:T(8,128)(2,1)}) custom-call(bf16[128,2048]{1,0:T(8,128)(2,1)} %fusion.3.refs_0_, bf16[128,2048]{1,0:T(8,128)(2,1)} %refs_1_.3, f32[1,2048]{1,0:T(1,128)} %bitcast.234, ...), custom_call_target="tpu_custom_call" | custom-call | tf_op jit(solution)/shard_map/last/pallas_call | solution.py:285
  356.0 2.2 bitcast_convert_fusion.2
  358.2 2.6 convolution_bitcast_fusion.3
  366.0 11.2 %weight_grad.2 = f32[16384,128]{1,0:T(8,128)} custom-call(bf16[1024,2048]{1,0:T(8,128)(2,1)} %bitcast.214, bf16[4,1024,256]{2,1,0:T(8,128)(2,1)} %bitcast.204), custom_call_target="tpu_custom_call" | custom-call | tf_op jit(solution)/shard_map/weight_grad/pallas_call | solution.py:635
  377.2 8.7 %weight_grad.3 = f32[8192,128]{1,0:T(8,128)} custom-call(bf16[1024,2048]{1,0:T(8,128)(2,1)} %bitcast.216, bf16[2,1024,256]{2,1,0:T(8,128)(2,1)} %get-tuple-element.56.b_ref), custom_call_target="tpu_custom_call" | custom-call | tf_op jit(solution)/shard_map/weight_grad/pallas_call | solution.py:635
  (160 shorter events, 48.1 us)
Async XLA Ops:
  0.6 150.6 %copy-start = (bf16[2048,2,256]{2,1,0:T(2,128)(2,1)S(1)}, bf16[2048,2,256]{2,1,0:T(2,128)(2,1)}, u32[]{:S(2)}) copy-start(bf16[2048,2,256]{2,1,0:T(2,128)(2,1)} %param.26) | copy-start | bytes 6291460
  0.7 39.8 %copy-start.26 = (f32[2048]{0:T(1024)S(1)}, f32[2048]{0:T(1024)}, u32[]{:S(2)}) copy-start(f32[2048]{0:T(1024)} %param.17) | copy-start | bytes 24580
  36.3 4.1 %copy-start.22 = (s32[8,1,128]{2,1,0:T(1,128)}, s32[8,1,128]{2,1,0:T(1,128)S(1)}, u32[]{:S(2)}) copy-start(s32[8,1,128]{2,1,0:T(1,128)S(1)} %slice.64) | copy-start | bytes 12292
  37.2 3.2 copy-start.24
  37.9 8.6 %copy-start.38 = (s32[128]{0:T(128)}, s32[128]{0:T(128)S(1)}, u32[]{:S(2)}) copy-start(s32[128]{0:T(128)S(1)} %convert_reduce_fusion.1) | copy-start | bytes 1540
  40.4 3.3 copy-start.4
  74.6 4.7 %copy-start.19 = (bf16[128,512]{1,0:T(8,128)(2,1)S(1)}, bf16[128,512]{1,0:T(8,128)(2,1)}, u32[]{:S(2)}) copy-start(bf16[128,512]{1,0:T(8,128)(2,1)} %get-tuple-element.48.refs_4_) | copy-start | bytes 393220
  86.8 3.5 copy-start.8
  160.4 6.3 %copy-start.6 = (bf16[2,2,1024,256]{3,2,0,1:T(8,128)(2,1)}, bf16[2,2,1024,256]{3,2,0,1:T(8,128)(2,1)S(1)}, u32[]{:S(2)}) copy-start(bf16[2,2,1024,256]{3,2,0,1:T(8,128)(2,1)S(1)} %pad_maximum_fusion) | copy-start | bytes 6291460
  232.0 4.2 %copy-start.9 = (bf16[8,256,512]{2,1,0:T(8,128)(2,1)S(1)}, bf16[8,256,512]{2,1,0:T(8,128)(2,1)}, u32[]{:S(2)}) copy-start(bf16[8,256,512]{2,1,0:T(8,128)(2,1)} %get-tuple-element.50) | copy-start | bytes 6291460
  232.0 4.2 %copy-start.13 = (bf16[4,32,2048]{2,1,0:T(8,128)(2,1)S(1)}, bf16[4,32,2048]{2,1,0:T(8,128)(2,1)}, u32[]{:S(2)}) copy-start(bf16[4,32,2048]{2,1,0:T(8,128)(2,1)} %get-tuple-element.58) | copy-start | bytes 1572868
  233.9 2.9 copy-start.21
  236.7 37.6 %copy-start.18 = (bf16[8,128,512]{2,1,0:T(8,128)(2,1)S(1)}, bf16[8,128,512]{2,1,0:T(8,128)(2,1)}, u32[]{:S(2)}) copy-start(bf16[8,128,512]{2,1,0:T(8,128)(2,1)} %get-tuple-element.61) | copy-start | bytes 3145732
  236.9 37.4 %copy-start.31 = (f32[128,4]{0,1:T(4,128)}, f32[128,4]{0,1:T(4,128)S(1)}, u32[]{:S(2)}) copy-start(f32[128,4]{0,1:T(4,128)S(1)} %multiply_reduce_fusion.4) | copy-start | bytes 6148
  236.9 37.3 %copy-start.32 = (f32[4,128]{1,0:T(4,128)}, f32[4,128]{1,0:T(4,128)S(1)}, u32[]{:S(2)}) copy-start(f32[4,128]{1,0:T(4,128)S(1)} %log_add_fusion) | copy-start | bytes 6148
  275.3 2.3 copy-start.10
  277.6 4.1 %copy-start.16 = (bf16[128,512]{1,0:T(8,128)(2,1)S(1)}, bf16[128,512]{1,0:T(8,128)(2,1)}, u32[]{:S(2)}) copy-start(bf16[128,512]{1,0:T(8,128)(2,1)} %convolution_convert_fusion.2.v) | copy-start | bytes 393220
  293.8 8.0 %copy-start.11 = (f32[128,512]{1,0:T(8,128)S(1)}, f32[128,512]{1,0:T(8,128)}, u32[]{:S(2)}) copy-start(f32[128,512]{1,0:T(8,128)} %fusion.74.k_raw) | copy-start | bytes 786436
  293.8 8.0 %copy-start.28 = (f32[512]{0:T(512)S(1)}, f32[512]{0:T(512)}, u32[]{:S(2)}) copy-start(f32[512]{0:T(512)} %param.23) | copy-start | bytes 6148
  293.8 9.1 %copy-start.27 = (f32[512]{0:T(512)S(1)}, f32[512]{0:T(512)}, u32[]{:S(2)}) copy-start(f32[512]{0:T(512)} %param.22) | copy-start | bytes 6148
  301.8 2.9 copy-start.36
  313.7 3.8 copy-start.12
  314.9 4.2 %copy-start.14 = (bf16[128,512]{1,0:T(8,128)(2,1)}, bf16[128,512]{1,0:T(8,128)(2,1)S(1)}, u32[]{:S(2)}) copy-start(bf16[128,512]{1,0:T(8,128)(2,1)S(1)} %subtract_convert_fusion.1.refs_5_) | copy-start | bytes 393220
  314.9 3.4 copy-start.5
  322.3 35.9 %copy-start.43 = (bf16[8,256,256]{2,1,0:T(8,128)(2,1)S(1)}, bf16[8,256,256]{2,1,0:T(8,128)(2,1)}, u32[]{:S(2)}) copy-start(bf16[8,256,256]{2,1,0:T(8,128)(2,1)} %get-tuple-element.68) | copy-start | bytes 3145732
  356.0 4.8 %copy-start.45 = (bf16[8,128,512]{2,1,0:T(8,128)(2,1)S(1)}, bf16[8,128,512]{2,1,0:T(8,128)(2,1)}, u32[]{:S(2)}) copy-start(bf16[8,128,512]{2,1,0:T(8,128)(2,1)} %get-tuple-element.70) | copy-start | bytes 3145732
  358.2 3.8 copy-start.44
  360.8 2.5 copy-start.42
  362.1 2.5 copy-start.7
  377.2 8.7 %copy-start.40 = (f32[8,256]{1,0:T(8,128)S(1)}, f32[8,256]{1,0:T(8,128)}, u32[]{:S(2)}) copy-start(f32[8,256]{1,0:T(8,128)} %get-tuple-element.73) | copy-start | bytes 24580
  377.2 9.3 %copy-start.20 = (bf16[4,32,2048]{2,1,0:T(8,128)(2,1)S(1)}, bf16[4,32,2048]{2,1,0:T(8,128)(2,1)}, u32[]{:S(2)}) copy-start(bf16[4,32,2048]{2,1,0:T(8,128)(2,1)} %get-tuple-element.59) | copy-start | bytes 1572868
  377.2 10.1 %copy-start.1 = (bf16[2048,2,256]{2,1,0:T(2,128)(2,1)S(1)}, bf16[2048,2,256]{2,1,0:T(2,128)(2,1)}, u32[]{:S(2)}) copy-start(bf16[2048,2,256]{2,1,0:T(2,128)(2,1)} %param.26) | copy-start | bytes 6291460
  (15 other events, 20.2 us)

commit v4 on v3

--- a/solution.py
+++ b/solution.py
@@ -498,127 +498,206 @@
                        [pltpu.VMEM((2, n, rows // 2, cols), bf16), DMA((2, n)), DMA((2, n))], (p,))
 
 
-def back_kernel(n, nt, count, *refs):
-    moe, h1, slices, srcs = *refs[:3], refs[3:3 + count]
-    out_all, slices_all, dsts = *refs[3 + count:5 + count], refs[5 + count:5 + 2 * count]
-    zgot, low, zs, zr, xs, xr, gs, gr, bs, br, loc = refs[5 + 2 * count:]
+def columns(row, lanes):
+    return jnp.transpose(jnp.broadcast_to(row, (lanes, row.shape[1])))
+
+
+def flat(x):
+    return x.reshape(-1, x.shape[-1])
+
+
+def back_kernel(n, nt, moe, h1, dh1r, dh1, hidden, gain, moe_gain_part, q, k, v, q_raw, k_raw, sums, q_gain, k_gain,
+                cosine, sine, attended, lse, spot, spots, wq, wk, wv, wo, k_all, v_all, q_all, o_all, slices,
+                out_all, grad_all, gains_out, q_grad, k_grad, v_grad, o_grad,
+                wbuf, rbuf, do, do_all, terms, terms_all, rows, dq, dk, dlow, dall, sl_all, zgot, low, acc, part,
+                cross, cross_all, gains, gpart, ggot, gsum, gall,
+                loc, gs, gr, zs, zr, ns, nr, bs, br):
     d, t = lax.axis_index("dp"), lax.axis_index("tensor")
+    heads = q.shape[1] // HD
+    scale = HD ** (-0.5)
+    steps = len(bit_list(n))
+    cols = q.shape[1]
     greet(n, nt, d, t, True)
-    z = ZSum(nt, t, moe, zgot, zs, zr)
-    gathers = [Gather(n, d, srcs[i], (lambda o, i=i: dsts[i].at[o]), gs.at[i], gr.at[i]) for i in range(count)]
-    own = [pltpu.make_async_copy(srcs[i], dsts[i].at[d], loc.at[i]) for i in range(count)]
-    own.append(pltpu.make_async_copy(slices.at[d], slices_all.at[d], loc.at[count]))
+    loads = {}
+    for i, (name, src, dst) in enumerate((("wo", wo, wbuf.at[3]), ("k", k_all, rbuf.at[0]), ("v", v_all, rbuf.at[1]),
+                                          ("q", q_all, rbuf.at[2]), ("wv", wv, wbuf.at[2]), ("wq", wq, wbuf.at[0]),
+                                          ("wk", wk, wbuf.at[1]), ("sl", slices.at[d], sl_all.at[d]), ("o", o_all, rbuf.at[0]))):
+        loads[name] = pltpu.make_async_copy(src, dst, loc.at[i])
+        if name != "o":
+            loads[name].start()
+    z1 = ZSum(nt, t, moe, zgot.at[0], zs.at[0], zr.at[0])
+    z1.start()
+
+    loads["wo"].wait()
+    do[...] = contract(dh1r[...], wbuf[3], 1, 0).astype(bf16)
+    do_all[d] = do[...]
+    terms[0:8] = lse[...]
+    terms[8:16] = jnp.zeros((8, terms.shape[1]), f32)
+    deltas = []
+    for h in range(heads):
+        at = slice(h * HD, (h + 1) * HD)
+        delta = jnp.sum(do[:, at].astype(f32) * attended[:, at], axis=1, keepdims=True)
+        deltas.append(delta)
+        terms[8 + h:9 + h] = across(delta, HD)[:1]
+    terms_all[d] = terms[...]
+    gathers = [Gather(n, d, do, lambda o: do_all.at[o], gs.at[0], gr.at[0]),
+               Gather(n, d, terms, lambda o: terms_all.at[o], gs.at[1], gr.at[1])]
     for g in gathers:
         g.start()
-    z.start()
-    b = Direct("dp", n, d, slices, slices_all, bs, br, True)
-    b.start()
-    for c in own:
-        c.start()
-    for g in gathers:
-        g.stage(0)
-    value = (h1[...] + z.total()).astype(bf16)
-    low[...] = value
-    out_all[t] = value
-    x = Direct("tensor", nt, t, low, out_all, xs, xr)
-    x.start()
-    for j in range(1, len(bit_list(n))):
+
+    spots_row = [jnp.concatenate([spots[i, j:j + 1] for i in range(n)], axis=1) for j in (0, 1)]
+    same = spot[:, 1:2] == spots_row[1]
+    allowed = same & (spots_row[0] <= spot[:, 0:1])
+    loads["k"].wait()
+    loads["v"].wait()
+    stage = 0
+    for h in range(heads):
+        at = slice(h * HD, (h + 1) * HD)
+        keys, values = flat(rbuf[0, :, :, at]), flat(rbuf[1, :, :, at])
+        score = scale * contract(q[:, at], keys, 1, 1)
+        prob = jnp.where(allowed, jnp.exp(score - columns(lse[h:h + 1], HD)[:, :1]), 0.0)
+        ds = (prob * (contract(do[:, at], values, 1, 1) - deltas[h])).astype(bf16)
+        dq[:, at] = scale * contract(ds, keys, 1, 0)
+        if h and stage < steps:
+            for g in gathers:
+                g.stage(stage)
+            stage += 1
+    for j in range(stage, steps):
         for g in gathers:
             g.stage(j)
-    x.wait()
+    loads["o"].start()
+    b = Direct("dp", n, d, slices, sl_all, bs.at[0], br.at[0], True)
+    b.start()
+    value = (h1[...] + z1.total()).astype(bf16)
+    low[0] = value
+    out_all[t] = value
+    x1 = Direct("tensor", nt, t, low.at[0], out_all, ns.at[0], nr.at[0])
+    x1.start()
+    toks = terms.shape[1]
+    for i in range(n):
+        rows[:, i * toks:(i + 1) * toks] = terms_all[i]
+    allowed = same & (spot[:, 0:1] <= spots_row[0])
+    loads["q"].wait()
+    for h in range(heads):
+        at = slice(h * HD, (h + 1) * HD)
+        queries, grads = flat(rbuf[2, :, :, at]), flat(do_all[:, :, at])
+        score = scale * contract(k[:, at], queries, 1, 1)
+        prob = jnp.where(allowed, jnp.exp(score - rows[h:h + 1]), 0.0)
+        dlow[2, :, at] = contract(prob.astype(bf16), grads, 1, 0).astype(bf16)
+        ds = (prob * (contract(v[:, at], grads, 1, 1) - rows[8 + h:9 + h])).astype(bf16)
+        dk[:, at] = scale * contract(ds, queries, 1, 0)
+    dall[2, d] = dlow[2]
+    gv = Gather(n, d, dlow.at[2], lambda o: dall.at[2, o], gs.at[2], gr.at[2])
+    gv.start()
+
+    gains[...] = jnp.zeros(gains.shape, f32)
+    gains[3:4] = moe_gain_part[0:1]
+    inv = lax.rsqrt(sums[...] / D + EPSILON)
+    invs = [columns(inv[i:i + 1], HD) for i in (0, 1)]
+    cross_rows = []
+    for i, (grad, raw, weight) in enumerate(((dq, q_raw, q_gain), (dk, k_raw, k_gain))):
+        total = jnp.zeros((toks, 1), f32)
+        for h in range(heads):
+            at = slice(h * HD, (h + 1) * HD)
+            y = grad[:, at]
+            y = y * cosine[...] - pltpu.roll(y, HD // 2, 1) * sine[...]
+            gains[1 + i:2 + i, pl.ds(pl.multiple_of(t * cols + h * HD, HD), HD)] = jnp.sum(
+                y * raw[:, at] * invs[i], axis=0, keepdims=True)
+            y = y * weight[:, at]
+            total = total + jnp.sum(y * raw[:, at], axis=1, keepdims=True)
+            grad[:, at] = y
+        cross_rows.append(across(total, HD)[:8])
+    row = lax.broadcasted_iota(jnp.int32, cross.shape, 0)
+    value = jnp.where(row == 0, cross_rows[0], cross_rows[1])
+    cross[...] = value
+    cross_all[t] = value
+    xc = Direct("tensor", nt, t, cross, cross_all, ns.at[1], nr.at[1])
+    xc.start()
+    loads["wv"].wait()
+    acc[...] = contract(dlow[2], wbuf[2], 1, 1)
+    gv.stage(0)
+    xc.wait()
+    total = cross_all[0]
+    for i in range(1, nt):
+        total = total + cross_all[i]
+    gathers2 = []
+    for i, (grad, raw) in enumerate(((dq, q_raw), (dk, k_raw))):
+        factor = invs[i] * invs[i] * invs[i] * columns(total[i:i + 1], HD) / D
+        for h in range(heads):
+            at = slice(h * HD, (h + 1) * HD)
+            dlow[i, :, at] = (invs[i] * grad[:, at] - raw[:, at] * factor).astype(bf16)
+        dall[i, d] = dlow[i]
+        g = Gather(n, d, dlow.at[i], lambda o, i=i: dall.at[i, o], gs.at[3 + i], gr.at[3 + i])
+        g.start()
+        gathers2.append(g)
+    loads["wq"].wait()
+    loads["wk"].wait()
+    part[...] = (acc[...] + contract(dlow[0], wbuf[0], 1, 1) + contract(dlow[1], wbuf[1], 1, 1)).astype(bf16)
+    z2 = ZSum(nt, t, part, zgot.at[1], zs.at[1], zr.at[1])
+    z2.start()
+    gathers2.append(gv)
+    for j in range(steps):
+        for g in gathers2:
+            if j or g is not gv:
+                g.stage(j)
     b.wait()
-    for g in gathers:
-        g.finish()
-    for c in own:
-        c.wait()
-    for e in (z, x, b):
-        e.finish()
-
-
-def back(n, nt, moe, h1, slices, arrs, cid):
-    rows, cols = moe.shape
-    share = rows // nt
-    sds = jax.ShapeDtypeStruct
-    k = len(arrs)
-    return kernel_call(
-        functools.partial(back_kernel, n, nt, k), "back", cid, [VM, VM] + [HB] * (k + 1),
-        [sds((nt, share, cols), bf16), sds(slices.shape, bf16)] + [sds((n,) + a.shape, a.dtype) for a in arrs], [VM] + [HB] * (k + 1),
-        [pltpu.VMEM((nt, share, cols), bf16), pltpu.VMEM((share, cols), bf16)] + [DMA((nt,))] * 4 + [DMA((k, 2, n))] * 2 + [DMA((n,))] * 2 + [DMA((k + 1,))],
-        (moe, h1, slices, *arrs))
-
-
-def last_kernel(n, nt, count, *refs):
-    dnormed, hidden, gain, dh1, gains, srcs = *refs[:5], refs[5:5 + count]
-    grad_all, gains_out, dsts = *refs[5 + count:7 + count], refs[7 + count:7 + 2 * count]
-    (zgot, low, gpart, ggot, gsum, gall, zs, zr, xs, xr, gs, gr, ps, pr, qs, qr, loc) = refs[7 + 2 * count:]
-    d, t = lax.axis_index("dp"), lax.axis_index("tensor")
-    greet(n, nt, d, t, True)
-    z = ZSum(nt, t, dnormed, zgot, zs, zr)
-    z.start()
-    gathers = [Gather(n, d, srcs[i], (lambda o, i=i: dsts[i].at[o]), gs.at[i], gr.at[i]) for i in range(count)]
-    own = [pltpu.make_async_copy(srcs[i], dsts[i].at[d], loc.at[i]) for i in range(count)]
-    for g in gathers:
-        g.start()
-    for c in own:
-        c.start()
-    for g in gathers:
-        g.stage(0)
-    dz = z.total()
-    value = hidden[pl.ds(t * z.share, z.share), :].astype(f32)
+    loads["sl"].wait()
+    loads["o"].wait()
+    normed_all, dh1r_all = flat(sl_all[:, :toks]), flat(sl_all[:, toks:])
+    o_grad[...] = contract(dh1r_all, flat(rbuf[0]), 0, 0)
+    dz = z2.total()
+    value = hidden[pl.ds(t * z2.share, z2.share), :].astype(f32)
     r = inv_rms(value)
     weighted = dz * gain[...]
     grad = r * weighted - value * (r * r * r) * jnp.mean(weighted * value, axis=-1, keepdims=True)
     grad = (dh1[...] + grad).astype(bf16)
-    low[...] = grad
+    low[1] = grad
     grad_all[t] = grad
-    x = Direct("tensor", nt, t, low, grad_all, xs, xr)
-    x.start()
-    row = jnp.sum(dz * value * r, axis=0, keepdims=True)
-    first = lax.broadcasted_iota(jnp.int32, gains.shape, 0) == 0
-    whole = jnp.where(first, row, gains[...])
+    x2 = Direct("tensor", nt, t, low.at[1], grad_all, ns.at[2], nr.at[2])
+    x2.start()
+    gains[0:1] = jnp.sum(dz * value * r, axis=0, keepdims=True)
     width = gpart.shape[2]
     for i in range(n):
-        gpart[i] = whole[:, i * width:(i + 1) * width]
-    p = Direct("dp", n, d, gpart, ggot, ps, pr, True)
+        gpart[i] = gains[:, i * width:(i + 1) * width]
+    p = Direct("dp", n, d, gpart, ggot, bs.at[1], br.at[1], True)
     p.start()
-    for j in range(1, len(bit_list(n))):
-        for g in gathers:
-            g.stage(j)
+    for i, out in enumerate((q_grad, k_grad, v_grad)):
+        out[...] = contract(normed_all, flat(dall[i]), 0, 0)
     p.wait()
     total = gpart[d]
     for m in range(1, n):
         total = total + ggot[flip(d, m)]
     gsum[...] = total
     gall[t] = total
-    q = Direct("tensor", nt, t, gsum, gall, qs, qr)
-    q.start()
-    x.wait()
-    q.wait()
+    xg = Direct("tensor", nt, t, gsum, gall, ns.at[3], nr.at[3])
+    xg.start()
+    x1.wait()
+    xg.wait()
     total = gall[0]
     for i in range(1, nt):
         total = total + gall[i]
     gains_out[...] = total
-    for g in gathers:
-        g.finish()
-    for c in own:
-        c.wait()
-    for e in (z, x, p, q):
+    x2.wait()
+    for e in (z1, z2, x1, xc, x2, xg, b, p, *gathers, *gathers2):
         e.finish()
 
 
-def last(n, nt, dnormed, hidden, gain, dh1, gains, arrs, cid):
-    rows, cols = dnormed.shape
-    share = rows // nt
-    width = cols // n
+def back(n, nt, in_vmem, in_hbm, cid):
+    moe, q, slices = in_vmem[0], in_vmem[7], in_hbm[-1]
+    toks, cols = q.shape
+    dim = moe.shape[1]
+    share, width = toks // nt, dim // n
     sds, vm = jax.ShapeDtypeStruct, pltpu.VMEM
-    k = len(arrs)
     return kernel_call(
-        functools.partial(last_kernel, n, nt, k), "last", cid, [VM] * 5 + [HB] * k,
-        [sds((nt, share, cols), bf16), sds((8, width), f32)] + [sds((n,) + a.shape, a.dtype) for a in arrs],
-        [VM, VM] + [HB] * k,
-        [vm((nt, share, cols), bf16), vm((share, cols), bf16), vm((n, 8, width), f32), vm((n, 8, width), f32), vm((8, width), f32),
-         vm((nt, 8, width), f32)] + [DMA((nt,))] * 4 + [DMA((k, 2, n))] * 2 + [DMA((n,))] * 2 + [DMA((nt,))] * 2 + [DMA((k,))],
-        (dnormed, hidden, gain, dh1, gains, *arrs))
+        functools.partial(back_kernel, n, nt), "back", cid, [VM] * len(in_vmem) + [HB] * len(in_hbm),
+        [sds((nt, share, dim), bf16)] * 2 + [sds((8, width), f32)] + [sds((width, cols), f32)] * 4, [VM] * 7,
+        [vm((4, dim, cols), bf16), vm((3, n, toks, cols), bf16), vm((toks, cols), bf16), vm((n, toks, cols), bf16),
+         vm((16, toks), f32), vm((n, 16, toks), f32), vm((16, n * toks), f32), vm((toks, cols), f32), vm((toks, cols), f32),
+         vm((3, toks, cols), bf16), vm((3, n, toks, cols), bf16), vm(slices.shape, bf16), vm((2, nt, share, dim), bf16),
+         vm((2, share, dim), bf16), vm((toks, dim), f32), vm((toks, dim), bf16), vm((8, toks), f32), vm((nt, 8, toks), f32),
+         vm((8, dim), f32), vm((n, 8, width), f32), vm((n, 8, width), f32), vm((8, width), f32), vm((nt, 8, width), f32),
+         DMA((9,)), DMA((5, 2, n)), DMA((5, 2, n)), DMA((2, nt)), DMA((2, nt)), DMA((4, nt)), DMA((4, nt)), DMA((2, n)), DMA((2, n))],
+        (*in_vmem, *in_hbm))
 
 
 def weight_grad_kernel(order, a_ref, b_ref, out_ref):
@@ -640,37 +719,6 @@
         out_shape=jax.ShapeDtypeStruct((rows * len(order), 128), f32),
         name="weight_grad",
     )(a, b)
-
-
-def direct_kernel(axis, n, split, count, *refs):
-    srcs, dsts, ss, rs, loc = refs[:count], refs[count:2 * count], *refs[2 * count:]
-    me = lax.axis_index(axis)
-    own = [pltpu.make_async_copy(srcs[i].at[me] if split else srcs[i], dsts[i].at[me], loc.at[i]) for i in range(count)]
-    hello(all_peers(axis, n, me))
-    sent = []
-    for m in range(1, n):
-        for i in range(count):
-            peer = flip(me, m)
-            c = rdma(srcs[i].at[peer] if split else srcs[i], dsts[i].at[me], ss.at[i, m], rs.at[i, m], {axis: peer})
-            c.start()
-            sent.append(c)
-    for c in own:
-        c.start()
-    for m in range(1, n):
-        for i in range(count):
-            place = dsts[i].at[flip(me, m)]
-            rdma(place, place, ss.at[i, m], rs.at[i, m], {axis: flip(me, m)}).wait_recv()
-    for c in sent:
-        c.wait_send()
-    for c in own:
-        c.wait()
-
-
-def direct(axis, n, arrs, cid, split=False):
-    arrs = list(arrs)
-    scratch = [pltpu.SemaphoreType.DMA((len(arrs), n))] * 2 + [pltpu.SemaphoreType.DMA((len(arrs),))]
-    outs = [jax.ShapeDtypeStruct(a.shape if split else (n,) + a.shape, a.dtype) for a in arrs]
-    return call(functools.partial(direct_kernel, axis, n, split, len(arrs)), "direct_" + axis, cid, outs, pltpu.VMEM, pltpu.VMEM, scratch, *arrs)
 
 
 D = 2048
@@ -760,7 +808,6 @@
     docs_all, _ = locate(anchor_all, lengths)
     cosine, sine = rope_tables(positions)
     allowed = pair_allowed(anchor, docs, anchor_all, docs_all)
-    allowed_back = pair_allowed(anchor_all, docs_all, anchor, docs)
 
     inv = lax.rsqrt(jnp.mean(hidden * hidden, axis=-1, keepdims=True) + EPSILON)
     normed = (hidden * inv * attn_gain).astype(bf16)
@@ -769,9 +816,7 @@
     q, k, k_all, v_all, wo, sq = mix(
         n, nt, q_raw, k_raw, v, cosine[:, 0], sine[:, 0], query_gain[None, :], key_gain[None, :], output_weight, 2)
     wo = wo.reshape(D, cols)
-    q_inv = lax.rsqrt(sq[0] / D + EPSILON)[:, None]
-    k_inv = lax.rsqrt(sq[1] / D + EPSILON)[:, None]
-    q_flat = q
+    q_flat, k_flat, v_flat, k_flat_all, v_flat_all = q, k, v, k_all, v_all
     q, k, v = (a.reshape(toks, heads, HD) for a in (q, k, v))
     k_all, v_all = (a.reshape(n * toks, heads, HD) for a in (k_all, v_all))
 
@@ -812,53 +857,15 @@
     moe = rest[0] if together else fold(n, nt, moe, 7)
     dh1r = dh1r.reshape(toks, D)
 
-    do = contract(dh1r, wo, 1, 0).astype(bf16)
-    delta = jnp.sum(do.reshape(toks, heads, HD).astype(f32) * attended, axis=2).T
-    terms = small(list(lse) + list(delta))
-    if terms.shape[0] % 16:
-        terms = jnp.pad(terms, ((0, 8), (0, 0)))
     slices = jnp.concatenate([normed, dh1r], axis=0).reshape(2 * toks, n, D // n).transpose(1, 0, 2)
-    output, slices, do_all, stats_all = back(n, nt, moe, h1, slices, (do, terms), 9)
+    spot = jnp.stack([anchor, docs], axis=1)
+    spots = jnp.stack([anchor_all, docs_all], axis=0).reshape(2, n, toks).transpose(1, 0, 2)
+    output, input_grad, gains, query_grad, key_grad, value_grad, output_grad = back(
+        n, nt,
+        (moe, h1, dh1r, dh1, hidden_in, attn_gain[None, :], moe_gain_part, q_flat, k_flat, v_flat, q_raw, k_raw, sq,
+         query_gain[None, :], key_gain[None, :], cosine[:, 0], sine[:, 0], attended.reshape(toks, cols), small(list(lse)), spot, spots),
+        (wq, wk, wv, wo, k_flat_all, v_flat_all, q_all, o_all, slices), 9)
     output = output.reshape(toks, D)
-
-    do = do.reshape(toks, heads, HD)
-    q_all, do_all = (a.reshape(n * toks, heads, HD) for a in (q_all, do_all))
-    lse_all = stats_all[:, :heads].transpose(1, 0, 2).reshape(heads, n * toks)
-    delta_all = stats_all[:, heads:2 * heads].transpose(1, 0, 2).reshape(heads, n * toks)
-    probs = jnp.where(allowed, jnp.exp(scores - lse[:, :, None]), 0.0)
-    dprobs = jnp.einsum("qhd,khd->hqk", do, v_all, preferred_element_type=f32)
-    ds = (probs * (dprobs - delta[:, :, None])).astype(bf16)
-    dq = scale * jnp.einsum("hqk,khd->qhd", ds, k_all, preferred_element_type=f32)
-    scores_b = scale * jnp.einsum("qhd,khd->hqk", q_all, k, preferred_element_type=f32)
-    probs_b = jnp.where(allowed_back, jnp.exp(scores_b - lse_all[:, :, None]), 0.0)
-    dv = jnp.einsum("hqk,qhd->khd", probs_b.astype(bf16), do_all, preferred_element_type=f32)
-    dprobs_b = jnp.einsum("qhd,khd->hqk", do_all, v, preferred_element_type=f32)
-    ds_b = (probs_b * (dprobs_b - delta_all[:, :, None])).astype(bf16)
-    dk = scale * jnp.einsum("hqk,qhd->khd", ds_b, q_all, preferred_element_type=f32)
-    dq_hat = turn(dq, cosine, -sine).reshape(toks, cols)
-    dk_hat = turn(dk, cosine, -sine).reshape(toks, cols)
-    dv = dv.reshape(toks, cols).astype(bf16)
-
-    wdq, wdk = dq_hat * query_gain, dk_hat * key_gain
-    q_gain_part = jnp.sum(dq_hat * q_raw * q_inv, axis=0)
-    k_gain_part = jnp.sum(dk_hat * k_raw * k_inv, axis=0)
-    (cross,) = direct("tensor", nt, [small([jnp.sum(wdq * q_raw, axis=1), jnp.sum(wdk * k_raw, axis=1)])], 11)
-    cross = jnp.sum(cross, axis=0)
-    dq_raw = (q_inv * wdq - q_raw * q_inv**3 * cross[0][:, None] / D).astype(bf16)
-    dk_raw = (k_inv * wdk - k_raw * k_inv**3 * cross[1][:, None] / D).astype(bf16)
-    dnormed = contract(dq_raw, wq, 1, 1) + contract(dk_raw, wk, 1, 1) + contract(dv, wv, 1, 1)
-
-    def wide(part):
-        return lax.dynamic_update_slice_in_dim(jnp.zeros((D,), f32), part, t * cols, 0)
-
-    gains = small([jnp.zeros((D,), f32), wide(q_gain_part), wide(k_gain_part), moe_gain_part[0]])
-    input_grad, gains, dq_all, dk_all, dv_all = last(
-        n, nt, dnormed.astype(bf16), hidden_in, attn_gain[None, :], dh1, gains, (dq_raw, dk_raw, dv), 12)
-    normed_all = slices[:, :toks].reshape(n * toks, D // n)
-    dh1r_all = slices[:, toks:].reshape(n * toks, D // n)
-    output_grad = contract(dh1r_all, o_all.reshape(n * toks, cols), 0, 0)
-    query_grad, key_grad, value_grad = (
-        contract(normed_all, a.reshape(n * toks, cols), 0, 0) for a in (dq_all, dk_all, dv_all))
     input_grad = input_grad.reshape(toks, D).astype(f32)
     return (output, input_grad, query_grad, key_grad, value_grad, output_grad, gate_up_grad, down_grad,
             gains[0], gains[1], gains[2], gains[3])

time: 389 us -> 334 us (0.86)
  matrix products: 64.3 us -> 41.1 us
  local copies, waits for them, and re-layouts: 37.9 us -> 24 us
  other arithmetic: 21.9 us -> 10.7 us
  Pallas kernels: 262 us -> 256 us
    dot_general x13 -> x5, matrix products: 19.4 us -> 7.62 us  [contract(): lax.dot_general(left, right, (((l,), (r,)), ((), ())), preferred_element_...]
    dot_general x4 -> x0, matrix products: 9.59 us -> none  [the longest x1 4.22 us: shards(): jnp.einsum('hqk,khd->qhd', ds, k_all, preferred_element_type=f32)]
    reshape x7 -> x1, local copies, waits for them, and re-layouts: 8.69 us -> 0.13 us  [shards(): o = attended.reshape(toks, cols).astype(bf16)]
    pallas_call x2 -> x1, Pallas kernels: 41.7 us -> 33.4 us  [call(): pl.pallas_call(kernel, out_shape=outs, in_specs=[pl.BlockSpec(memory_spac...]
    unnamed x97 -> x47, local copies, waits for them, and re-layouts: 7.1 us -> 10.3 us
    pallas_call x5 -> x4, Pallas kernels: 200 us -> 203 us  [kernel_call(): pl.pallas_call(kernel, out_shape=outs, in_specs=in_specs, out_specs=out_s...]
where the time goes in v4:
time: 334 us; the launch traced here: 333 us
  Pallas kernels  256 us (77%)
  matrix products  41.1 us (12%)
  local copies, waits for them, and re-layouts  24 us (7%)
  other arithmetic  10.7 us (3%)
    pallas_call x4, Pallas kernels, kernel_call(): pl.pallas_call(kernel, out_shape=outs, in_specs=in_specs, out_specs=out_s...  203 us
    pallas_call x1, Pallas kernels, call(): pl.pallas_call(kernel, out_shape=outs, in_specs=[pl.BlockSpec(memory_spac...  33.4 us
    pallas_call x2, Pallas kernels, weight_grad(): pl.pallas_call(functools.partial(weight_grad_kernel, order), grid=(rows /...  19.8 us
    unnamed x47, local copies, waits for them, and re-layouts  10.3 us
    dot_general x1, matrix products, shards(): jnp.einsum('td,dezf->eztf', n2_all, expert_gate_up, preferred_element_typ...  9.97 us
    dot_general x5, matrix products, contract(): lax.dot_general(left, right, (((l,), (r,)), ((), ())), preferred_element_...  7.62 us
    dot_general x1, matrix products, shards(): jnp.einsum('td,def->etf', dy_all, expert_down, preferred_element_type=f32)  6.91 us

profile of v4, /device:TPU:0, one launch (start us, length us, event | category | flops | bytes accessed | tf_op | source)
XLA Modules:
  0.0 332.8 jit_solution(14279328532930798793)
XLA Ops:
  0.7 1.4 broadcast_in_dim.92.refs_3_
  2.1 33.4 %gather_dp.1 = (bf16[8,256,512]{2,1,0:T(8,128)(2,1)}, bf16[8,256,512]{2,1,0:T(8,128)(2,1)}, bf16[8,256,512]{2,1,0:T(8,128)(2,1)}, s32[8,16,128]{2,1,0:T(8,128)}) custom-call(bf16[256,512]{1,0:T(8,128)(2,1)} %refs_0_.1, bf16[256,512]{1,0:T(8,128)(2,1)} %refs_1_.1, bf16[256,512]{1,0:T(8,128)(2,1)} %refs_2_.2, s32[16,128]{1,0:T(8,128)} %broadcast_in_dim.92.refs_3_), custom_call_target="tpu_custom_call" | custom-call | tf_op jit(solution)/shard_map/gather_dp/pallas_call | solution.py:104
  35.5 0.9 copy.87
  36.4 0.8 reduce-window.8
  38.0 0.8 compare_and_fusion
  38.9 1.3 copy.86
  40.8 2.9 fusion.40.q_raw
  43.8 1.2 fusion.41.k_raw
  45.5 1.1 convolution_convert_fusion.1.v
  47.8 26.8 %mix.1 = (bf16[128,512]{1,0:T(8,128)(2,1)}, bf16[128,512]{1,0:T(8,128)(2,1)}, bf16[8,128,512]{2,1,0:T(8,128)(2,1)}, bf16[8,128,512]{2,1,0:T(8,128)(2,1)}, bf16[8...) custom-call(f32[128,512]{1,0:T(8,128)} %fusion.40.q_raw, f32[128,512]{1,0:T(8,128)} %fusion.41.k_raw, ...), custom_call_target="tpu_custom_call" | custom-call | tf_op jit(solution)/shard_map/mix/pallas_call | solution.py:285
  74.6 2.3 reshape.205
  77.0 1.9 select_reduce_fusion
  78.9 1.3 copy-done.6
  80.8 2.1 reshape.203
  83.0 2.8 fusion.37
  85.8 1.6 convolution_convert_fusion.part
  88.3 47.8 %enter.1 = (bf16[8,4,32,2048]{3,2,1,0:T(8,128)(2,1)}, f32[32,2048]{1,0:T(8,128)}, bf16[8,128,2048]{2,1,0:T(8,128)(2,1)}, f32[8,16,128]{2,1,0:T(8,128)}) custom-call(bf16[128,2048]{1,0:T(8,128)(2,1)} %convolution_convert_fusion.part, bf16[128,2048]{1,0:T(8,128)(2,1)} %hidden.3, f32[1,2048]{1,0:T(1,128)} %bitcast.157, bf16[128,2048]{1,0:T(8,128)(2,1)} %refs_2_.3, ...), custom_call_target="tpu_custom_call" | custom-call | tf_op jit(solution)/shard_map/enter/pallas_call | solution.py:285
  136.0 10.0 %fusion.3 = f32[2,2,1024,256]{3,2,0,1:T(8,128)} fusion(bf16[1024,2048,1,1]{1,0,2,3:T(8,128)(2,1)} %bitcast.142, bf16[2048,2,2,256]{3,2,1,0:T(2,128)(2,1)} %param.25), kind=kOutput, calls=%fused_computation.6 | convolution fusion | flops 4294967296 | bytes 12582912 | tf_op jit(solution)/shard_map/td,dezf->eztf/dot_general | solution.py:837
  146.8 6.9 %fusion.27 = (bf16[2,1,1024,256]{3,2,0,1:T(8,128)(2,1)S(1)}, bf16[2,1,1024,256]{3,2,0,1:T(8,128)(2,1)S(1)}, bf16[2,1024,256]{2,1,0:T(8,128)(2,1)}) fusion(f32[2,2,1024,256]{3,2,0,1:T(8,128)} %fusion.3, f32[2,1024]{1,0:T(2,128)S(1)} %dynamic-slice_bitcast_fusion, bf16[1024,2048,1]{1,0,2:T(8,128)(2,1)} %bitcast.144, bf16[2048,2,256]{2,1,0:T(2,128)(2,1)S(1)} %copy-done), kind=kOutput, calls=%fused_computation.43 | convolution fusion | flops 2156396544 | bytes 13639680 | tf_op jit(solution)/shard_map/td,def->etf/dot_general | solution.py:841
  153.9 2.0 copy-done.18
  155.9 6.2 %bitcast_convert_fusion = bf16[1024,2048]{1,0:T(8,128)(2,1)} fusion(bf16[2048,2,2,256]{3,2,1,0:T(2,128)(2,1)S(1)} %copy-done.18, bf16[2,2,1024,256]{3,2,0,1:T(8,128)(2,1)S(1)} %pad_maximum_fusion), kind=kOutput, calls=%fused_computation | convolution fusion | flops 4297064448 | bytes 10485760 | tf_op jit(solution)/shard_map/eztf,dezf->td/dot_general | solution.py:844
  163.0 5.6 %bitcast_convert_fusion.1 = bf16[1024,2048]{1,0:T(8,128)(2,1)} fusion(bf16[2,1024,256]{2,1,0:T(8,128)(2,1)} %get-tuple-element.54.b_ref, bf16[2048,2,256]{2,1,0:T(2,128)(2,1)S(1)} %copy-done), kind=kOutput, calls=%fused_computation.1 | convolution fusion | flops 2149580800 | bytes 7340032 | tf_op jit(solution)/shard_map/etf,def->td/dot_general | solution.py:845
  168.6 57.8 %leave.1 = (f32[32,2048]{1,0:T(8,128)}, bf16[4,32,2048]{2,1,0:T(8,128)(2,1)}, f32[8,2048]{1,0:T(8,128)}, bf16[8,128,512]{2,1,0:T(8,128)(2,1)}, bf16[8,128,512]{2,1,0:T(8,128)(2,1)}, /*index=5*/bf16[128,2048]{1,0:T(8,128)(2,1)}) custom-call(bf16[8,128,2048]{2,1,0:T(8,128)(2,1)} %bitcast.147, f32[32,2048]{1,0:T(8,128)} %get-tuple-element.53.refs_1_.h1, ...), custom_call_target="tpu_custom_call" | custom-call | tf_op jit(solution)/shard_map/leave/pallas_call | solution.py:285
  228.4 1.1 copy.110
  229.7 1.0 copy.98
  230.7 2.1 maximum_bitcast_fusion.slices
  232.8 70.5 %back.1 = (bf16[4,32,2048]{2,1,0:T(8,128)(2,1)}, bf16[4,32,2048]{2,1,0:T(8,128)(2,1)}, f32[8,256]{1,0:T(8,128)}, f32[256,512]{1,0:T(8,128)}, f32[256,512]{1,0:T(...) custom-call(bf16[128,2048]{1,0:T(8,128)(2,1)} %get-tuple-element.55.moe, f32[32,2048]{1,0:T(8,128)} %get-tuple-element.53.refs_1_.h1, ...), custom_call_target="tpu_custom_call" | custom-call | tf_op jit(solution)/shard_map/back/pallas_call | solution.py:285
  303.3 2.1 bitcast_convert_fusion.2
  305.4 3.0 copy.94
  308.4 11.2 %weight_grad.2 = f32[16384,128]{1,0:T(8,128)} custom-call(bf16[1024,2048]{1,0:T(8,128)(2,1)} %bitcast.143, bf16[4,1024,256]{2,1,0:T(8,128)(2,1)} %bitcast.141), custom_call_target="tpu_custom_call" | custom-call | tf_op jit(solution)/shard_map/weight_grad/pallas_call | solution.py:714
  319.6 8.7 %weight_grad.3 = f32[8192,128]{1,0:T(8,128)} custom-call(bf16[1024,2048]{1,0:T(8,128)(2,1)} %bitcast.145, bf16[2,1024,256]{2,1,0:T(8,128)(2,1)} %get-tuple-element.54.b_ref), custom_call_target="tpu_custom_call" | custom-call | tf_op jit(solution)/shard_map/weight_grad/pallas_call | solution.py:714
  328.8 0.8 copy.144
  (69 shorter events, 12.3 us)
Async XLA Ops:
  0.6 146.1 %copy-start = (bf16[2048,2,256]{2,1,0:T(2,128)(2,1)S(1)}, bf16[2048,2,256]{2,1,0:T(2,128)(2,1)}, u32[]{:S(2)}) copy-start(bf16[2048,2,256]{2,1,0:T(2,128)(2,1)} %param.26) | copy-start | bytes 6291460
  0.7 39.8 %copy-start.13 = (f32[2048]{0:T(1024)S(1)}, f32[2048]{0:T(1024)}, u32[]{:S(2)}) copy-start(f32[2048]{0:T(1024)} %param.17) | copy-start | bytes 24580
  40.5 3.3 copy-start.1
  43.8 1.7 copy-start.2
  45.0 1.6 copy-start.19
  45.0 1.7 copy-start.15
  74.6 2.3 copy-start.7
  78.9 1.3 copy-start.6
  83.0 2.9 copy-start.3
  85.8 1.6 copy-start.14
  85.8 1.7 copy-start.16
  153.7 2.2 copy-start.18
  155.9 6.2 %copy-start.4 = (bf16[2,2,1024,256]{3,2,0,1:T(8,128)(2,1)}, bf16[2,2,1024,256]{3,2,0,1:T(8,128)(2,1)S(1)}, u32[]{:S(2)}) copy-start(bf16[2,2,1024,256]{3,2,0,1:T(8,128)(2,1)S(1)} %pad_maximum_fusion) | copy-start | bytes 6291460
  162.3 6.4 %copy-start.5 = (f32[128,512]{1,0:T(8,128)}, f32[128,512]{1,0:T(8,128)S(1)}, u32[]{:S(2)}) copy-start(f32[128,512]{1,0:T(8,128)S(1)} %copy.108.attended) | copy-start | bytes 786436
  319.6 8.7 %copy-start.17 = (f32[8,256]{1,0:T(8,128)S(1)}, f32[8,256]{1,0:T(8,128)}, u32[]{:S(2)}) copy-start(f32[8,256]{1,0:T(8,128)} %get-tuple-element.69) | copy-start | bytes 24580
  319.6 9.3 %copy-start.12 = (bf16[4,32,2048]{2,1,0:T(8,128)(2,1)S(1)}, bf16[4,32,2048]{2,1,0:T(8,128)(2,1)}, u32[]{:S(2)}) copy-start(bf16[4,32,2048]{2,1,0:T(8,128)(2,1)} %get-tuple-element.63) | copy-start | bytes 1572868
  319.6 10.0 %copy-start.11 = (f32[256,512]{1,0:T(8,128)S(1)}, f32[256,512]{1,0:T(8,128)}, u32[]{:S(2)}) copy-start(f32[256,512]{1,0:T(8,128)} %get-tuple-element.102) | copy-start | bytes 1572868
  328.2 2.2 copy-start.10
  328.3 3.0 copy-start.9
  328.8 3.2 copy-start.8
